TPU v7x, 32 devices: a whole 2x2x4 slice. The times are simulated.
32 devices in a mesh: section: 4 (over x, core), tensor: 4 (over z), dp: 2 (over y).
Axes of the slice: x: 2, y: 2, z: 4, core: 2. Of those that a mesh axis runs over, the one named last changes fastest.
Arguments:
- layer_in: bfloat16 [2, 2, 4, 2, 128, 2560], P(None, None, 'section', 'dp', 'tensor'), may hold values from -6 to 6
- carry_in: bfloat16 [2, 4, 2, 128, 2560], P(None, 'section', 'dp', 'tensor'), may hold values from -6 to 6
- top_grad: bfloat16 [1, 2, 128, 2560], P(None, 'dp', 'tensor'), may hold values from -6 to 6
- w_qkv: bfloat16 [2, 4, 2560, 2560], P(None, 'section', None, 'tensor'), may hold values from -1 to 1
- w_out: bfloat16 [2, 4, 2048, 2560], P(None, 'section', 'tensor'), may hold values from -0.125 to 0.125
- gain: float32 [2, 4, 2560], P(None, 'section'), may hold values from 0.5 to 1.5
Outputs:
- unit_grads: bfloat16 [2, 2, 4, 2, 128, 2560], P(None, None, 'section', 'dp', 'tensor')
- grad_qkv: bfloat16 [2, 4, 2560, 2560], P(None, 'section', 'dp', 'tensor')
- grad_out: bfloat16 [2, 4, 2048, 2560], P(None, 'section', ('tensor', 'dp'))
- grad_gain: float32 [2, 4, 2560], P(None, 'section')
All inputs are finite; a program needn't handle non-finite values.
Results may differ from a plain program's by a relative error of at most 0.022.
The roundings to bfloat16 on the way count: a program that leaves them out, or rounds other values in their place, can miss the bound.
Values may be sent and summed in bfloat16 or wider, within the bound.
No kernel may reach another device: no remote copies, remote signals or barrier semaphores. Data moves between devices by JAX's collectives and lax.ppermute only.
A program may use at most 128 MiB of HBM per device.

v0:
```python
import functools
import math

import jax
import jax.numpy as jnp
from jax import lax
from jax.experimental import pallas as pl
from jax.experimental.pallas import tpu as pltpu
from jax.sharding import PartitionSpec as P


HD = 64
GROUP = 8

epsilon = 1e-06
rope_base = 1000000.0


ROWS = (((0,), (0,)), ((), ()))
COLS = (((1,), (1,)), ((), ()))
VMEM_BYTES = 28 * 1024 * 1024


def swap_halves(values, lane):
    width = values.shape[-1]
    half = HD // 2
    ahead = pltpu.roll(values, width - half, 1)
    behind = pltpu.roll(values, half, 1)
    return jnp.where(lane % HD < half, ahead, behind)


def pair_up(values, lane):
    low = jnp.where(lane < HD, values, 0.0)
    high = pltpu.roll(low, HD, 1)
    return jnp.concatenate([low, high], axis=0).astype(jnp.bfloat16)


def forward_kernel(nt, kv_local, *refs):
    parts, rest = refs[:nt], refs[nt:]
    gain_ref, *weight_refs, cos_ref, sin_ref, bias_ref = rest[:6]
    normed_ref, attended_ref, rotated_ref, softmax_ref = rest[6:]
    cosine, sine, bias = cos_ref[...], sin_ref[...], bias_ref[...]
    scale = 1.0 / math.sqrt(HD)
    chunks = GROUP // 2
    for m in range(2):
        rows = jnp.concatenate([p[m].astype(jnp.float32) for p in parts], axis=0)
        inverse = lax.rsqrt(jnp.mean(rows * rows, axis=-1, keepdims=True) + epsilon)
        normed = (rows * inverse * gain_ref[m]).astype(jnp.bfloat16)
        normed_ref[m] = normed
        projected = jnp.dot(normed, weight_refs[m][...], preferred_element_type=jnp.float32)
        length = rows.shape[0]
        lane = lax.broadcasted_iota(jnp.int32, (length, 2 * HD), 1)
        for group in range(kv_local):
            base = group * (GROUP + 2) * HD
            at = base + GROUP * HD
            pair = projected[:, at : at + 2 * HD]
            turned = pair * cosine + swap_halves(pair, lane) * sine
            key_value = jnp.where(lane < HD, turned, pair)
            rotated_ref[m, :, at : at + 2 * HD] = key_value.astype(jnp.bfloat16)
            keys = pair_up(key_value, lane)
            values = pair_up(pltpu.roll(key_value, HD, 1), lane)
            for c in range(chunks):
                lo = base + c * 2 * HD
                heads = projected[:, lo : lo + 2 * HD]
                query = (heads * cosine + swap_halves(heads, lane) * sine).astype(jnp.bfloat16)
                rotated_ref[m, :, lo : lo + 2 * HD] = query
                scores = lax.dot_general(query, keys, COLS, preferred_element_type=jnp.float32)
                softmax = []
                for h in range(2):
                    one = scores[:, h * length : (h + 1) * length] * scale + bias
                    power = jnp.exp(one - jnp.max(one, axis=-1, keepdims=True))
                    softmax.append(power / jnp.sum(power, axis=-1, keepdims=True))
                softmax = jnp.concatenate(softmax, axis=1)
                so = (group * chunks + c) * 2 * length
                softmax_ref[m, :, so : so + 2 * length] = softmax
                attended = jnp.dot(
                    softmax.astype(jnp.bfloat16), values, preferred_element_type=jnp.float32
                )
                ao = (group * chunks + c) * 2 * HD
                attended_ref[m, :, ao : ao + 2 * HD] = attended.astype(jnp.bfloat16)


def backward_kernel(nt, kv_local, *refs):
    parts, rest = refs[:nt], refs[nt:]
    wout_refs, wqkv_refs = rest[0:2], rest[2:4]
    rotated_ref, softmax_ref, cos_ref, sin_ref, projected_ref = rest[4:9]
    partial_refs = rest[9:]
    own = parts[0].shape[1]
    length = own * nt
    lane = lax.broadcasted_iota(jnp.int32, (length, 2 * HD), 1)
    cosine, sine = cos_ref[...], sin_ref[...]
    scale = 1.0 / math.sqrt(HD)
    chunks = GROUP // 2

    def unturn(values):
        return values * cosine - swap_halves(values, lane) * sine

    for m in (1, 0):
        grad_full = jnp.concatenate([p[m] for p in parts], axis=0)
        grad_attended = lax.dot_general(
            grad_full, wout_refs[m][...], COLS, preferred_element_type=jnp.float32
        ).astype(jnp.bfloat16)
        for group in range(kv_local):
            base = group * (GROUP + 2) * HD
            at = base + GROUP * HD
            key_value = rotated_ref[m, :, at : at + 2 * HD].astype(jnp.float32)
            keys = pair_up(key_value, lane)
            values = pair_up(pltpu.roll(key_value, HD, 1), lane)
            key_sum = jnp.zeros((2 * length, 2 * HD), jnp.float32)
            value_sum = jnp.zeros((2 * length, 2 * HD), jnp.float32)
            for c in range(chunks):
                lo = base + c * 2 * HD
                ao = (group * chunks + c) * 2 * HD
                so = (group * chunks + c) * 2 * length
                grad_heads = grad_attended[:, ao : ao + 2 * HD]
                softmax = softmax_ref[m, :, so : so + 2 * length]
                grad_softmax = lax.dot_general(
                    grad_heads, values, COLS, preferred_element_type=jnp.float32
                )
                grad_scores = []
                for h in range(2):
                    here = slice(h * length, (h + 1) * length)
                    sm, gs = softmax[:, here], grad_softmax[:, here]
                    total = jnp.sum(sm * gs, axis=-1, keepdims=True)
                    grad_scores.append((sm * (gs - total) * scale).astype(jnp.bfloat16))
                grad_scores = jnp.concatenate(grad_scores, axis=1)
                grad_query = jnp.dot(grad_scores, keys, preferred_element_type=jnp.float32)
                projected_ref[m, :, lo : lo + 2 * HD] = unturn(grad_query).astype(jnp.bfloat16)
                query = rotated_ref[m, :, lo : lo + 2 * HD]
                key_sum = key_sum + lax.dot_general(
                    grad_scores, query, ROWS, preferred_element_type=jnp.float32
                )
                value_sum = value_sum + lax.dot_general(
                    softmax.astype(jnp.bfloat16),
                    grad_heads,
                    ROWS,
                    preferred_element_type=jnp.float32,
                )
            grad_key = unturn(key_sum[:length] + pltpu.roll(key_sum[length:], HD, 1))
            grad_value = pltpu.roll(value_sum[:length], HD, 1) + value_sum[length:]
            projected_ref[m, :, at : at + 2 * HD] = jnp.where(
                lane < HD, grad_key, grad_value
            ).astype(jnp.bfloat16)
        partial = lax.dot_general(
            projected_ref[m], wqkv_refs[m][...], COLS, preferred_element_type=jnp.float32
        ).astype(jnp.bfloat16)
        for k in range(nt):
            partial_refs[k][m] = partial[k * own : (k + 1) * own]


def gain_kernel(nt, *refs):
    for m in range(2):
        total = None
        for k in range(nt):
            rows = refs[k][m].astype(jnp.float32)
            inverse = lax.rsqrt(jnp.mean(rows * rows, axis=-1, keepdims=True) + epsilon)
            term = refs[nt + k][m].astype(jnp.float32) * (rows * inverse)
            total = term if total is None else total + term
        refs[2 * nt][m] = jnp.sum(total, axis=0, keepdims=True)


def weight_kernel(count, *refs):
    left = jnp.concatenate([r[0] for r in refs[:count]], axis=0)
    right = jnp.concatenate([r[0] for r in refs[count:-1]], axis=0)
    total = lax.dot_general(left, right, ROWS, preferred_element_type=jnp.float32)
    refs[-1][0] = total.astype(jnp.bfloat16)


def call(kernel, inputs, outs, flops):
    whole = pl.BlockSpec(memory_space=pltpu.VMEM)
    moved = sum(math.prod(a.shape) * a.dtype.itemsize for a in [*inputs, *outs])
    return pl.pallas_call(
        kernel,
        out_shape=outs,
        in_specs=[whole] * len(inputs),
        out_specs=[whole] * len(outs),
        cost_estimate=pl.CostEstimate(flops=flops, bytes_accessed=moved, transcendentals=0),
        compiler_params=pltpu.CompilerParams(vmem_limit_bytes=VMEM_BYTES),
    )(*inputs)


def weight_grad(lefts, rights, split_left):
    members, _, high = lefts[0].shape
    wide = rights[0].shape[2]
    depth = sum(a.shape[1] for a in lefts)
    extent = high if split_left else wide
    tile = 640 if extent % 640 == 0 else extent
    rows = lambda a: a.shape[1]
    if split_left:
        left = [pl.BlockSpec((1, rows(a), tile), lambda m, i: (m, 0, i)) for a in lefts]
        right = [pl.BlockSpec((1, rows(a), wide), lambda m, i: (m, 0, 0)) for a in rights]
        out = pl.BlockSpec((1, tile, wide), lambda m, i: (m, i, 0))
    else:
        left = [pl.BlockSpec((1, rows(a), high), lambda m, i: (m, 0, 0)) for a in lefts]
        right = [pl.BlockSpec((1, rows(a), tile), lambda m, i: (m, 0, i)) for a in rights]
        out = pl.BlockSpec((1, high, tile), lambda m, i: (m, 0, i))
    return pl.pallas_call(
        functools.partial(weight_kernel, len(lefts)),
        grid=(members, extent // tile),
        out_shape=jax.ShapeDtypeStruct((members, high, wide), jnp.bfloat16),
        in_specs=[*left, *right],
        out_specs=out,
        cost_estimate=pl.CostEstimate(
            flops=2 * members * depth * high * wide,
            bytes_accessed=2 * members * (depth * (high + wide) + high * wide),
            transcendentals=0,
        ),
        compiler_params=pltpu.CompilerParams(vmem_limit_bytes=VMEM_BYTES),
    )(*lefts, *rights)


def shift(value, axis, steps):
    count = lax.axis_size(axis)
    return lax.ppermute(value, axis, [(i, (i + steps) % count) for i in range(count)])


def sum_over(value, axis):
    count = lax.axis_size(axis)
    if count & (count - 1):
        return lax.psum(value, axis)
    terms = [value] + [
        lax.ppermute(value, axis, [(i, i ^ step) for i in range(count)]) for step in range(1, count)
    ]
    while len(terms) > 1:
        terms = [terms[i] + terms[i + 1] for i in range(0, len(terms), 2)]
    return terms[0]


def local(layer_in, carry_in, top_grad, w_qkv, w_out, gain):
    ticks = layer_in.shape[0]
    own_rows = layer_in.shape[4]
    width = layer_in.shape[5]
    nt = lax.axis_size("tensor")
    ns = lax.axis_size("section")
    nd = lax.axis_size("dp")
    length = own_rows * nt
    section = lax.axis_index("section")
    place = lax.axis_index("tensor")
    replica = lax.axis_index("dp")
    at_first = section == 0
    at_last = section == ns - 1
    x_rows = layer_in[:, :, 0, 0]
    carried = carry_in[:, 0, 0]
    fresh_rows = top_grad[:, 0]
    weight_qkv = [w_qkv[m, 0] for m in range(2)]
    weight_out = [w_out[m, 0] for m in range(2)]
    qkv_width = w_qkv.shape[3]
    head_width = w_out.shape[2]
    kv_local = qkv_width // ((GROUP + 2) * HD)
    bf16, f32 = jnp.bfloat16, jnp.float32

    block = jnp.arange(length) // own_rows
    positions = lax.rem(place - block + nt, nt) * own_rows + lax.rem(jnp.arange(length), own_rows)
    lanes = jnp.arange(2 * HD)
    frequency = rope_base ** (-((lanes % (HD // 2)).astype(f32) * (2.0 / HD)))
    angle = positions.astype(f32)[:, None] * frequency[None, :]
    cosine = jnp.cos(angle)
    sine = jnp.where(lanes[None, :] % HD < HD // 2, -jnp.sin(angle), jnp.sin(angle))
    bias = jnp.where(positions[:, None] >= positions[None, :], 0.0, -1e30).astype(f32)

    def gather_rotated(value):
        values = value if isinstance(value, list) else [value] * nt
        parts = [values[0]]
        for k in range(1, nt):
            parts.append(shift(values[k], "tensor", k))
        return parts

    def normalize(rows):
        rows = rows.astype(f32)
        inverse = lax.rsqrt(jnp.mean(rows * rows, axis=-1, keepdims=True) + epsilon)
        return rows * inverse, inverse

    def slice_for(value, p):
        extent = value.shape[2] // nd
        return lax.dynamic_slice_in_dim(value, ((replica + p) % nd) * extent, extent, axis=2)

    def peers(value, columns):
        return [shift(slice_for(value, p) if columns else value, "dp", p) for p in range(1, nd)]

    def send_parts(parts):
        sent = []
        for part in parts:
            sent.append(peers(part, False))
        return sent

    def shaped(*shape, dtype=bf16):
        return jax.ShapeDtypeStruct((2,) + shape, dtype)

    def forward(parts):
        return call(
            functools.partial(forward_kernel, nt, kv_local),
            [*parts, gain[:, 0:1], *weight_qkv, cosine, sine, bias],
            [
                shaped(length, width),
                shaped(length, head_width),
                shaped(length, qkv_width),
                shaped(length, kv_local * GROUP * length, dtype=f32),
            ],
            4 * length * width * qkv_width,
        )

    def backward(parts, rotated, softmax):
        outs = call(
            functools.partial(backward_kernel, nt, kv_local),
            [*parts, *weight_out, *weight_qkv, rotated, softmax, cosine, sine],
            [shaped(length, qkv_width)] + [shaped(own_rows, width)] * nt,
            4 * length * width * (qkv_width + head_width),
        )
        return outs[0], outs[1:]

    x_parts = gather_rotated(x_rows[0])
    own_grads = carried
    grad_parts = gather_rotated(carried)
    normed, attended, rotated, softmax = forward(x_parts)
    normed_peers = peers(normed, True)
    attended_peers = peers(attended, True)
    sent_parts = send_parts(grad_parts)
    qkv_lefts, qkv_rights, out_lefts, out_rights = [], [], [], []
    gain_total = 0.0
    per_tick = []
    for t in range(ticks):
        projected, partials = backward(grad_parts, rotated, softmax)
        received = []
        for k in range(1, nt):
            received.append(shift(partials[k], "tensor", -k))
        grad_peers = sent_parts
        projected_peers = peers(projected, False)
        gain_total = gain_total + call(
            functools.partial(gain_kernel, nt),
            [*x_parts, *partials],
            [shaped(1, width, dtype=f32)],
            2 * length * width,
        )[0]
        total = partials[0].astype(f32)
        for part in received:
            total = total + part.astype(f32)
        unit_own, inverse = normalize(x_rows[t])
        grad_unit = total * gain[:, 0:1]
        grad_rows = inverse * (
            grad_unit - unit_own * jnp.mean(grad_unit * unit_own, axis=-1, keepdims=True)
        )
        outcome = (own_grads.astype(f32) + grad_rows).astype(bf16)
        per_tick.append(outcome)
        qkv_lefts.extend([slice_for(normed, 0), *normed_peers])
        qkv_rights.extend([projected, *projected_peers])
        out_lefts.extend([slice_for(attended, 0), *attended_peers])
        out_rights.extend(grad_parts)
        for p in range(nd - 1):
            out_rights.extend(g[p] for g in grad_peers)
        if t + 1 < ticks:
            upward = lax.ppermute(outcome[1], "section", [(s, s + 1) for s in range(ns - 1)])
            downward = lax.ppermute(outcome[0], "section", [(s, s - 1) for s in range(1, ns)])
            own_grads = jnp.stack(
                [
                    jnp.where(at_last, outcome[1], downward),
                    jnp.where(at_first, fresh_rows[t], upward),
                ]
            )
            beside, _ = lax.optimization_barrier((x_rows[t + 1], grad_parts))
            later, _ = lax.optimization_barrier((x_rows[t + 1], received))
            x_parts = gather_rotated([beside if k == nt // 2 else later for k in range(nt)])
            grad_parts = gather_rotated(own_grads)
            normed, attended, rotated, softmax = forward(x_parts)
            normed_peers = peers(normed, True)
            attended_peers = peers(attended, True)
            sent_parts = send_parts(grad_parts)
            grad_parts, qkv_lefts, qkv_rights, out_lefts, out_rights = lax.optimization_barrier(
                (grad_parts, qkv_lefts, qkv_rights, out_lefts, out_rights)
            )

    grad_out = weight_grad(out_lefts, out_rights, False)
    grad_qkv = weight_grad(qkv_lefts, qkv_rights, True)
    for axis in ("dp", "tensor"):
        gain_total = sum_over(gain_total, axis)
    return (
        jnp.stack(per_tick)[:, :, None, None],
        grad_qkv[:, None],
        grad_out[:, None],
        gain_total,
    )


def solution(mesh):
    in_specs = (
        P(None, None, "section", "dp", "tensor", None),
        P(None, "section", "dp", "tensor", None),
        P(None, "dp", "tensor", None),
        P(None, "section", None, "tensor"),
        P(None, "section", "tensor", None),
        P(None, "section", None),
    )
    out_specs = (
        P(None, None, "section", "dp", "tensor", None),
        P(None, "section", "dp", "tensor"),
        P(None, "section", ("tensor", "dp"), None),
        P(None, "section", None),
    )

    return jax.shard_map(local, mesh=mesh, in_specs=in_specs, out_specs=out_specs, check_vma=False)
```

profile of v0, /device:TPU:0, one launch (start us, length us, event | category | flops | bytes accessed | tf_op | source)
XLA Modules:
  0.0 270.8 jit_solution(1940291043797250436)
XLA Ops:
  0.6 5.1 %collective-permute-start.2 = (bf16[2,32,2560]{2,1,0:T(8,128)(2,1)}, bf16[2,32,2560]{2,1,0:T(8,128)(2,1)}, u32[]{:S(2)}, u32[]{:S(2)}) collective-permute-start(bf16[2,32,2560]{2,1,0:T(8,128)(2,1)} %bitcast.57), channel_id=1, source_target_pairs={{0,6},{2,0},{4,2},{6,4},{1,7},{3,1},{5,3},{7,5},{8,14},{10,8},{12,... | collective-permute-start | bytes 983048 | tf_op jit(solution)/shard_map/ppermute | solution.py:214
  5.8 1.0 collective-permute-start
  6.8 2.0 slice_bitcast_fusion.4
  8.7 2.8 %collective-permute-start.5 = (bf16[2,32,2560]{2,1,0:T(8,128)(2,1)}, bf16[2,32,2560]{2,1,0:T(8,128)(2,1)}, u32[]{:S(2)}, u32[]{:S(2)}) collective-permute-start(bf16[2,32,2560]{2,1,0:T(8,128)(2,1)} %get-tuple-element.95.refs_0_), channel_id=1, source_target_pairs={{0,6},{2,0},{4,2},{6,4},{1,7},{3,1},{5,3},{7,5},{8,14},{10,8},{12,... | collective-permute-start | bytes 983048 | tf_op jit(solution)/shard_map/ppermute | solution.py:214
  11.5 1.1 collective-permute-start.4
  12.7 1.1 fusion.14
  13.8 5.4 %slice_bitcast_fusion.2 = (bf16[512,2560]{1,0:T(8,128)(2,1)}, bf16[512,2560]{1,0:T(8,128)(2,1)}) fusion(bf16[2,1,512,2560]{3,2,1,0:T(8,128)(2,1)} %param.10), kind=kLoop, calls=%fused_computation.2 | loop fusion | bytes 10485760 | tf_op jit(solution)/shard_map/squeeze | solution.py:246
  19.3 2.3 slice_bitcast_fusion
  21.6 13.7 %collective-permute-done.5.refs_3_ = bf16[2,32,2560]{2,1,0:T(8,128)(2,1)} collective-permute-done((bf16[2,32,2560]{2,1,0:T(8,128)(2,1)}, bf16[2,32,2560]{2,1,0:T(8,128)(2,1)}, u32[]{:S(2)}, u32[]{:S(2)}) %collective-permute-start.5) | collective-permute-done | bytes 327712 | tf_op jit(solution)/shard_map/ppermute | solution.py:214
  35.3 21.4 %collective-permute-start.3 = (bf16[2,32,2560]{2,1,0:T(8,128)(2,1)}, bf16[2,32,2560]{2,1,0:T(8,128)(2,1)}, u32[]{:S(2)}, u32[]{:S(2)}) collective-permute-start(bf16[2,32,2560]{2,1,0:T(8,128)(2,1)} %get-tuple-element.95.refs_0_), channel_id=1, source_target_pairs={{0,2},{2,4},{4,6},{6,0},{1,3},{3,5},{5,7},{7,1},{8,10},{10,12},{12... | collective-permute-start | bytes 983048 | tf_op jit(solution)/shard_map/ppermute | solution.py:214
  57.1 5.0 %collective-permute-done.4.refs_2_ = bf16[2,32,2560]{2,1,0:T(8,128)(2,1)} collective-permute-done((bf16[2,32,2560]{2,1,0:T(8,128)(2,1)}, bf16[2,32,2560]{2,1,0:T(8,128)(2,1)}, u32[]{:S(2)}, u32[]{:S(2)}) %collective-permute-start.4) | collective-permute-done | bytes 327712 | tf_op jit(solution)/shard_map/ppermute | solution.py:214
  62.1 1.5 collective-permute-start.17
  63.6 1.9 copy-done
  65.5 4.5 %shard_map.93 = (bf16[2,128,2560]{2,1,0:T(8,128)(2,1)S(1)}, bf16[2,128,512]{2,1,0:T(8,128)(2,1)S(1)}, bf16[2,128,640]{2,1,0:T(8,128)(2,1)S(1)}, f32[2,128,1024]{2,1,0:T(8,128)S(1)}) custom-call(bf16[2,32,2560]{2,1,0:T(8,128)(2,1)} %get-tuple-element.95.refs_0_, bf16[2,32,2560]{2,1,0:T(8,128)(2,1)} %collective-permute-done.3.refs_1_, ...), custom_call_target="tpu_custom_call" | custom-call | flops 838860800 | bytes 11030528 | tf_op jit(solution)/shard_map/pallas_call | solution.py:172
  70.1 7.6 %shard_map.94 = (bf16[2,128,640]{2,1,0:T(8,128)(2,1)S(1)}, bf16[2,32,2560]{2,1,0:T(8,128)(2,1)S(1)}, bf16[2,32,2560]{2,1,0:T(8,128)(2,1)S(1)}, bf16[2,32,2560]{2,1,0:T(8,128)(2,1)S(1)}, bf16[2,32,2560]{2,1,0:T(8,128)(2,1)S(1)}) custom-call(bf16[2,32,2560]{2,1,0:T(8,128)(2,1)S(1)} %bitcast.61, bf16[2,32,2560]{2,1,0:T(8,128)(2,1)} %collective-permute-done.refs_1_.refs_5_, ...), custom_call_target="tpu_custom_call" | custom-call | flops 1509949440 | bytes 16252928 | tf_op jit(solution)/shard_map/pallas_call | solution.py:172
  77.7 2.2 collective-permute-start.6
  80.1 1.0 collective-permute-start.8
  81.1 1.8 collective-permute-start.22
  82.9 5.2 %collective-permute-done.6 = bf16[2,32,2560]{2,1,0:T(8,128)(2,1)S(1)} collective-permute-done((bf16[2,32,2560]{2,1,0:T(8,128)(2,1)S(1)}, bf16[2,32,2560]{2,1,0:T(8,128)(2,1)S(1)}, u32[]{:S(2)}, u32[]{:S(2)}) %collective-permute-start.6) | collective-permute-done | bytes 327712 | tf_op jit(solution)/shard_map/ppermute | solution.py:214
  88.2 1.4 collective-permute-start.16
  89.6 26.7 %collective-permute-done.7 = bf16[2,32,2560]{2,1,0:T(8,128)(2,1)S(1)} collective-permute-done((bf16[2,32,2560]{2,1,0:T(8,128)(2,1)S(1)}, bf16[2,32,2560]{2,1,0:T(8,128)(2,1)S(1)}, u32[]{:S(2)}, u32[]{:S(2)}) %collective-permute-start.7) | collective-permute-done | bytes 327712 | tf_op jit(solution)/shard_map/ppermute | solution.py:214
  116.3 1.5 collective-permute-start.20
  117.8 0.4 fusion.9
  118.6 1.3 collective-permute-start.9
  120.1 1.9 collective-permute-done.9
  121.9 5.1 %collective-permute-start.10 = (bf16[32,2560]{1,0:T(8,128)(2,1)S(1)}, bf16[32,2560]{1,0:T(8,128)(2,1)S(1)}, u32[]{:S(2)}, u32[]{:S(2)}) collective-permute-start(bf16[32,2560]{1,0:T(8,128)(2,1)S(1)} %get-tuple-element.97), channel_id=1, source_target_pairs={{0,8},{8,16},{16,24},{1,9},{9,17},{17,25},{2,10},{10,18},{18,26},{... | collective-permute-start | bytes 491528 | tf_op jit(solution)/shard_map/ppermute | solution.py:351
  127.1 1.0 collective-permute-done.10
  128.1 0.5 collective-permute-start.19
  128.6 1.6 collective-permute-start.14
  130.2 0.5 collective-permute-start.18
  130.7 7.9 %collective-permute-done.19.refs_10_ = bf16[2,32,2560]{2,1,0:T(8,128)(2,1)S(1)} collective-permute-done((bf16[2,32,2560]{2,1,0:T(8,128)(2,1)}, bf16[2,32,2560]{2,1,0:T(8,128)(2,1)S(1)}, u32[]{:S(2)}, u32[]{:S(2)}) %collective-permute-start.19) | collective-permute-done | bytes 327712 | tf_op jit(solution)/shard_map/ppermute | solution.py:214
  138.6 21.0 %collective-permute-done.18.refs_9_ = bf16[2,32,2560]{2,1,0:T(8,128)(2,1)S(1)} collective-permute-done((bf16[2,32,2560]{2,1,0:T(8,128)(2,1)}, bf16[2,32,2560]{2,1,0:T(8,128)(2,1)S(1)}, u32[]{:S(2)}, u32[]{:S(2)}) %collective-permute-start.18) | collective-permute-done | bytes 327712 | tf_op jit(solution)/shard_map/ppermute | solution.py:214
  159.7 0.5 collective-permute-start.15
  160.2 1.5 collective-permute-start.12
  161.7 2.0 collective-permute-start.11
  163.6 2.1 shard_map.99
  165.8 3.1 %shard_map.95 = (bf16[2,128,2560]{2,1,0:T(8,128)(2,1)S(1)}, bf16[2,128,512]{2,1,0:T(8,128)(2,1)S(1)}, bf16[2,128,640]{2,1,0:T(8,128)(2,1)S(1)}, f32[2,128,1024]{2,1,0:T(8,128)S(1)}) custom-call(bf16[2,32,2560]{2,1,0:T(8,128)(2,1)S(1)} %copy-done.4, bf16[2,32,2560]{2,1,0:T(8,128)(2,1)S(1)} %collective-permute-done.21.refs_1_, ...), custom_call_target="tpu_custom_call" | custom-call | flops 838860800 | bytes 11030528 | tf_op jit(solution)/shard_map/pallas_call | solution.py:172
  168.9 0.5 collective-permute-done.15.refs_5_
  169.4 0.5 collective-permute-start.30
  169.9 0.4 collective-permute-done.13.refs_3_.refs_15_
  170.3 20.1 %collective-permute-done.12.refs_2_.refs_14_ = bf16[2,32,2560]{2,1,0:T(8,128)(2,1)S(1)} collective-permute-done((bf16[2,32,2560]{2,1,0:T(8,128)(2,1)S(1)}, bf16[2,32,2560]{2,1,0:T(8,128)(2,1)S(1)}, u32[]{:S(2)}, u32[]{:S(2)}) %collective-permute-start.12) | collective-permute-done | bytes 327712 | tf_op jit(solution)/shard_map/ppermute | solution.py:214
  190.4 6.3 %shard_map.96 = (bf16[2,128,640]{2,1,0:T(8,128)(2,1)S(1)}, bf16[2,32,2560]{2,1,0:T(8,128)(2,1)S(1)}, bf16[2,32,2560]{2,1,0:T(8,128)(2,1)S(1)}, bf16[2,32,2560]{2,1,0:T(8,128)(2,1)S(1)}, bf16[2,32,2560]{2,1,0:T(8,128)(2,1)S(1)}) custom-call(bf16[2,32,2560]{2,1,0:T(8,128)(2,1)S(1)} %pad_maximum_fusion.refs_0_.refs_12_, ...), custom_call_target="tpu_custom_call" | custom-call | flops 1509949440 | bytes 16252928 | tf_op jit(solution)/shard_map/pallas_call | solution.py:172
  196.7 0.9 shard_map.100
  197.7 0.6 collective-permute-start.34
  198.2 1.6 collective-permute-start.29
  199.8 1.7 collective-permute-done.34
  201.6 1.6 collective-permute-start.36
  203.2 2.8 %collective-permute-start.35 = (f32[2,1,2560]{2,1,0:T(1,128)S(1)}, f32[2,1,2560]{2,1,0:T(1,128)S(1)}, u32[]{:S(2)}, u32[]{:S(2)}) collective-permute-start(f32[2,1,2560]{2,1,0:T(1,128)S(1)} %add.173), channel_id=1, source_target_pairs={{0,2},{2,0},{4,6},{6,4},{1,3},{3,1},{5,7},{7,5},{8,10},{10,8},{12,... | collective-permute-start | bytes 61448 | tf_op jit(solution)/shard_map/ppermute | solution.py:222
  206.1 1.3 collective-permute-done.37
  207.4 0.5 collective-permute-start.25
  208.0 12.5 %collective-permute-start.26 = (bf16[2,32,2560]{2,1,0:T(8,128)(2,1)S(1)}, bf16[2,32,2560]{2,1,0:T(8,128)(2,1)S(1)}, u32[]{:S(2)}, u32[]{:S(2)}) collective-permute-start(bf16[2,32,2560]{2,1,0:T(8,128)(2,1)S(1)} %get-tuple-element.62.refs_7_), channel_id=1, source_target_pairs={{0,2},{2,4},{4,6},{6,0},{1,3},{3,5},{5,7},{7,1},{8,10},{10,12},{12... | collective-permute-start | bytes 983048 | tf_op jit(solution)/shard_map/ppermute | solution.py:214
  220.5 0.6 add_add_fusion
  221.1 2.7 collective-permute-start.27
  223.8 10.7 %collective-permute-done.25 = bf16[2,32,2560]{2,1,0:T(8,128)(2,1)S(1)} collective-permute-done((bf16[2,32,2560]{2,1,0:T(8,128)(2,1)S(1)}, bf16[2,32,2560]{2,1,0:T(8,128)(2,1)S(1)}, u32[]{:S(2)}, u32[]{:S(2)}) %collective-permute-start.25) | collective-permute-done | bytes 327712 | tf_op jit(solution)/shard_map/ppermute | solution.py:214
  234.5 1.3 collective-permute-start.33
  235.8 0.7 collective-permute-start.32
  236.9 1.3 collective-permute-start.31
  238.6 0.8 collective-permute-start.28
  239.4 5.7 %collective-permute-done.33.refs_19_ = bf16[2,32,2560]{2,1,0:T(8,128)(2,1)S(1)} collective-permute-done((bf16[2,32,2560]{2,1,0:T(8,128)(2,1)S(1)}, bf16[2,32,2560]{2,1,0:T(8,128)(2,1)S(1)}, u32[]{:S(2)}, u32[]{:S(2)}) %collective-permute-start.33) | collective-permute-done | bytes 327712 | tf_op jit(solution)/shard_map/ppermute | solution.py:214
  245.1 7.0 %collective-permute-done.32.refs_18_ = bf16[2,32,2560]{2,1,0:T(8,128)(2,1)S(1)} collective-permute-done((bf16[2,32,2560]{2,1,0:T(8,128)(2,1)S(1)}, bf16[2,32,2560]{2,1,0:T(8,128)(2,1)S(1)}, u32[]{:S(2)}, u32[]{:S(2)}) %collective-permute-start.32) | collective-permute-done | bytes 327712 | tf_op jit(solution)/shard_map/ppermute | solution.py:214
  252.1 7.0 %collective-permute-done.31.refs_17_ = bf16[2,32,2560]{2,1,0:T(8,128)(2,1)S(1)} collective-permute-done((bf16[2,32,2560]{2,1,0:T(8,128)(2,1)S(1)}, bf16[2,32,2560]{2,1,0:T(8,128)(2,1)S(1)}, u32[]{:S(2)}, u32[]{:S(2)}) %collective-permute-start.31) | collective-permute-done | bytes 327712 | tf_op jit(solution)/shard_map/ppermute | solution.py:214
  259.1 6.6 %shard_map.98 = bf16[2,256,2560]{2,1,0:T(8,128)(2,1)} custom-call(bf16[2,128,256]{2,1,0:T(8,128)(2,1)S(1)} %get-tuple-element.69.refs_0_, bf16[2,128,256]{2,1,0:T(8,128)(2,1)S(1)} %collective-permute-done.16.refs_1_, bf16[2,128,256]{2,1,0:T(8,128)(2,1)S(1)} %get-tuple-element.99.refs_2_, bf16[2,128,256]{2,1,0:T(8,128)(2,1)S(1)} %collective-permute-done.29.refs_3_, ...), custom_call_target="tpu_custom_call" | custom-call | flops 1342177280 | bytes 8388608 | tf_op jit(solution)/shard_map/pallas_call | solution.py:197
  265.7 0.9 maximum_bitcast_fusion
  266.6 4.2 %shard_map.97 = bf16[2,1280,640]{2,1,0:T(8,128)(2,1)} custom-call(bf16[2,128,1280]{2,1,0:T(8,128)(2,1)S(1)} %get-tuple-element.63.refs_0_, bf16[2,128,1280]{2,1,0:T(8,128)(2,1)S(1)} %collective-permute-done.14.refs_1_, bf16[2,128,1280]{2,1,0:T(8,128)(2,1)S(1)} %get-tuple-element.91.refs_2_, bf16[2,128,1280]{2,1,0:T(8,128)(2,1)S(1)} %collective-permute-done.27.refs_3_, ...), custom_call_target="tpu_custom_call" | custom-call | flops 1677721600 | bytes 7208960 | tf_op jit(solution)/shard_map/pallas_call | solution.py:197
  (71 shorter events, 2.4 us)
Async XLA Ops:
  0.6 69.4 %collective-permute-start.2 = (bf16[2,32,2560]{2,1,0:T(8,128)(2,1)}, bf16[2,32,2560]{2,1,0:T(8,128)(2,1)}, u32[]{:S(2)}, u32[]{:S(2)}) collective-permute-start(bf16[2,32,2560]{2,1,0:T(8,128)(2,1)} %bitcast.57), channel_id=1, source_target_pairs={{0,6},{2,0},{4,2},{6,4},{1,7},{3,1},{5,3},{7,5},{8,14},{10,8},{12,... | collective-permute-start | bytes 983048 | tf_op jit(solution)/shard_map/ppermute | solution.py:214
  5.8 64.3 %collective-permute-start.1 = (bf16[2,32,2560]{2,1,0:T(8,128)(2,1)}, bf16[2,32,2560]{2,1,0:T(8,128)(2,1)}, u32[]{:S(2)}, u32[]{:S(2)}) collective-permute-start(bf16[2,32,2560]{2,1,0:T(8,128)(2,1)} %bitcast.58), channel_id=1, source_target_pairs={{0,4},{2,6},{4,0},{6,2},{1,5},{3,7},{5,1},{7,3},{8,12},{10,14},{12... | collective-permute-start | bytes 983048 | tf_op jit(solution)/shard_map/ppermute | solution.py:214
  5.8 64.3 %collective-permute-start = (bf16[2,32,2560]{2,1,0:T(8,128)(2,1)}, bf16[2,32,2560]{2,1,0:T(8,128)(2,1)}, u32[]{:S(2)}, u32[]{:S(2)}) collective-permute-start(bf16[2,32,2560]{2,1,0:T(8,128)(2,1)} %bitcast.59), channel_id=1, source_target_pairs={{0,2},{2,4},{4,6},{6,0},{1,3},{3,5},{5,7},{7,1},{8,10},{10,12},{12... | collective-permute-start | bytes 983048 | tf_op jit(solution)/shard_map/ppermute | solution.py:214
  8.7 26.6 %collective-permute-start.5 = (bf16[2,32,2560]{2,1,0:T(8,128)(2,1)}, bf16[2,32,2560]{2,1,0:T(8,128)(2,1)}, u32[]{:S(2)}, u32[]{:S(2)}) collective-permute-start(bf16[2,32,2560]{2,1,0:T(8,128)(2,1)} %get-tuple-element.95.refs_0_), channel_id=1, source_target_pairs={{0,6},{2,0},{4,2},{6,4},{1,7},{3,1},{5,3},{7,5},{8,14},{10,8},{12,... | collective-permute-start | bytes 983048 | tf_op jit(solution)/shard_map/ppermute | solution.py:214
  11.5 50.6 %collective-permute-start.4 = (bf16[2,32,2560]{2,1,0:T(8,128)(2,1)}, bf16[2,32,2560]{2,1,0:T(8,128)(2,1)}, u32[]{:S(2)}, u32[]{:S(2)}) collective-permute-start(bf16[2,32,2560]{2,1,0:T(8,128)(2,1)} %get-tuple-element.95.refs_0_), channel_id=1, source_target_pairs={{0,4},{2,6},{4,0},{6,2},{1,5},{3,7},{5,1},{7,3},{8,12},{10,14},{12... | collective-permute-start | bytes 983048 | tf_op jit(solution)/shard_map/ppermute | solution.py:214
  13.8 5.5 %copy-start.8 = (bf16[2,1,2560,640]{3,2,1,0:T(8,128)(2,1)S(1)}, bf16[2,1,2560,640]{3,2,1,0:T(8,128)(2,1)}, u32[]{:S(2)}) copy-start(bf16[2,1,2560,640]{3,2,1,0:T(8,128)(2,1)} %param.9) | copy-start | bytes 19660804
  19.3 37.5 %copy-start.6 = (f32[2,1,2560]{2,1,0:T(1,128)S(1)}, f32[2,1,2560]{2,1,0:T(1,128)}, u32[]{:S(2)}) copy-start(f32[2,1,2560]{2,1,0:T(1,128)} %refs_4_.3) | copy-start | bytes 61444
  35.3 28.3 %collective-permute-start.3 = (bf16[2,32,2560]{2,1,0:T(8,128)(2,1)}, bf16[2,32,2560]{2,1,0:T(8,128)(2,1)}, u32[]{:S(2)}, u32[]{:S(2)}) collective-permute-start(bf16[2,32,2560]{2,1,0:T(8,128)(2,1)} %get-tuple-element.95.refs_0_), channel_id=1, source_target_pairs={{0,2},{2,4},{4,6},{6,0},{1,3},{3,5},{5,7},{7,1},{8,10},{10,12},{12... | collective-permute-start | bytes 983048 | tf_op jit(solution)/shard_map/ppermute | solution.py:214
  62.1 66.5 %collective-permute-start.17 = (bf16[2,32,2560]{2,1,0:T(8,128)(2,1)}, bf16[2,32,2560]{2,1,0:T(8,128)(2,1)S(1)}, u32[]{:S(2)}, u32[]{:S(2)}) collective-permute-start(bf16[2,32,2560]{2,1,0:T(8,128)(2,1)} %bitcast.60), channel_id=1, source_target_pairs={{0,1},{1,0},{2,3},{3,2},{4,5},{5,4},{6,7},{7,6},{8,9},{9,8},{10,11... | collective-permute-start | bytes 983048 | tf_op jit(solution)/shard_map/ppermute | solution.py:214
  63.6 1.9 copy-start
  65.5 4.5 %copy-start.2 = (bf16[512,2560]{1,0:T(8,128)(2,1)S(1)}, bf16[512,2560]{1,0:T(8,128)(2,1)}, u32[]{:S(2)}) copy-start(bf16[512,2560]{1,0:T(8,128)(2,1)} %get-tuple-element.88.refs_5_) | copy-start | bytes 7864324
  65.5 4.5 %copy-start.3 = (bf16[512,2560]{1,0:T(8,128)(2,1)S(1)}, bf16[512,2560]{1,0:T(8,128)(2,1)}, u32[]{:S(2)}) copy-start(bf16[512,2560]{1,0:T(8,128)(2,1)} %get-tuple-element.89.refs_4_) | copy-start | bytes 7864324
  65.5 4.5 %copy-start.5 = (bf16[2,1,1,32,2560]{4,3,2,1,0:T(8,128)(2,1)S(1)}, bf16[2,1,1,32,2560]{4,3,2,1,0:T(8,128)(2,1)}, u32[]{:S(2)}) copy-start(bf16[2,1,1,32,2560]{4,3,2,1,0:T(8,128)(2,1)} %param.7) | copy-start | bytes 983044
  70.1 11.0 %copy-start.4 = (bf16[2,32,2560]{2,1,0:T(8,128)(2,1)S(1)}, bf16[2,32,2560]{2,1,0:T(8,128)(2,1)}, u32[]{:S(2)}) copy-start(bf16[2,32,2560]{2,1,0:T(8,128)(2,1)} %get-tuple-element.56.refs_0_) | copy-start | bytes 983044
  70.1 47.8 %copy-start.7 = (bf16[2,2,1,1,32,2560]{5,4,3,2,1,0:T(8,128)(2,1)S(1)}, bf16[2,2,1,1,32,2560]{5,4,3,2,1,0:T(8,128)(2,1)}, u32[]{:S(2)}) copy-start(bf16[2,2,1,1,32,2560]{5,4,3,2,1,0:T(8,128)(2,1)} %param.6) | copy-start | bytes 1966084
  77.7 10.5 %collective-permute-start.6 = (bf16[2,32,2560]{2,1,0:T(8,128)(2,1)S(1)}, bf16[2,32,2560]{2,1,0:T(8,128)(2,1)S(1)}, u32[]{:S(2)}, u32[]{:S(2)}) collective-permute-start(bf16[2,32,2560]{2,1,0:T(8,128)(2,1)S(1)} %get-tuple-element.45.refs_5_), channel_id=1, source_target_pairs={{0,6},{2,0},{4,2},{6,4},{1,7},{3,1},{5,3},{7,5},{8,14},{10,8},{12,... | collective-permute-start | bytes 983048 | tf_op jit(solution)/shard_map/ppermute | solution.py:214
  79.9 36.4 %collective-permute-start.7 = (bf16[2,32,2560]{2,1,0:T(8,128)(2,1)S(1)}, bf16[2,32,2560]{2,1,0:T(8,128)(2,1)S(1)}, u32[]{:S(2)}, u32[]{:S(2)}) collective-permute-start(bf16[2,32,2560]{2,1,0:T(8,128)(2,1)S(1)} %get-tuple-element.46.refs_6_), channel_id=1, source_target_pairs={{0,4},{2,6},{4,0},{6,2},{1,5},{3,7},{5,1},{7,3},{8,12},{10,14},{12... | collective-permute-start | bytes 983048 | tf_op jit(solution)/shard_map/ppermute | solution.py:214
  80.1 37.7 %collective-permute-start.8 = (bf16[2,32,2560]{2,1,0:T(8,128)(2,1)S(1)}, bf16[2,32,2560]{2,1,0:T(8,128)(2,1)S(1)}, u32[]{:S(2)}, u32[]{:S(2)}) collective-permute-start(bf16[2,32,2560]{2,1,0:T(8,128)(2,1)S(1)} %get-tuple-element.47.refs_7_), channel_id=1, source_target_pairs={{0,2},{2,4},{4,6},{6,0},{1,3},{3,5},{5,7},{7,1},{8,10},{10,12},{12... | collective-permute-start | bytes 983048 | tf_op jit(solution)/shard_map/ppermute | solution.py:214
  81.1 79.1 %collective-permute-start.22 = (bf16[2,32,2560]{2,1,0:T(8,128)(2,1)S(1)}, bf16[2,32,2560]{2,1,0:T(8,128)(2,1)S(1)}, u32[]{:S(2)}, u32[]{:S(2)}) collective-permute-start(bf16[2,32,2560]{2,1,0:T(8,128)(2,1)S(1)} %copy-done.4), channel_id=1, source_target_pairs={{0,4},{2,6},{4,0},{6,2},{1,5},{3,7},{5,1},{7,3},{8,12},{10,14},{12... | collective-permute-start | bytes 983048 | tf_op jit(solution)/shard_map/ppermute | solution.py:214
  88.2 42.0 %collective-permute-start.16 = (bf16[2,128,256]{2,1,0:T(8,128)(2,1)S(1)}, bf16[2,128,256]{2,1,0:T(8,128)(2,1)S(1)}, u32[]{:S(2)}, u32[]{:S(2)}) collective-permute-start(bf16[2,128,256]{2,1,0:T(8,128)(2,1)S(1)} %get-tuple-element.100), channel_id=1, source_target_pairs={{0,1},{1,0},{2,3},{3,2},{4,5},{5,4},{6,7},{7,6},{8,9},{9,8},{10,11... | collective-permute-start | bytes 393224 | tf_op jit(solution)/shard_map/ppermute | solution.py:214
  116.3 14.4 %collective-permute-start.20 = (bf16[2,32,2560]{2,1,0:T(8,128)(2,1)}, bf16[2,32,2560]{2,1,0:T(8,128)(2,1)S(1)}, u32[]{:S(2)}, u32[]{:S(2)}) collective-permute-start(bf16[2,32,2560]{2,1,0:T(8,128)(2,1)} %collective-permute-done.2.refs_3_.refs_7_), channel_id=1, source_target_pairs={{0,1},{1,0},{2,3},{3,2},{4,5},{5,4},{6,7},{7,6},{8,9},{9,8},{10,11... | collective-permute-start | bytes 983048 | tf_op jit(solution)/shard_map/ppermute | solution.py:214
  118.3 10.3 %copy-start.9 = (bf16[1,1,32,2560]{3,2,1,0:T(8,128)(2,1)S(1)}, bf16[1,1,32,2560]{3,2,1,0:T(8,128)(2,1)}, u32[]{:S(2)}) copy-start(bf16[1,1,32,2560]{3,2,1,0:T(8,128)(2,1)} %param.8) | copy-start | bytes 491524
  118.6 3.3 %collective-permute-start.9 = (bf16[32,2560]{1,0:T(8,128)(2,1)S(1)}, bf16[32,2560]{1,0:T(8,128)(2,1)S(1)}, u32[]{:S(2)}, u32[]{:S(2)}) collective-permute-start(bf16[32,2560]{1,0:T(8,128)(2,1)S(1)} %get-tuple-element.96), channel_id=1, source_target_pairs={{8,0},{16,8},{24,16},{9,1},{17,9},{25,17},{10,2},{18,10},{26,18},{... | collective-permute-start | bytes 491528 | tf_op jit(solution)/shard_map/ppermute | solution.py:352
  119.9 45.9 %copy-start.1 = (bf16[2560,640]{1,0:T(8,128)(2,1)S(1)}, bf16[2560,640]{1,0:T(8,128)(2,1)}, u32[]{:S(2)}) copy-start(bf16[2560,640]{1,0:T(8,128)(2,1)} %get-tuple-element.87.refs_5_.refs_6_) | copy-start | bytes 9830404
  121.9 6.1 %collective-permute-start.10 = (bf16[32,2560]{1,0:T(8,128)(2,1)S(1)}, bf16[32,2560]{1,0:T(8,128)(2,1)S(1)}, u32[]{:S(2)}, u32[]{:S(2)}) collective-permute-start(bf16[32,2560]{1,0:T(8,128)(2,1)S(1)} %get-tuple-element.97), channel_id=1, source_target_pairs={{0,8},{8,16},{16,24},{1,9},{9,17},{17,25},{2,10},{10,18},{18,26},{... | collective-permute-start | bytes 491528 | tf_op jit(solution)/shard_map/ppermute | solution.py:351
  128.1 10.5 %collective-permute-start.19 = (bf16[2,32,2560]{2,1,0:T(8,128)(2,1)}, bf16[2,32,2560]{2,1,0:T(8,128)(2,1)S(1)}, u32[]{:S(2)}, u32[]{:S(2)}) collective-permute-start(bf16[2,32,2560]{2,1,0:T(8,128)(2,1)} %collective-permute-done.1.refs_2_.refs_6_), channel_id=1, source_target_pairs={{0,1},{1,0},{2,3},{3,2},{4,5},{5,4},{6,7},{7,6},{8,9},{9,8},{10,11... | collective-permute-start | bytes 983048 | tf_op jit(solution)/shard_map/ppermute | solution.py:214
  128.6 41.3 %collective-permute-start.14 = (bf16[2,128,1280]{2,1,0:T(8,128)(2,1)S(1)}, bf16[2,128,1280]{2,1,0:T(8,128)(2,1)S(1)}, u32[]{:S(2)}, u32[]{:S(2)}) collective-permute-start(bf16[2,128,1280]{2,1,0:T(8,128)(2,1)S(1)} %get-tuple-element.92), channel_id=1, source_target_pairs={{0,1},{1,0},{2,3},{3,2},{4,5},{5,4},{6,7},{7,6},{8,9},{9,8},{10,11... | collective-permute-start | bytes 1966088 | tf_op jit(solution)/shard_map/ppermute | solution.py:214
  130.2 29.5 %collective-permute-start.18 = (bf16[2,32,2560]{2,1,0:T(8,128)(2,1)}, bf16[2,32,2560]{2,1,0:T(8,128)(2,1)S(1)}, u32[]{:S(2)}, u32[]{:S(2)}) collective-permute-start(bf16[2,32,2560]{2,1,0:T(8,128)(2,1)} %collective-permute-done.refs_1_.refs_5_), channel_id=1, source_target_pairs={{0,1},{1,0},{2,3},{3,2},{4,5},{5,4},{6,7},{7,6},{8,9},{9,8},{10,11... | collective-permute-start | bytes 983048 | tf_op jit(solution)/shard_map/ppermute | solution.py:214
  130.7 29.5 %collective-permute-start.23 = (bf16[2,32,2560]{2,1,0:T(8,128)(2,1)S(1)}, bf16[2,32,2560]{2,1,0:T(8,128)(2,1)S(1)}, u32[]{:S(2)}, u32[]{:S(2)}) collective-permute-start(bf16[2,32,2560]{2,1,0:T(8,128)(2,1)S(1)} %copy-done.4), channel_id=1, source_target_pairs={{0,6},{2,0},{4,2},{6,4},{1,7},{3,1},{5,3},{7,5},{8,14},{10,8},{12,... | collective-permute-start | bytes 983048 | tf_op jit(solution)/shard_map/ppermute | solution.py:214
  138.6 23.1 %collective-permute-start.21 = (bf16[2,32,2560]{2,1,0:T(8,128)(2,1)S(1)}, bf16[2,32,2560]{2,1,0:T(8,128)(2,1)S(1)}, u32[]{:S(2)}, u32[]{:S(2)}) collective-permute-start(bf16[2,32,2560]{2,1,0:T(8,128)(2,1)S(1)} %copy-done.4), channel_id=1, source_target_pairs={{0,2},{2,4},{4,6},{6,0},{1,3},{3,5},{5,7},{7,1},{8,10},{10,12},{12... | collective-permute-start | bytes 983048 | tf_op jit(solution)/shard_map/ppermute | solution.py:214
  159.7 9.7 %collective-permute-start.15 = (bf16[2,128,640]{2,1,0:T(8,128)(2,1)S(1)}, bf16[2,128,640]{2,1,0:T(8,128)(2,1)S(1)}, u32[]{:S(2)}, u32[]{:S(2)}) collective-permute-start(bf16[2,128,640]{2,1,0:T(8,128)(2,1)S(1)} %get-tuple-element.66.refs_4_), channel_id=1, source_target_pairs={{0,1},{1,0},{2,3},{3,2},{4,5},{5,4},{6,7},{7,6},{8,9},{9,8},{10,11... | collective-permute-start | bytes 983048 | tf_op jit(solution)/shard_map/ppermute | solution.py:214
  160.2 10.1 %collective-permute-start.13 = (bf16[2,32,2560]{2,1,0:T(8,128)(2,1)S(1)}, bf16[2,32,2560]{2,1,0:T(8,128)(2,1)S(1)}, u32[]{:S(2)}, u32[]{:S(2)}) collective-permute-start(bf16[2,32,2560]{2,1,0:T(8,128)(2,1)S(1)} %pad_maximum_fusion.refs_0_.refs_12_), channel_id=1, source_target_pairs={{0,6},{2,0},{4,2},{6,4},{1,7},{3,1},{5,3},{7,5},{8,14},{10,8},{12,... | collective-permute-start | bytes 983048 | tf_op jit(solution)/shard_map/ppermute | solution.py:214
  160.2 30.2 %collective-permute-start.12 = (bf16[2,32,2560]{2,1,0:T(8,128)(2,1)S(1)}, bf16[2,32,2560]{2,1,0:T(8,128)(2,1)S(1)}, u32[]{:S(2)}, u32[]{:S(2)}) collective-permute-start(bf16[2,32,2560]{2,1,0:T(8,128)(2,1)S(1)} %pad_maximum_fusion.refs_0_.refs_12_), channel_id=1, source_target_pairs={{0,4},{2,6},{4,0},{6,2},{1,5},{3,7},{5,1},{7,3},{8,12},{10,14},{12... | collective-permute-start | bytes 983048 | tf_op jit(solution)/shard_map/ppermute | solution.py:214
  161.7 28.7 %collective-permute-start.11 = (bf16[2,32,2560]{2,1,0:T(8,128)(2,1)S(1)}, bf16[2,32,2560]{2,1,0:T(8,128)(2,1)S(1)}, u32[]{:S(2)}, u32[]{:S(2)}) collective-permute-start(bf16[2,32,2560]{2,1,0:T(8,128)(2,1)S(1)} %pad_maximum_fusion.refs_0_.refs_12_), channel_id=1, source_target_pairs={{0,2},{2,4},{4,6},{6,0},{1,3},{3,5},{5,7},{7,1},{8,10},{10,12},{12... | collective-permute-start | bytes 983048 | tf_op jit(solution)/shard_map/ppermute | solution.py:214
  169.4 69.2 %collective-permute-start.30 = (bf16[2,32,2560]{2,1,0:T(8,128)(2,1)S(1)}, bf16[2,32,2560]{2,1,0:T(8,128)(2,1)S(1)}, u32[]{:S(2)}, u32[]{:S(2)}) collective-permute-start(bf16[2,32,2560]{2,1,0:T(8,128)(2,1)S(1)} %pad_maximum_fusion.refs_0_.refs_12_), channel_id=1, source_target_pairs={{0,1},{1,0},{2,3},{3,2},{4,5},{5,4},{6,7},{7,6},{8,9},{9,8},{10,11... | collective-permute-start | bytes 983048 | tf_op jit(solution)/shard_map/ppermute | solution.py:214
  197.7 3.9 %collective-permute-start.34 = (f32[2,1,2560]{2,1,0:T(1,128)S(1)}, f32[2,1,2560]{2,1,0:T(1,128)S(1)}, u32[]{:S(2)}, u32[]{:S(2)}) collective-permute-start(f32[2,1,2560]{2,1,0:T(1,128)S(1)} %add.172), channel_id=1, source_target_pairs={{0,1},{1,0},{2,3},{3,2},{4,5},{5,4},{6,7},{7,6},{8,9},{9,8},{10,11... | collective-permute-start | bytes 61448 | tf_op jit(solution)/shard_map/ppermute | solution.py:222
  198.2 38.7 %collective-permute-start.29 = (bf16[2,128,256]{2,1,0:T(8,128)(2,1)S(1)}, bf16[2,128,256]{2,1,0:T(8,128)(2,1)S(1)}, u32[]{:S(2)}, u32[]{:S(2)}) collective-permute-start(bf16[2,128,256]{2,1,0:T(8,128)(2,1)S(1)} %get-tuple-element.98), channel_id=1, source_target_pairs={{0,1},{1,0},{2,3},{3,2},{4,5},{5,4},{6,7},{7,6},{8,9},{9,8},{10,11... | collective-permute-start | bytes 393224 | tf_op jit(solution)/shard_map/ppermute | solution.py:214
  201.5 5.9 %collective-permute-start.37 = (f32[2,1,2560]{2,1,0:T(1,128)S(1)}, f32[2,1,2560]{2,1,0:T(1,128)S(1)}, u32[]{:S(2)}, u32[]{:S(2)}) collective-permute-start(f32[2,1,2560]{2,1,0:T(1,128)S(1)} %add.173), channel_id=1, source_target_pairs={{0,6},{2,4},{4,2},{6,0},{1,7},{3,5},{5,3},{7,1},{8,14},{10,12},{12... | collective-permute-start | bytes 61448 | tf_op jit(solution)/shard_map/ppermute | solution.py:222
  201.6 5.8 %collective-permute-start.36 = (f32[2,1,2560]{2,1,0:T(1,128)S(1)}, f32[2,1,2560]{2,1,0:T(1,128)S(1)}, u32[]{:S(2)}, u32[]{:S(2)}) collective-permute-start(f32[2,1,2560]{2,1,0:T(1,128)S(1)} %add.173), channel_id=1, source_target_pairs={{0,4},{2,6},{4,0},{6,2},{1,5},{3,7},{5,1},{7,3},{8,12},{10,14},{12... | collective-permute-start | bytes 61448 | tf_op jit(solution)/shard_map/ppermute | solution.py:222
  203.2 4.8 %collective-permute-start.35 = (f32[2,1,2560]{2,1,0:T(1,128)S(1)}, f32[2,1,2560]{2,1,0:T(1,128)S(1)}, u32[]{:S(2)}, u32[]{:S(2)}) collective-permute-start(f32[2,1,2560]{2,1,0:T(1,128)S(1)} %add.173), channel_id=1, source_target_pairs={{0,2},{2,0},{4,6},{6,4},{1,3},{3,1},{5,7},{7,5},{8,10},{10,8},{12,... | collective-permute-start | bytes 61448 | tf_op jit(solution)/shard_map/ppermute | solution.py:222
  207.4 13.7 %collective-permute-start.24 = (bf16[2,32,2560]{2,1,0:T(8,128)(2,1)S(1)}, bf16[2,32,2560]{2,1,0:T(8,128)(2,1)S(1)}, u32[]{:S(2)}, u32[]{:S(2)}) collective-permute-start(bf16[2,32,2560]{2,1,0:T(8,128)(2,1)S(1)} %get-tuple-element.60.refs_5_), channel_id=1, source_target_pairs={{0,6},{2,0},{4,2},{6,4},{1,7},{3,1},{5,3},{7,5},{8,14},{10,8},{12,... | collective-permute-start | bytes 983048 | tf_op jit(solution)/shard_map/ppermute | solution.py:214
  207.4 27.1 %collective-permute-start.25 = (bf16[2,32,2560]{2,1,0:T(8,128)(2,1)S(1)}, bf16[2,32,2560]{2,1,0:T(8,128)(2,1)S(1)}, u32[]{:S(2)}, u32[]{:S(2)}) collective-permute-start(bf16[2,32,2560]{2,1,0:T(8,128)(2,1)S(1)} %get-tuple-element.61.refs_6_), channel_id=1, source_target_pairs={{0,4},{2,6},{4,0},{6,2},{1,5},{3,7},{5,1},{7,3},{8,12},{10,14},{12... | collective-permute-start | bytes 983048 | tf_op jit(solution)/shard_map/ppermute | solution.py:214
  208.0 27.9 %collective-permute-start.26 = (bf16[2,32,2560]{2,1,0:T(8,128)(2,1)S(1)}, bf16[2,32,2560]{2,1,0:T(8,128)(2,1)S(1)}, u32[]{:S(2)}, u32[]{:S(2)}) collective-permute-start(bf16[2,32,2560]{2,1,0:T(8,128)(2,1)S(1)} %get-tuple-element.62.refs_7_), channel_id=1, source_target_pairs={{0,2},{2,4},{4,6},{6,0},{1,3},{3,5},{5,7},{7,1},{8,10},{10,12},{12... | collective-permute-start | bytes 983048 | tf_op jit(solution)/shard_map/ppermute | solution.py:214
  221.1 45.5 %collective-permute-start.27 = (bf16[2,128,1280]{2,1,0:T(8,128)(2,1)S(1)}, bf16[2,128,1280]{2,1,0:T(8,128)(2,1)S(1)}, u32[]{:S(2)}, u32[]{:S(2)}) collective-permute-start(bf16[2,128,1280]{2,1,0:T(8,128)(2,1)S(1)} %get-tuple-element.90), channel_id=1, source_target_pairs={{0,1},{1,0},{2,3},{3,2},{4,5},{5,4},{6,7},{7,6},{8,9},{9,8},{10,11... | collective-permute-start | bytes 1966088 | tf_op jit(solution)/shard_map/ppermute | solution.py:214
  234.5 10.6 %collective-permute-start.33 = (bf16[2,32,2560]{2,1,0:T(8,128)(2,1)S(1)}, bf16[2,32,2560]{2,1,0:T(8,128)(2,1)S(1)}, u32[]{:S(2)}, u32[]{:S(2)}) collective-permute-start(bf16[2,32,2560]{2,1,0:T(8,128)(2,1)S(1)} %collective-permute-done.13.refs_3_.refs_15_), channel_id=1, source_target_pairs={{0,1},{1,0},{2,3},{3,2},{4,5},{5,4},{6,7},{7,6},{8,9},{9,8},{10,11... | collective-permute-start | bytes 983048 | tf_op jit(solution)/shard_map/ppermute | solution.py:214
  235.8 16.3 %collective-permute-start.32 = (bf16[2,32,2560]{2,1,0:T(8,128)(2,1)S(1)}, bf16[2,32,2560]{2,1,0:T(8,128)(2,1)S(1)}, u32[]{:S(2)}, u32[]{:S(2)}) collective-permute-start(bf16[2,32,2560]{2,1,0:T(8,128)(2,1)S(1)} %collective-permute-done.12.refs_2_.refs_14_), channel_id=1, source_target_pairs={{0,1},{1,0},{2,3},{3,2},{4,5},{5,4},{6,7},{7,6},{8,9},{9,8},{10,11... | collective-permute-start | bytes 983048 | tf_op jit(solution)/shard_map/ppermute | solution.py:214
  236.9 22.2 %collective-permute-start.31 = (bf16[2,32,2560]{2,1,0:T(8,128)(2,1)S(1)}, bf16[2,32,2560]{2,1,0:T(8,128)(2,1)S(1)}, u32[]{:S(2)}, u32[]{:S(2)}) collective-permute-start(bf16[2,32,2560]{2,1,0:T(8,128)(2,1)S(1)} %collective-permute-done.11.refs_1_.refs_13_), channel_id=1, source_target_pairs={{0,1},{1,0},{2,3},{3,2},{4,5},{5,4},{6,7},{7,6},{8,9},{9,8},{10,11... | collective-permute-start | bytes 983048 | tf_op jit(solution)/shard_map/ppermute | solution.py:214
  238.6 28.0 %collective-permute-start.28 = (bf16[2,128,640]{2,1,0:T(8,128)(2,1)S(1)}, bf16[2,128,640]{2,1,0:T(8,128)(2,1)S(1)}, u32[]{:S(2)}, u32[]{:S(2)}) collective-permute-start(bf16[2,128,640]{2,1,0:T(8,128)(2,1)S(1)} %get-tuple-element.68.refs_6_), channel_id=1, source_target_pairs={{0,1},{1,0},{2,3},{3,2},{4,5},{5,4},{6,7},{7,6},{8,9},{9,8},{10,11... | collective-permute-start | bytes 983048 | tf_op jit(solution)/shard_map/ppermute | solution.py:214
where the time goes:
time: 273 us; the launch traced here: 271 us
  waiting for transfers between devices  137 us (50%)
  starting transfers between devices  81.1 us (30%)
  Pallas kernels  35.3 us (13%)
  local copies, waits for them, and re-layouts  11.9 us (4%)
  other arithmetic  4.71 us (2%)
    ppermute x32, waiting for transfers between devices, shift(): lax.ppermute(value, axis, [(i, (i + steps) % count) for i in range(count)])  131 us
    ppermute x32, starting transfers between devices, shift(): lax.ppermute(value, axis, [(i, (i + steps) % count) for i in range(count)])  69.7 us
    pallas_call x6, Pallas kernels, call(): pl.pallas_call(kernel, out_shape=outs, in_specs=[whole] * len(inputs), ou...  24.5 us
    pallas_call x2, Pallas kernels, weight_grad(): pl.pallas_call(functools.partial(weight_kernel, len(lefts)), grid=(member...  10.8 us
  transfers between devices with their start and end apart: 38, of which 18 were waited for; matrix products, arithmetic and copies ran while one was open for 5% of the time, Pallas kernels for 11%

commit v1 on v0

v1 whole, which is shorter than its diff:
```python
import functools
import math

import jax
import jax.numpy as jnp
from jax import lax
from jax.experimental import pallas as pl
from jax.experimental.pallas import tpu as pltpu
from jax.sharding import PartitionSpec as P


HD = 64
GROUP = 8

epsilon = 1e-06
rope_base = 1000000.0


ROWS = (((0,), (0,)), ((), ()))
COLS = (((1,), (1,)), ((), ()))
VMEM_BYTES = 8 * 1024 * 1024


def swap_halves(values, lane):
    width = values.shape[-1]
    half = HD // 2
    ahead = pltpu.roll(values, width - half, 1)
    behind = pltpu.roll(values, half, 1)
    return jnp.where(lane % HD < half, ahead, behind)


def pair_up(values, lane):
    low = jnp.where(lane < HD, values, 0.0)
    high = pltpu.roll(low, HD, 1)
    return jnp.concatenate([low, high], axis=0).astype(jnp.bfloat16)


def pick(parts, nt, flag_ref, m):
    blocks = [p[m] if len(p.shape) == 3 else p[...] for p in parts]
    if len(parts) > nt:
        far = blocks.pop()
        blocks[1] = jnp.where(flag_ref[0] == 0, far, blocks[1])
        blocks[nt - 1] = jnp.where(flag_ref[0] == nt - 1, far, blocks[nt - 1])
    return blocks


def forward_kernel(nt, given, kv_local, flag_ref, *refs):
    parts, rest = refs[:given], refs[given:]
    gain_ref, *weight_refs, cos_ref, sin_ref, bias_ref = rest[:6]
    normed_ref, attended_ref, rotated_ref, softmax_ref = rest[6:]
    cosine, sine, bias = cos_ref[...], sin_ref[...], bias_ref[...]
    scale = 1.0 / math.sqrt(HD)
    chunks = GROUP // 2
    for m in range(2):
        blocks = pick(parts, nt, flag_ref, m)
        rows = jnp.concatenate([b.astype(jnp.float32) for b in blocks], axis=0)
        inverse = lax.rsqrt(jnp.mean(rows * rows, axis=-1, keepdims=True) + epsilon)
        normed = (rows * inverse * gain_ref[m]).astype(jnp.bfloat16)
        normed_ref[m] = normed
        projected = jnp.dot(normed, weight_refs[m][...], preferred_element_type=jnp.float32)
        length = rows.shape[0]
        lane = lax.broadcasted_iota(jnp.int32, (length, 2 * HD), 1)
        for group in range(kv_local):
            base = group * (GROUP + 2) * HD
            at = base + GROUP * HD
            pair = projected[:, at : at + 2 * HD]
            turned = pair * cosine + swap_halves(pair, lane) * sine
            key_value = jnp.where(lane < HD, turned, pair)
            rotated_ref[m, :, at : at + 2 * HD] = key_value.astype(jnp.bfloat16)
            keys = pair_up(key_value, lane)
            values = pair_up(pltpu.roll(key_value, HD, 1), lane)
            for c in range(chunks):
                lo = base + c * 2 * HD
                heads = projected[:, lo : lo + 2 * HD]
                query = (heads * cosine + swap_halves(heads, lane) * sine).astype(jnp.bfloat16)
                rotated_ref[m, :, lo : lo + 2 * HD] = query
                scores = lax.dot_general(query, keys, COLS, preferred_element_type=jnp.float32)
                softmax = []
                for h in range(2):
                    one = scores[:, h * length : (h + 1) * length] * scale + bias
                    power = jnp.exp(one - jnp.max(one, axis=-1, keepdims=True))
                    softmax.append(power / jnp.sum(power, axis=-1, keepdims=True))
                softmax = jnp.concatenate(softmax, axis=1)
                so = (group * chunks + c) * 2 * length
                softmax_ref[m, :, so : so + 2 * length] = softmax
                attended = jnp.dot(
                    softmax.astype(jnp.bfloat16), values, preferred_element_type=jnp.float32
                )
                ao = (group * chunks + c) * 2 * HD
                attended_ref[m, :, ao : ao + 2 * HD] = attended.astype(jnp.bfloat16)


def backward_kernel(nt, given, kv_local, m, flag_ref, *refs):
    parts, rest = refs[:given], refs[given:]
    wout_ref, wqkv_ref, rotated_ref, softmax_ref, cos_ref, sin_ref = rest[:6]
    projected_ref = rest[-nt - 1]
    partial_refs = rest[-nt:]
    own = parts[0].shape[-2]
    length = own * nt
    lane = lax.broadcasted_iota(jnp.int32, (length, 2 * HD), 1)
    cosine, sine = cos_ref[...], sin_ref[...]
    scale = 1.0 / math.sqrt(HD)
    chunks = GROUP // 2

    def unturn(values):
        return values * cosine - swap_halves(values, lane) * sine

    grad_full = jnp.concatenate(pick(parts, nt, flag_ref, m), axis=0)
    grad_attended = lax.dot_general(
        grad_full, wout_ref[...], COLS, preferred_element_type=jnp.float32
    ).astype(jnp.bfloat16)
    for group in range(kv_local):
        base = group * (GROUP + 2) * HD
        at = base + GROUP * HD
        key_value = rotated_ref[m, :, at : at + 2 * HD].astype(jnp.float32)
        keys = pair_up(key_value, lane)
        values = pair_up(pltpu.roll(key_value, HD, 1), lane)
        key_sum = jnp.zeros((2 * length, 2 * HD), jnp.float32)
        value_sum = jnp.zeros((2 * length, 2 * HD), jnp.float32)
        for c in range(chunks):
            lo = base + c * 2 * HD
            ao = (group * chunks + c) * 2 * HD
            so = (group * chunks + c) * 2 * length
            grad_heads = grad_attended[:, ao : ao + 2 * HD]
            softmax = softmax_ref[m, :, so : so + 2 * length]
            grad_softmax = lax.dot_general(
                grad_heads, values, COLS, preferred_element_type=jnp.float32
            )
            grad_scores = []
            for h in range(2):
                here = slice(h * length, (h + 1) * length)
                sm, gs = softmax[:, here], grad_softmax[:, here]
                total = jnp.sum(sm * gs, axis=-1, keepdims=True)
                grad_scores.append((sm * (gs - total) * scale).astype(jnp.bfloat16))
            grad_scores = jnp.concatenate(grad_scores, axis=1)
            grad_query = jnp.dot(grad_scores, keys, preferred_element_type=jnp.float32)
            projected_ref[:, lo : lo + 2 * HD] = unturn(grad_query).astype(jnp.bfloat16)
            query = rotated_ref[m, :, lo : lo + 2 * HD]
            key_sum = key_sum + lax.dot_general(
                grad_scores, query, ROWS, preferred_element_type=jnp.float32
            )
            value_sum = value_sum + lax.dot_general(
                softmax.astype(jnp.bfloat16),
                grad_heads,
                ROWS,
                preferred_element_type=jnp.float32,
            )
        grad_key = unturn(key_sum[:length] + pltpu.roll(key_sum[length:], HD, 1))
        grad_value = pltpu.roll(value_sum[:length], HD, 1) + value_sum[length:]
        projected_ref[:, at : at + 2 * HD] = jnp.where(
            lane < HD, grad_key, grad_value
        ).astype(jnp.bfloat16)
    partial = lax.dot_general(
        projected_ref[...], wqkv_ref[...], COLS, preferred_element_type=jnp.float32
    ).astype(jnp.bfloat16)
    for k in range(nt):
        partial_refs[k][...] = partial[k * own : (k + 1) * own]


def choose_kernel(flag, where_ref, chosen_ref, otherwise_ref, out_ref):
    out_ref[...] = jnp.where(where_ref[flag] == 1, chosen_ref[...], otherwise_ref[...])


def norm_kernel(m, _, x_ref, grad_ref, gain_ref, *refs):
    grad_normed = refs[0][...].astype(jnp.float32)
    for ref in refs[1:-1]:
        grad_normed = grad_normed + ref[...].astype(jnp.float32)
    rows = x_ref[m].astype(jnp.float32)
    inverse = lax.rsqrt(jnp.mean(rows * rows, axis=-1, keepdims=True) + epsilon)
    unit = rows * inverse
    grad_unit = grad_normed * gain_ref[m]
    grad_rows = inverse * (
        grad_unit - unit * jnp.mean(grad_unit * unit, axis=-1, keepdims=True)
    )
    refs[-1][...] = (grad_ref[...].astype(jnp.float32) + grad_rows).astype(jnp.bfloat16)


def gain_kernel(nt, given, flag_ref, *refs):
    parts, partials, out_ref = refs[:given], refs[given:-1], refs[-1]
    for m in range(2):
        total = None
        for k, block in enumerate(pick(parts, nt, flag_ref, m)):
            rows = block.astype(jnp.float32)
            inverse = lax.rsqrt(jnp.mean(rows * rows, axis=-1, keepdims=True) + epsilon)
            term = partials[m * nt + k][...].astype(jnp.float32) * (rows * inverse)
            total = term if total is None else total + term
        out_ref[m] = jnp.sum(total, axis=0, keepdims=True)


def weight_kernel(count, rights, *refs):
    def joined(some):
        return jnp.concatenate([r[0] if len(r.shape) == 3 else r[...] for r in some], axis=0)

    total = lax.dot_general(
        joined(refs[:count]),
        joined(refs[count : count + rights]),
        ROWS,
        preferred_element_type=jnp.float32,
    )
    refs[-1][0] = total.astype(jnp.bfloat16)


def call(kernel, inputs, outs, flops):
    whole = pl.BlockSpec(memory_space=pltpu.VMEM)
    moved = sum(math.prod(a.shape) * a.dtype.itemsize for a in [*inputs, *outs])
    return pl.pallas_call(
        kernel,
        out_shape=outs,
        in_specs=[pl.BlockSpec(memory_space=pltpu.SMEM)] + [whole] * (len(inputs) - 1),
        out_specs=[whole] * len(outs),
        cost_estimate=pl.CostEstimate(flops=flops, bytes_accessed=moved, transcendentals=0),
        compiler_params=pltpu.CompilerParams(vmem_limit_bytes=VMEM_BYTES),
    )(*inputs)


def weight_grad(lefts, rights, split_left, only=None, earlier=None):
    members = 2
    depth = sum(a.shape[-2] for a in lefts)
    high, wide = lefts[0].shape[-1], rights[0].shape[-1]
    extent = high if split_left else wide
    tile = 640 if extent % 640 == 0 else extent

    def member(m):
        return m if only is None else only

    def spec(a, tiled):
        rows, columns = a.shape[-2], tile if tiled else a.shape[-1]
        if len(a.shape) == 3:
            return pl.BlockSpec(
                (1, rows, columns), lambda m, i: (member(m), 0, i if tiled else 0)
            )
        return pl.BlockSpec((rows, columns), lambda m, i: (0, i if tiled else 0))

    specs = [spec(a, split_left) for a in lefts] + [spec(a, not split_left) for a in rights]
    inputs = [*lefts, *rights]
    aliases = {}
    if earlier is not None:
        aliases = {len(inputs): 0}
        inputs.append(earlier)
        specs.append(pl.BlockSpec(memory_space=pl.ANY))
    if split_left:
        out = pl.BlockSpec((1, tile, wide), lambda m, i: (member(m), i, 0))
    else:
        out = pl.BlockSpec((1, high, tile), lambda m, i: (member(m), 0, i))
    count = members if only is None else 1
    return pl.pallas_call(
        functools.partial(weight_kernel, len(lefts), len(rights)),
        grid=(count, extent // tile),
        out_shape=jax.ShapeDtypeStruct((members, high, wide), jnp.bfloat16),
        in_specs=specs,
        out_specs=out,
        input_output_aliases=aliases,
        cost_estimate=pl.CostEstimate(
            flops=2 * count * depth * high * wide,
            bytes_accessed=2 * count * (depth * (high + wide) + high * wide),
            transcendentals=0,
        ),
        compiler_params=pltpu.CompilerParams(vmem_limit_bytes=VMEM_BYTES),
    )(*inputs)


def shift(value, axis, steps):
    count = lax.axis_size(axis)
    return lax.ppermute(value, axis, [(i, (i + steps) % count) for i in range(count)])


def sum_over(value, axis):
    count = lax.axis_size(axis)
    if count & (count - 1):
        return lax.psum(value, axis)
    terms = [value] + [
        lax.ppermute(value, axis, [(i, i ^ step) for i in range(count)]) for step in range(1, count)
    ]
    while len(terms) > 1:
        terms = [terms[i] + terms[i + 1] for i in range(0, len(terms), 2)]
    return terms[0]


def local(layer_in, carry_in, top_grad, w_qkv, w_out, gain):
    ticks = layer_in.shape[0]
    own_rows = layer_in.shape[4]
    width = layer_in.shape[5]
    nt = lax.axis_size("tensor")
    ns = lax.axis_size("section")
    nd = lax.axis_size("dp")
    length = own_rows * nt
    section = lax.axis_index("section")
    place = lax.axis_index("tensor")
    replica = lax.axis_index("dp")
    at_first = section == 0
    at_last = section == ns - 1
    at_far_low, at_far_high = place == 0, place == nt - 1
    x_rows = layer_in[:, :, 0, 0]
    carried = carry_in[:, 0, 0]
    fresh_rows = top_grad[:, 0]
    weight_qkv = [w_qkv[m, 0] for m in range(2)]
    weight_out = [w_out[m, 0] for m in range(2)]
    qkv_width = w_qkv.shape[3]
    head_width = w_out.shape[2]
    kv_local = qkv_width // ((GROUP + 2) * HD)
    bf16, f32 = jnp.bfloat16, jnp.float32

    block = jnp.arange(length) // own_rows
    positions = lax.rem(place - block + nt, nt) * own_rows + lax.rem(jnp.arange(length), own_rows)
    lanes = jnp.arange(2 * HD)
    frequency = rope_base ** (-((lanes % (HD // 2)).astype(f32) * (2.0 / HD)))
    angle = positions.astype(f32)[:, None] * frequency[None, :]
    cosine = jnp.cos(angle)
    sine = jnp.where(lanes[None, :] % HD < HD // 2, -jnp.sin(angle), jnp.sin(angle))
    bias = jnp.where(positions[:, None] >= positions[None, :], 0.0, -1e30).astype(f32)

    def gather_rotated(value):
        parts = [value]
        for k in range(1, nt):
            parts.append(shift(value, "tensor", k))
        return parts

    def gather_line(near, far):
        if nt != 4:
            return gather_rotated(near)
        middle = shift(far, "tensor", 2)
        ahead = lax.ppermute(near, "tensor", [(i, i + 1) for i in range(nt - 1)])
        behind = lax.ppermute(near, "tensor", [(i, i - 1) for i in range(1, nt)])
        ends = lax.ppermute(middle, "tensor", [(1, 0), (nt - 2, nt - 1)])
        return [near, ahead, middle, behind, ends]

    def slice_for(value, p):
        extent = value.shape[2] // nd
        return lax.dynamic_slice_in_dim(value, ((replica + p) % nd) * extent, extent, axis=2)

    def peers(value, columns):
        return [shift(slice_for(value, p) if columns else value, "dp", p) for p in range(1, nd)]

    def send_parts(parts):
        sent = []
        for part in parts:
            sent.append(peers(part, False))
        return sent

    def shaped(*shape, dtype=bf16):
        return jax.ShapeDtypeStruct((2,) + shape, dtype)

    where = jnp.stack([place, at_last, at_first, at_far_low, at_far_high]).astype(jnp.int32)

    def choose(flag, chosen, otherwise):
        return call(
            functools.partial(choose_kernel, flag),
            [where, chosen, otherwise],
            [jax.ShapeDtypeStruct(otherwise.shape, bf16)],
            own_rows * width,
        )[0]


    def settled(parts):
        if len(parts) == nt:
            return parts
        parts, ends = list(parts[:nt]), parts[nt]
        parts[1] = choose(3, ends, parts[1])
        parts[nt - 1] = choose(4, ends, parts[nt - 1])
        return parts

    def forward(parts):
        return call(
            functools.partial(forward_kernel, nt, len(parts), kv_local),
            [where, *parts, gain[:, 0:1], *weight_qkv, cosine, sine, bias],
            [
                shaped(length, width),
                shaped(length, head_width),
                shaped(length, qkv_width),
                shaped(length, kv_local * GROUP * length, dtype=f32),
            ],
            4 * length * width * qkv_width,
        )

    def backward(parts, m, rotated, softmax):
        outs = call(
            functools.partial(backward_kernel, nt, len(parts), kv_local, m),
            [where, *parts, weight_out[m], weight_qkv[m], rotated, softmax, cosine, sine],
            [jax.ShapeDtypeStruct((length, qkv_width), bf16)]
            + [jax.ShapeDtypeStruct((own_rows, width), bf16)] * nt,
            2 * length * width * (qkv_width + head_width),
        )
        return outs[0], outs[1:]

    members = (1, 0)
    x_parts = gather_rotated(x_rows[0])
    own_grads = [carried[0], carried[1]]
    first_parts = gather_line(carried, carried)
    grad_parts = [first_parts, first_parts]
    normed, attended, rotated, softmax = forward(x_parts)
    normed_peers = peers(normed, True)
    attended_peers = peers(attended, True)
    placed = settled(first_parts)
    shared = send_parts(placed)
    placed, sent_parts = [placed, placed], [shared, shared]
    qkv_lefts, qkv_rights, out_lefts, out_rights = [], [], [], [[], []]
    gain_total = 0.0
    per_tick = []
    for t in range(ticks):
        projected = [None, None]
        partials, received = [None, None], [[], []]
        for m in members:
            projected[m], partials[m] = backward(grad_parts[m], m, rotated, softmax)
            for k in range(1, nt):
                received[m].append(shift(partials[m][k], "tensor", -k))
        projected = jnp.stack(projected)
        projected_peers = peers(projected, False)
        gain_total = gain_total + call(
            functools.partial(gain_kernel, nt, len(x_parts)),
            [where, *x_parts, *partials[0], *partials[1]],
            [shaped(1, width, dtype=f32)],
            2 * length * width,
        )[0]
        outcome = [None, None]
        for m in members:
            outcome[m] = call(
                functools.partial(norm_kernel, m),
                [where, x_parts[0], own_grads[m], gain[:, 0:1], partials[m][0], *received[m]],
                [jax.ShapeDtypeStruct((own_rows, width), bf16)],
                own_rows * width,
            )[0]
        per_tick.append(jnp.stack(outcome))
        qkv_lefts.extend([slice_for(normed, 0), *normed_peers])
        qkv_rights.extend([projected, *projected_peers])
        out_lefts.extend([slice_for(attended, 0), *attended_peers])
        for m in members:
            out_rights[m].extend(placed[m])
            for p in range(nd - 1):
                out_rights[m].extend(g[p] for g in sent_parts[m])
        if t + 1 < ticks:
            later = x_rows[t + 1]
            if t > 0:
                later, _ = lax.optimization_barrier((later, received))
            x_parts = gather_line(later, later)
            normed, attended, rotated, softmax = forward(x_parts)
            normed_peers = peers(normed, True)
            attended_peers = peers(attended, True)
            own_grads, grad_parts, sent_parts = [None, None], [None, None], [None, None]
            for m in members:
                if m == 1:
                    moves = [(s, s + 1) for s in range(ns - 1)]
                    came = lax.ppermute(outcome[1], "section", moves)
                    own_grads[1] = choose(2, fresh_rows[t], came)
                else:
                    moves = [(s, s - 1) for s in range(1, ns)]
                    came = lax.ppermute(outcome[0], "section", moves)
                    own_grads[0] = choose(1, outcome[1], came)
                grad_parts[m] = gather_rotated(own_grads[m])
                sent_parts[m] = send_parts(grad_parts[m])
            placed = grad_parts

    grad_out = None
    for m in members:
        grad_out = weight_grad(out_lefts, out_rights[m], False, m, grad_out)
    grad_qkv = weight_grad(qkv_lefts, qkv_rights, True)
    for axis in ("dp", "tensor"):
        gain_total = sum_over(gain_total, axis)
    return (
        jnp.stack(per_tick)[:, :, None, None],
        grad_qkv[:, None],
        grad_out[:, None],
        gain_total,
    )


def solution(mesh):
    in_specs = (
        P(None, None, "section", "dp", "tensor", None),
        P(None, "section", "dp", "tensor", None),
        P(None, "dp", "tensor", None),
        P(None, "section", None, "tensor"),
        P(None, "section", "tensor", None),
        P(None, "section", None),
    )
    out_specs = (
        P(None, None, "section", "dp", "tensor", None),
        P(None, "section", "dp", "tensor"),
        P(None, "section", ("tensor", "dp"), None),
        P(None, "section", None),
    )

    return jax.shard_map(local, mesh=mesh, in_specs=in_specs, out_specs=out_specs, check_vma=False)
```

time: 273 us -> 277 us (1.015)
  waiting for transfers between devices: 137 us -> 103 us
  Pallas kernels: 35.3 us -> 52.4 us
  starting transfers between devices: 81.1 us -> 97.3 us
  local copies, waits for them, and re-layouts: 11.9 us -> 20 us
    ppermute x32 -> x41, waiting for transfers between devices: 131 us -> 86.8 us  [shift(): lax.ppermute(value, axis, [(i, (i + steps) % count) for i in range(count)])]
    ppermute x2 -> x8, starting transfers between devices: 6.43 us -> 24.4 us  [the longest x2 14.9 us: gather_line(): ahead = lax.ppermute(near, 'tensor', [(i, i + 1) for i in range(nt - 1)])]
    pallas_call x8 -> x19, Pallas kernels: 35.3 us -> 52.4 us  [the longest x16 40.4 us: call(): pl.pallas_call(kernel, out_shape=outs, in_specs=[pl.BlockSpec(memory_spac...]
    ppermute x4, waiting for transfers between devices: 3.09 us -> 14 us  [sum_over(): lax.ppermute(value, axis, [(i, i ^ step) for i in range(count)])]
    unnamed x21 -> x78, local copies, waits for them, and re-layouts: 2.05 us -> 7.75 us
    squeeze x1, local copies, waits for them, and re-layouts: 2.27 us -> 5.33 us  [local(): weight_qkv = [w_qkv[m, 0] for m in range(2)]]
    ppermute x32 -> x41, starting transfers between devices: 69.7 us -> 67.3 us  [shift(): lax.ppermute(value, axis, [(i, (i + steps) % count) for i in range(count)])]
  transfers between devices with their start and end apart: 38 -> 53, of which waited for: 18 -> 13; matrix products, arithmetic and copies ran while one was open for 5% -> 5% of each run, Pallas kernels for 11% -> 16%
where the time goes in v1:
time: 277 us; the launch traced here: 276 us
  waiting for transfers between devices  103 us (37%)
  starting transfers between devices  97.3 us (35%)
  Pallas kernels  52.4 us (19%)
  local copies, waits for them, and re-layouts  20 us (7%)
    ppermute x41, waiting for transfers between devices, shift(): lax.ppermute(value, axis, [(i, (i + steps) % count) for i in range(count)])  86.8 us
    ppermute x41, starting transfers between devices, shift(): lax.ppermute(value, axis, [(i, (i + steps) % count) for i in range(count)])  67.3 us
    pallas_call x16, Pallas kernels, call(): pl.pallas_call(kernel, out_shape=outs, in_specs=[pl.BlockSpec(memory_spac...  40.4 us
    ppermute x2, starting transfers between devices, gather_line(): ahead = lax.ppermute(near, 'tensor', [(i, i + 1) for i in range(nt - 1)])  14.9 us
    ppermute x4, waiting for transfers between devices, sum_over(): lax.ppermute(value, axis, [(i, i ^ step) for i in range(count)])  14 us
    pallas_call x3, Pallas kernels, weight_grad(): pl.pallas_call(functools.partial(weight_kernel, len(lefts), len(rights)),...  12.1 us
    unnamed x78, local copies, waits for them, and re-layouts  7.75 us
    ppermute x4, starting transfers between devices, sum_over(): lax.ppermute(value, axis, [(i, i ^ step) for i in range(count)])  5.61 us
  transfers between devices with their start and end apart: 53, of which 13 were waited for; matrix products, arithmetic and copies ran while one was open for 5% of the time, Pallas kernels for 16%

profile of v1, /device:TPU:0, one launch (start us, length us, event | category | flops | bytes accessed | tf_op | source)
XLA Modules:
  0.0 275.8 jit_solution(1179178501013631086)
XLA Ops:
  0.6 2.0 slice_bitcast_fusion.5
  2.6 3.1 %collective-permute-start.4 = (bf16[2,32,2560]{2,1,0:T(8,128)(2,1)}, bf16[2,32,2560]{2,1,0:T(8,128)(2,1)}, u32[]{:S(2)}, u32[]{:S(2)}) collective-permute-start(bf16[2,32,2560]{2,1,0:T(8,128)(2,1)} %get-tuple-element.72.refs_0_.x_ref), channel_id=1, source_target_pairs={{0,2},{2,4},{4,6},{6,0},{1,3},{3,5},{5,7},{7,1},{8,10},{10,12},{12... | collective-permute-start | bytes 983048 | tf_op jit(solution)/shard_map/ppermute | solution.py:264
  5.6 2.6 collective-permute-start.5
  8.2 1.3 collective-permute-start.6
  9.7 3.5 %collective-permute-start = (bf16[2,32,2560]{2,1,0:T(8,128)(2,1)}, bf16[2,32,2560]{2,1,0:T(8,128)(2,1)}, u32[]{:S(2)}, u32[]{:S(2)}) collective-permute-start(bf16[2,32,2560]{2,1,0:T(8,128)(2,1)} %bitcast.8.refs_0_.refs_4_), channel_id=1, source_target_pairs={{0,2},{2,4},{4,6},{1,3},{3,5},{5,7},{8,10},{10,12},{12,14},{9,11},... | collective-permute-start | bytes 983048 | tf_op jit(solution)/shard_map/ppermute | solution.py:322
  13.3 5.3 %slice_bitcast_fusion.1 = (bf16[2560,640]{1,0:T(8,128)(2,1)}, bf16[2560,640]{1,0:T(8,128)(2,1)S(1)}) fusion(bf16[2,1,2560,640]{3,2,1,0:T(8,128)(2,1)} %param.9), kind=kLoop, calls=%fused_computation.1 | loop fusion | bytes 13107200 | tf_op jit(solution)/shard_map/squeeze | solution.py:296
  18.6 2.7 slice_bitcast_fusion.3
  21.4 1.3 collective-permute-start.2
  22.7 28.3 %collective-permute-done.1.refs_2_.refs_6_ = bf16[2,32,2560]{2,1,0:T(8,128)(2,1)} collective-permute-done((bf16[2,32,2560]{2,1,0:T(8,128)(2,1)}, bf16[2,32,2560]{2,1,0:T(8,128)(2,1)}, u32[]{:S(2)}, u32[]{:S(2)}) %collective-permute-start.1) | collective-permute-done | bytes 327712 | tf_op jit(solution)/shard_map/ppermute | solution.py:264
  51.0 1.3 collective-permute-start.3
  52.7 1.9 copy-done
  54.7 4.6 %shard_map.93 = (bf16[2,128,2560]{2,1,0:T(8,128)(2,1)S(1)}, bf16[2,128,512]{2,1,0:T(8,128)(2,1)S(1)}, bf16[2,128,640]{2,1,0:T(8,128)(2,1)S(1)}, f32[2,128,1024]{2,1,0:T(8,128)S(1)}) custom-call(s32[5]{0:T(128)S(1)} %stack.84.flag_ref._.where_ref, bf16[2,32,2560]{2,1,0:T(8,128)(2,1)} %get-tuple-element.72.refs_0_.x_ref, ...), custom_call_target="tpu_custom_call" | custom-call | flops 838860800 | bytes 11030548 | tf_op jit(solution)/shard_map/pallas_call | solution.py:206
  61.0 1.7 collective-permute-done.3.refs_4_.chosen_ref
  62.7 4.8 %shard_map.94 = (bf16[128,640]{1,0:T(8,128)(2,1)S(1)}, bf16[32,2560]{1,0:T(8,128)(2,1)S(1)}, bf16[32,2560]{1,0:T(8,128)(2,1)S(1)}, bf16[32,2560]{1,0:T(8,128)(2,1)S(1)}, bf16[32,2560]{1,0:T(8,128)(2,1)S(1)}) custom-call(s32[5]{0:T(128)S(1)} %stack.84.flag_ref._.where_ref, bf16[2,32,2560]{2,1,0:T(8,128)(2,1)} %bitcast.8.refs_0_.refs_4_, ...), custom_call_target="tpu_custom_call" | custom-call | flops 754974720 | bytes 9863188 | tf_op jit(solution)/shard_map/pallas_call | solution.py:206
  68.6 2.2 collective-permute-start.8
  72.6 4.6 %shard_map.96 = (bf16[128,640]{1,0:T(8,128)(2,1)S(1)}, bf16[32,2560]{1,0:T(8,128)(2,1)S(1)}, bf16[32,2560]{1,0:T(8,128)(2,1)S(1)}, bf16[32,2560]{1,0:T(8,128)(2,1)S(1)}, bf16[32,2560]{1,0:T(8,128)(2,1)S(1)}) custom-call(s32[5]{0:T(128)S(1)} %stack.84.flag_ref._.where_ref, bf16[2,32,2560]{2,1,0:T(8,128)(2,1)} %bitcast.8.refs_0_.refs_4_, ...), custom_call_target="tpu_custom_call" | custom-call | flops 754974720 | bytes 9863188 | tf_op jit(solution)/shard_map/pallas_call | solution.py:206
  77.9 2.8 %collective-permute-start.10 = (bf16[32,2560]{1,0:T(8,128)(2,1)S(1)}, bf16[32,2560]{1,0:T(8,128)(2,1)S(1)}, u32[]{:S(2)}, u32[]{:S(2)}) collective-permute-start(bf16[32,2560]{1,0:T(8,128)(2,1)S(1)} %get-tuple-element.39.refs_9_), channel_id=1, source_target_pairs={{0,6},{2,0},{4,2},{6,4},{1,7},{3,1},{5,3},{7,5},{8,14},{10,8},{12,... | collective-permute-start | bytes 491528 | tf_op jit(solution)/shard_map/ppermute | solution.py:264
  80.7 6.5 %collective-permute-start.11 = (bf16[32,2560]{1,0:T(8,128)(2,1)S(1)}, bf16[32,2560]{1,0:T(8,128)(2,1)S(1)}, u32[]{:S(2)}, u32[]{:S(2)}) collective-permute-start(bf16[32,2560]{1,0:T(8,128)(2,1)S(1)} %get-tuple-element.40.refs_10_), channel_id=1, source_target_pairs={{0,4},{2,6},{4,0},{6,2},{1,5},{3,7},{5,1},{7,3},{8,12},{10,14},{12... | collective-permute-start | bytes 491528 | tf_op jit(solution)/shard_map/ppermute | solution.py:264
  87.2 7.6 %collective-permute-done.8.refs_2_ = bf16[32,2560]{1,0:T(8,128)(2,1)S(1)} collective-permute-done((bf16[32,2560]{1,0:T(8,128)(2,1)S(1)}, bf16[32,2560]{1,0:T(8,128)(2,1)S(1)}, u32[]{:S(2)}, u32[]{:S(2)}) %collective-permute-start.8) | collective-permute-done | bytes 163872 | tf_op jit(solution)/shard_map/ppermute | solution.py:264
  95.9 11.4 %collective-permute-start.17 = (bf16[2,32,2560]{2,1,0:T(8,128)(2,1)}, bf16[2,32,2560]{2,1,0:T(8,128)(2,1)}, u32[]{:S(2)}, u32[]{:S(2)}) collective-permute-start(bf16[2,32,2560]{2,1,0:T(8,128)(2,1)} %get-tuple-element.73.refs_0_.x_ref), channel_id=1, source_target_pairs={{0,2},{2,4},{4,6},{1,3},{3,5},{5,7},{8,10},{10,12},{12,14},{9,11},... | collective-permute-start | bytes 983048 | tf_op jit(solution)/shard_map/ppermute | solution.py:322
  107.3 1.3 shard_map.95
  108.6 1.3 collective-permute-start.19
  109.9 1.3 collective-permute-start.20
  111.2 2.6 collective-permute-done.11.refs_2_
  113.8 1.3 collective-permute-start.13
  115.1 1.3 shard_map.97.chosen_ref
  116.4 3.0 %collective-permute-start.24 = (bf16[32,2560]{1,0:T(8,128)(2,1)S(1)}, bf16[32,2560]{1,0:T(8,128)(2,1)S(1)}, u32[]{:S(2)}, u32[]{:S(2)}) collective-permute-start(bf16[32,2560]{1,0:T(8,128)(2,1)S(1)} %shard_map.97.chosen_ref), channel_id=1, source_target_pairs={{0,8},{8,16},{16,24},{1,9},{9,17},{17,25},{2,10},{10,18},{18,26},{... | collective-permute-start | bytes 491528 | tf_op jit(solution)/shard_map/ppermute | solution.py:442
  119.4 1.2 shard_map.98.refs_0_.grad_ref.refs_12_
  122.8 2.6 collective-permute-start.15
  127.9 3.0 %collective-permute-start.16 = (bf16[32,2560]{1,0:T(8,128)(2,1)}, bf16[32,2560]{1,0:T(8,128)(2,1)S(1)}, u32[]{:S(2)}, u32[]{:S(2)}) collective-permute-start(bf16[32,2560]{1,0:T(8,128)(2,1)} %shard_map.98.refs_0_.grad_ref.refs_12_), channel_id=1, source_target_pairs={{0,6},{2,0},{4,2},{6,4},{1,7},{3,1},{5,3},{7,5},{8,14},{10,8},{12,... | collective-permute-start | bytes 491528 | tf_op jit(solution)/shard_map/ppermute | solution.py:264
  131.6 3.4 %collective-permute-start.27 = (bf16[32,2560]{1,0:T(8,128)(2,1)S(1)}, bf16[32,2560]{1,0:T(8,128)(2,1)S(1)}, u32[]{:S(2)}, u32[]{:S(2)}) collective-permute-start(bf16[32,2560]{1,0:T(8,128)(2,1)S(1)} %shard_map.102.refs_0_.grad_ref.refs_12_), channel_id=1, source_target_pairs={{0,6},{2,0},{4,2},{6,4},{1,7},{3,1},{5,3},{7,5},{8,14},{10,8},{12,... | collective-permute-start | bytes 491528 | tf_op jit(solution)/shard_map/ppermute | solution.py:264
  138.3 2.2 shard_map.110
  140.5 1.6 collective-permute-start.37
  142.1 4.5 %shard_map.99 = (bf16[2,128,2560]{2,1,0:T(8,128)(2,1)S(1)}, bf16[2,128,512]{2,1,0:T(8,128)(2,1)S(1)}, bf16[2,128,640]{2,1,0:T(8,128)(2,1)S(1)}, f32[2,128,1024]{2,1,0:T(8,128)S(1)}) custom-call(s32[5]{0:T(128)S(1)} %stack.84.flag_ref._.where_ref, bf16[2,32,2560]{2,1,0:T(8,128)(2,1)} %get-tuple-element.73.refs_0_.x_ref, ...), custom_call_target="tpu_custom_call" | custom-call | flops 838860800 | bytes 11358228 | tf_op jit(solution)/shard_map/pallas_call | solution.py:206
  147.4 4.5 %shard_map.100 = (bf16[128,640]{1,0:T(8,128)(2,1)S(1)}, bf16[32,2560]{1,0:T(8,128)(2,1)S(1)}, bf16[32,2560]{1,0:T(8,128)(2,1)S(1)}, bf16[32,2560]{1,0:T(8,128)(2,1)S(1)}, bf16[32,2560]{1,0:T(8,128)(2,1)S(1)}) custom-call(s32[5]{0:T(128)S(1)} %stack.84.flag_ref._.where_ref, bf16[32,2560]{1,0:T(8,128)(2,1)} %shard_map.98.refs_0_.grad_ref.refs_12_, ...), custom_call_target="tpu_custom_call" | custom-call | flops 754974720 | bytes 8880148 | tf_op jit(solution)/shard_map/pallas_call | solution.py:206
  151.8 1.4 collective-permute-start.38
  153.9 3.8 %shard_map.103 = (bf16[128,640]{1,0:T(8,128)(2,1)S(1)}, bf16[32,2560]{1,0:T(8,128)(2,1)S(1)}, bf16[32,2560]{1,0:T(8,128)(2,1)S(1)}, bf16[32,2560]{1,0:T(8,128)(2,1)S(1)}, bf16[32,2560]{1,0:T(8,128)(2,1)S(1)}) custom-call(s32[5]{0:T(128)S(1)} %stack.84.flag_ref._.where_ref, bf16[32,2560]{1,0:T(8,128)(2,1)S(1)} %shard_map.102.refs_0_.grad_ref.refs_12_, ...), custom_call_target="tpu_custom_call" | custom-call | flops 754974720 | bytes 8880148 | tf_op jit(solution)/shard_map/pallas_call | solution.py:206
  157.7 2.4 shard_map.111
  160.2 1.4 collective-permute-start.49
  162.3 10.4 %collective-permute-done.49 = f32[2,1,2560]{2,1,0:T(1,128)S(1)} collective-permute-done((f32[2,1,2560]{2,1,0:T(1,128)S(1)}, f32[2,1,2560]{2,1,0:T(1,128)S(1)}, u32[]{:S(2)}, u32[]{:S(2)}) %collective-permute-start.49) | collective-permute-done | bytes 20512 | tf_op jit(solution)/shard_map/ppermute | solution.py:272
  172.8 1.6 collective-permute-start.36
  175.6 1.6 collective-permute-start.45
  177.2 9.8 %collective-permute-start.21 = (bf16[32,2560]{1,0:T(8,128)(2,1)S(1)}, bf16[32,2560]{1,0:T(8,128)(2,1)S(1)}, u32[]{:S(2)}, u32[]{:S(2)}) collective-permute-start(bf16[32,2560]{1,0:T(8,128)(2,1)S(1)} %get-tuple-element.45.refs_6_), channel_id=1, source_target_pairs={{0,6},{2,0},{4,2},{6,4},{1,7},{3,1},{5,3},{7,5},{8,14},{10,8},{12,... | collective-permute-start | bytes 491528 | tf_op jit(solution)/shard_map/ppermute | solution.py:264
  187.5 1.5 collective-permute-start.47
  189.1 2.4 collective-permute-start.51
  191.6 1.3 collective-permute-done.50
  192.8 1.8 collective-permute-start.52
  194.7 1.8 collective-permute-start.22
  196.5 2.3 collective-permute-done.52
  199.1 3.5 %collective-permute-start.28 = (bf16[32,2560]{1,0:T(8,128)(2,1)S(1)}, bf16[32,2560]{1,0:T(8,128)(2,1)S(1)}, u32[]{:S(2)}, u32[]{:S(2)}) collective-permute-start(bf16[32,2560]{1,0:T(8,128)(2,1)S(1)} %get-tuple-element.49.refs_10_), channel_id=1, source_target_pairs={{0,6},{2,0},{4,2},{6,4},{1,7},{3,1},{5,3},{7,5},{8,14},{10,8},{12,... | collective-permute-start | bytes 491528 | tf_op jit(solution)/shard_map/ppermute | solution.py:264
  203.4 7.1 %collective-permute-done.22.refs_2_ = bf16[32,2560]{1,0:T(8,128)(2,1)S(1)} collective-permute-done((bf16[32,2560]{1,0:T(8,128)(2,1)S(1)}, bf16[32,2560]{1,0:T(8,128)(2,1)S(1)}, u32[]{:S(2)}, u32[]{:S(2)}) %collective-permute-start.22) | collective-permute-done | bytes 163872 | tf_op jit(solution)/shard_map/ppermute | solution.py:264
  211.3 1.2 collective-permute-start.48
  213.3 6.9 %collective-permute-done.29.refs_2_ = bf16[32,2560]{1,0:T(8,128)(2,1)S(1)} collective-permute-done((bf16[32,2560]{1,0:T(8,128)(2,1)S(1)}, bf16[32,2560]{1,0:T(8,128)(2,1)S(1)}, u32[]{:S(2)}, u32[]{:S(2)}) %collective-permute-start.29) | collective-permute-done | bytes 163872 | tf_op jit(solution)/shard_map/ppermute | solution.py:264
  220.8 1.5 collective-permute-start.44
  222.9 1.3 shard_map.101
  224.2 1.3 shard_map.104
  226.1 3.9 %shard_map.108.refs_20_ = bf16[2,256,2560]{2,1,0:T(8,128)(2,1)} custom-call(bf16[2,128,256]{2,1,0:T(8,128)(2,1)S(1)} %get-tuple-element.79.refs_0_, bf16[2,128,256]{2,1,0:T(8,128)(2,1)S(1)} %collective-permute-done.35.refs_1_, bf16[2,128,256]{2,1,0:T(8,128)(2,1)S(1)} %get-tuple-element.77.refs_2_, bf16[2,128,256]{2,1,0:T(8,128)(2,1)S(1)} %collective-permute-done.36.refs_3_, ...), custom_call_target="tpu_custom_call" | custom-call | flops 671088640 | bytes 4194304 | tf_op jit(solution)/shard_map/pallas_call | solution.py:246
  229.9 1.5 collective-permute-start.33
  232.0 1.5 collective-permute-start.34
  233.5 4.0 %shard_map.109 = bf16[2,256,2560]{2,1,0:T(8,128)(2,1)} custom-call(bf16[2,128,256]{2,1,0:T(8,128)(2,1)S(1)} %get-tuple-element.79.refs_0_, bf16[2,128,256]{2,1,0:T(8,128)(2,1)S(1)} %collective-permute-done.35.refs_1_, bf16[2,128,256]{2,1,0:T(8,128)(2,1)S(1)} %get-tuple-element.77.refs_2_, ...), custom_call_target="tpu_custom_call", output_to_operand_aliasing={{}: (20, {})} | custom-call | flops 671088640 | bytes 4194304 | tf_op jit(solution)/shard_map/pallas_call | solution.py:246
  238.4 13.7 %collective-permute-done.33.refs_5_ = bf16[2,128,640]{2,1,0:T(8,128)(2,1)S(1)} collective-permute-done((bf16[2,128,640]{2,1,0:T(8,128)(2,1)S(1)}, bf16[2,128,640]{2,1,0:T(8,128)(2,1)S(1)}, u32[]{:S(2)}, u32[]{:S(2)}) %collective-permute-start.33) | collective-permute-done | bytes 327712 | tf_op jit(solution)/shard_map/ppermute | solution.py:264
  252.1 14.0 %collective-permute-done.32.refs_3_ = bf16[2,128,1280]{2,1,0:T(8,128)(2,1)S(1)} collective-permute-done((bf16[2,128,1280]{2,1,0:T(8,128)(2,1)S(1)}, bf16[2,128,1280]{2,1,0:T(8,128)(2,1)S(1)}, u32[]{:S(2)}, u32[]{:S(2)}) %collective-permute-start.32) | collective-permute-done | bytes 655392 | tf_op jit(solution)/shard_map/ppermute | solution.py:264
  266.1 5.4 %collective-permute-done.34.refs_7_ = bf16[2,128,640]{2,1,0:T(8,128)(2,1)S(1)} collective-permute-done((bf16[2,128,640]{2,1,0:T(8,128)(2,1)S(1)}, bf16[2,128,640]{2,1,0:T(8,128)(2,1)S(1)}, u32[]{:S(2)}, u32[]{:S(2)}) %collective-permute-start.34) | collective-permute-done | bytes 327712 | tf_op jit(solution)/shard_map/ppermute | solution.py:264
  271.6 4.2 %shard_map.105 = bf16[2,1280,640]{2,1,0:T(8,128)(2,1)} custom-call(bf16[2,128,1280]{2,1,0:T(8,128)(2,1)S(1)} %get-tuple-element.71.refs_0_, bf16[2,128,1280]{2,1,0:T(8,128)(2,1)S(1)} %collective-permute-done.31.refs_1_, bf16[2,128,1280]{2,1,0:T(8,128)(2,1)S(1)} %get-tuple-element.69.refs_2_, bf16[2,128,1280]{2,1,0:T(8,128)(2,1)S(1)} %collective-permute-done.32.refs_3_, ...), custom_call_target="tpu_custom_call" | custom-call | flops 1677721600 | bytes 7208960 | tf_op jit(solution)/shard_map/pallas_call | solution.py:246
  (162 shorter events, 25.5 us)
Async XLA Ops:
  2.6 18.8 %collective-permute-start.4 = (bf16[2,32,2560]{2,1,0:T(8,128)(2,1)}, bf16[2,32,2560]{2,1,0:T(8,128)(2,1)}, u32[]{:S(2)}, u32[]{:S(2)}) collective-permute-start(bf16[2,32,2560]{2,1,0:T(8,128)(2,1)} %get-tuple-element.72.refs_0_.x_ref), channel_id=1, source_target_pairs={{0,2},{2,4},{4,6},{6,0},{1,3},{3,5},{5,7},{7,1},{8,10},{10,12},{12... | collective-permute-start | bytes 983048 | tf_op jit(solution)/shard_map/ppermute | solution.py:264
  5.6 47.1 %collective-permute-start.5 = (bf16[2,32,2560]{2,1,0:T(8,128)(2,1)}, bf16[2,32,2560]{2,1,0:T(8,128)(2,1)}, u32[]{:S(2)}, u32[]{:S(2)}) collective-permute-start(bf16[2,32,2560]{2,1,0:T(8,128)(2,1)} %get-tuple-element.72.refs_0_.x_ref), channel_id=1, source_target_pairs={{0,4},{2,6},{4,0},{6,2},{1,5},{3,7},{5,1},{7,3},{8,12},{10,14},{12... | collective-permute-start | bytes 983048 | tf_op jit(solution)/shard_map/ppermute | solution.py:264
  8.2 44.5 %collective-permute-start.6 = (bf16[2,32,2560]{2,1,0:T(8,128)(2,1)}, bf16[2,32,2560]{2,1,0:T(8,128)(2,1)}, u32[]{:S(2)}, u32[]{:S(2)}) collective-permute-start(bf16[2,32,2560]{2,1,0:T(8,128)(2,1)} %get-tuple-element.72.refs_0_.x_ref), channel_id=1, source_target_pairs={{0,6},{2,0},{4,2},{6,4},{1,7},{3,1},{5,3},{7,5},{8,14},{10,8},{12,... | collective-permute-start | bytes 983048 | tf_op jit(solution)/shard_map/ppermute | solution.py:264
  9.6 41.4 %collective-permute-start.1 = (bf16[2,32,2560]{2,1,0:T(8,128)(2,1)}, bf16[2,32,2560]{2,1,0:T(8,128)(2,1)}, u32[]{:S(2)}, u32[]{:S(2)}) collective-permute-start(bf16[2,32,2560]{2,1,0:T(8,128)(2,1)} %bitcast.8.refs_0_.refs_4_), channel_id=1, source_target_pairs={{0,4},{2,6},{4,0},{6,2},{1,5},{3,7},{5,1},{7,3},{8,12},{10,14},{12... | collective-permute-start | bytes 983048 | tf_op jit(solution)/shard_map/ppermute | solution.py:264
  9.7 51.3 %collective-permute-start = (bf16[2,32,2560]{2,1,0:T(8,128)(2,1)}, bf16[2,32,2560]{2,1,0:T(8,128)(2,1)}, u32[]{:S(2)}, u32[]{:S(2)}) collective-permute-start(bf16[2,32,2560]{2,1,0:T(8,128)(2,1)} %bitcast.8.refs_0_.refs_4_), channel_id=1, source_target_pairs={{0,2},{2,4},{4,6},{1,3},{3,5},{5,7},{8,10},{10,12},{12,14},{9,11},... | collective-permute-start | bytes 983048 | tf_op jit(solution)/shard_map/ppermute | solution.py:322
  18.6 34.1 %copy-start.11 = (f32[2,1,2560]{2,1,0:T(1,128)S(1)}, f32[2,1,2560]{2,1,0:T(1,128)}, u32[]{:S(2)}) copy-start(f32[2,1,2560]{2,1,0:T(1,128)} %gain_ref.7) | copy-start | bytes 61444
  21.4 39.6 %collective-permute-start.2 = (bf16[2,32,2560]{2,1,0:T(8,128)(2,1)}, bf16[2,32,2560]{2,1,0:T(8,128)(2,1)}, u32[]{:S(2)}, u32[]{:S(2)}) collective-permute-start(bf16[2,32,2560]{2,1,0:T(8,128)(2,1)} %bitcast.8.refs_0_.refs_4_), channel_id=1, source_target_pairs={{2,0},{4,2},{6,4},{3,1},{5,3},{7,5},{10,8},{12,10},{14,12},{11,9},... | collective-permute-start | bytes 983048 | tf_op jit(solution)/shard_map/ppermute | solution.py:323
  51.0 11.7 %collective-permute-start.3 = (bf16[2,32,2560]{2,1,0:T(8,128)(2,1)}, bf16[2,32,2560]{2,1,0:T(8,128)(2,1)}, u32[]{:S(2)}, u32[]{:S(2)}) collective-permute-start(bf16[2,32,2560]{2,1,0:T(8,128)(2,1)} %collective-permute-done.1.refs_2_.refs_6_), channel_id=1, source_target_pairs={{2,0},{4,6},{3,1},{5,7},{10,8},{12,14},{11,9},{13,15},{18,16},{20,... | collective-permute-start | bytes 983048 | tf_op jit(solution)/shard_map/ppermute | solution.py:324
  67.6 39.7 %copy-start.12 = (bf16[32,2560]{1,0:T(8,128)(2,1)}, bf16[32,2560]{1,0:T(8,128)(2,1)S(1)}, u32[]{:S(2)}) copy-start(bf16[32,2560]{1,0:T(8,128)(2,1)S(1)} %get-tuple-element.34.refs_0_.refs_4_) | copy-start | bytes 491524
  67.6 13.2 %collective-permute-start.7 = (bf16[32,2560]{1,0:T(8,128)(2,1)S(1)}, bf16[32,2560]{1,0:T(8,128)(2,1)S(1)}, u32[]{:S(2)}, u32[]{:S(2)}) collective-permute-start(bf16[32,2560]{1,0:T(8,128)(2,1)S(1)} %get-tuple-element.35.refs_5_), channel_id=1, source_target_pairs={{0,6},{2,0},{4,2},{6,4},{1,7},{3,1},{5,3},{7,5},{8,14},{10,8},{12,... | collective-permute-start | bytes 491528 | tf_op jit(solution)/shard_map/ppermute | solution.py:264
  68.6 26.3 %collective-permute-start.8 = (bf16[32,2560]{1,0:T(8,128)(2,1)S(1)}, bf16[32,2560]{1,0:T(8,128)(2,1)S(1)}, u32[]{:S(2)}, u32[]{:S(2)}) collective-permute-start(bf16[32,2560]{1,0:T(8,128)(2,1)S(1)} %get-tuple-element.36.refs_6_), channel_id=1, source_target_pairs={{0,4},{2,6},{4,0},{6,2},{1,5},{3,7},{5,1},{7,3},{8,12},{10,14},{12... | collective-permute-start | bytes 491528 | tf_op jit(solution)/shard_map/ppermute | solution.py:264
  70.8 37.8 %collective-permute-start.18 = (bf16[2,32,2560]{2,1,0:T(8,128)(2,1)}, bf16[2,32,2560]{2,1,0:T(8,128)(2,1)}, u32[]{:S(2)}, u32[]{:S(2)}) collective-permute-start(bf16[2,32,2560]{2,1,0:T(8,128)(2,1)} %get-tuple-element.73.refs_0_.x_ref), channel_id=1, source_target_pairs={{0,4},{2,6},{4,0},{6,2},{1,5},{3,7},{5,1},{7,3},{8,12},{10,14},{12... | collective-permute-start | bytes 983048 | tf_op jit(solution)/shard_map/ppermute | solution.py:264
  71.5 24.4 %collective-permute-start.9 = (bf16[32,2560]{1,0:T(8,128)(2,1)S(1)}, bf16[32,2560]{1,0:T(8,128)(2,1)S(1)}, u32[]{:S(2)}, u32[]{:S(2)}) collective-permute-start(bf16[32,2560]{1,0:T(8,128)(2,1)S(1)} %get-tuple-element.37.refs_7_), channel_id=1, source_target_pairs={{0,2},{2,4},{4,6},{6,0},{1,3},{3,5},{5,7},{7,1},{8,10},{10,12},{12... | collective-permute-start | bytes 491528 | tf_op jit(solution)/shard_map/ppermute | solution.py:264
  77.9 44.2 %copy-start.14 = (bf16[32,2560]{1,0:T(8,128)(2,1)}, bf16[32,2560]{1,0:T(8,128)(2,1)S(1)}, u32[]{:S(2)}) copy-start(bf16[32,2560]{1,0:T(8,128)(2,1)S(1)} %get-tuple-element.38.refs_0_.refs_8_) | copy-start | bytes 491524
  77.9 44.2 %copy-start.25 = (bf16[32,2560]{1,0:T(8,128)(2,1)}, bf16[32,2560]{1,0:T(8,128)(2,1)S(1)}, u32[]{:S(2)}) copy-start(bf16[32,2560]{1,0:T(8,128)(2,1)S(1)} %get-tuple-element.39.refs_9_) | copy-start | bytes 491524
  77.9 44.2 %copy-start.27 = (bf16[32,2560]{1,0:T(8,128)(2,1)}, bf16[32,2560]{1,0:T(8,128)(2,1)S(1)}, u32[]{:S(2)}) copy-start(bf16[32,2560]{1,0:T(8,128)(2,1)S(1)} %get-tuple-element.40.refs_10_) | copy-start | bytes 491524
  77.9 44.2 %copy-start.29 = (bf16[32,2560]{1,0:T(8,128)(2,1)}, bf16[32,2560]{1,0:T(8,128)(2,1)S(1)}, u32[]{:S(2)}) copy-start(bf16[32,2560]{1,0:T(8,128)(2,1)S(1)} %get-tuple-element.41.refs_11_) | copy-start | bytes 491524
  77.9 32.0 %collective-permute-start.10 = (bf16[32,2560]{1,0:T(8,128)(2,1)S(1)}, bf16[32,2560]{1,0:T(8,128)(2,1)S(1)}, u32[]{:S(2)}, u32[]{:S(2)}) collective-permute-start(bf16[32,2560]{1,0:T(8,128)(2,1)S(1)} %get-tuple-element.39.refs_9_), channel_id=1, source_target_pairs={{0,6},{2,0},{4,2},{6,4},{1,7},{3,1},{5,3},{7,5},{8,14},{10,8},{12,... | collective-permute-start | bytes 491528 | tf_op jit(solution)/shard_map/ppermute | solution.py:264
  80.7 33.0 %collective-permute-start.11 = (bf16[32,2560]{1,0:T(8,128)(2,1)S(1)}, bf16[32,2560]{1,0:T(8,128)(2,1)S(1)}, u32[]{:S(2)}, u32[]{:S(2)}) collective-permute-start(bf16[32,2560]{1,0:T(8,128)(2,1)S(1)} %get-tuple-element.40.refs_10_), channel_id=1, source_target_pairs={{0,4},{2,6},{4,0},{6,2},{1,5},{3,7},{5,1},{7,3},{8,12},{10,14},{12... | collective-permute-start | bytes 491528 | tf_op jit(solution)/shard_map/ppermute | solution.py:264
  94.9 20.2 %collective-permute-start.12 = (bf16[32,2560]{1,0:T(8,128)(2,1)S(1)}, bf16[32,2560]{1,0:T(8,128)(2,1)S(1)}, u32[]{:S(2)}, u32[]{:S(2)}) collective-permute-start(bf16[32,2560]{1,0:T(8,128)(2,1)S(1)} %get-tuple-element.41.refs_11_), channel_id=1, source_target_pairs={{0,2},{2,4},{4,6},{6,0},{1,3},{3,5},{5,7},{7,1},{8,10},{10,12},{12... | collective-permute-start | bytes 491528 | tf_op jit(solution)/shard_map/ppermute | solution.py:264
  95.9 32.0 %collective-permute-start.17 = (bf16[2,32,2560]{2,1,0:T(8,128)(2,1)}, bf16[2,32,2560]{2,1,0:T(8,128)(2,1)}, u32[]{:S(2)}, u32[]{:S(2)}) collective-permute-start(bf16[2,32,2560]{2,1,0:T(8,128)(2,1)} %get-tuple-element.73.refs_0_.x_ref), channel_id=1, source_target_pairs={{0,2},{2,4},{4,6},{1,3},{3,5},{5,7},{8,10},{10,12},{12,14},{9,11},... | collective-permute-start | bytes 983048 | tf_op jit(solution)/shard_map/ppermute | solution.py:322
  108.6 22.3 %collective-permute-start.19 = (bf16[2,32,2560]{2,1,0:T(8,128)(2,1)}, bf16[2,32,2560]{2,1,0:T(8,128)(2,1)}, u32[]{:S(2)}, u32[]{:S(2)}) collective-permute-start(bf16[2,32,2560]{2,1,0:T(8,128)(2,1)} %get-tuple-element.73.refs_0_.x_ref), channel_id=1, source_target_pairs={{2,0},{4,2},{6,4},{3,1},{5,3},{7,5},{10,8},{12,10},{14,12},{11,9},... | collective-permute-start | bytes 983048 | tf_op jit(solution)/shard_map/ppermute | solution.py:323
  109.9 21.0 %collective-permute-start.20 = (bf16[2,32,2560]{2,1,0:T(8,128)(2,1)}, bf16[2,32,2560]{2,1,0:T(8,128)(2,1)}, u32[]{:S(2)}, u32[]{:S(2)}) collective-permute-start(bf16[2,32,2560]{2,1,0:T(8,128)(2,1)} %collective-permute-done.18.refs_2_), channel_id=1, source_target_pairs={{2,0},{4,6},{3,1},{5,7},{10,8},{12,14},{11,9},{13,15},{18,16},{20,... | collective-permute-start | bytes 983048 | tf_op jit(solution)/shard_map/ppermute | solution.py:324
  113.8 5.6 %collective-permute-start.13 = (bf16[32,2560]{1,0:T(8,128)(2,1)S(1)}, bf16[32,2560]{1,0:T(8,128)(2,1)S(1)}, u32[]{:S(2)}, u32[]{:S(2)}) collective-permute-start(bf16[32,2560]{1,0:T(8,128)(2,1)S(1)} %shard_map.95), channel_id=1, source_target_pairs={{8,0},{16,8},{24,16},{9,1},{17,9},{25,17},{10,2},{18,10},{26,18},{... | collective-permute-start | bytes 491528 | tf_op jit(solution)/shard_map/ppermute | solution.py:446
  116.4 5.7 %collective-permute-start.24 = (bf16[32,2560]{1,0:T(8,128)(2,1)S(1)}, bf16[32,2560]{1,0:T(8,128)(2,1)S(1)}, u32[]{:S(2)}, u32[]{:S(2)}) collective-permute-start(bf16[32,2560]{1,0:T(8,128)(2,1)S(1)} %shard_map.97.chosen_ref), channel_id=1, source_target_pairs={{0,8},{8,16},{16,24},{1,9},{9,17},{17,25},{2,10},{10,18},{18,26},{... | collective-permute-start | bytes 491528 | tf_op jit(solution)/shard_map/ppermute | solution.py:442
  121.3 10.2 %collective-permute-start.14 = (bf16[32,2560]{1,0:T(8,128)(2,1)}, bf16[32,2560]{1,0:T(8,128)(2,1)}, u32[]{:S(2)}, u32[]{:S(2)}) collective-permute-start(bf16[32,2560]{1,0:T(8,128)(2,1)} %shard_map.98.refs_0_.grad_ref.refs_12_), channel_id=1, source_target_pairs={{0,2},{2,4},{4,6},{6,0},{1,3},{3,5},{5,7},{7,1},{8,10},{10,12},{12... | collective-permute-start | bytes 491528 | tf_op jit(solution)/shard_map/ppermute | solution.py:264
  122.8 17.7 %collective-permute-start.15 = (bf16[32,2560]{1,0:T(8,128)(2,1)}, bf16[32,2560]{1,0:T(8,128)(2,1)}, u32[]{:S(2)}, u32[]{:S(2)}) collective-permute-start(bf16[32,2560]{1,0:T(8,128)(2,1)} %shard_map.98.refs_0_.grad_ref.refs_12_), channel_id=1, source_target_pairs={{0,4},{2,6},{4,0},{6,2},{1,5},{3,7},{5,1},{7,3},{8,12},{10,14},{12... | collective-permute-start | bytes 491528 | tf_op jit(solution)/shard_map/ppermute | solution.py:264
  127.9 18.6 %collective-permute-start.16 = (bf16[32,2560]{1,0:T(8,128)(2,1)}, bf16[32,2560]{1,0:T(8,128)(2,1)S(1)}, u32[]{:S(2)}, u32[]{:S(2)}) collective-permute-start(bf16[32,2560]{1,0:T(8,128)(2,1)} %shard_map.98.refs_0_.grad_ref.refs_12_), channel_id=1, source_target_pairs={{0,6},{2,0},{4,2},{6,4},{1,7},{3,1},{5,3},{7,5},{8,14},{10,8},{12,... | collective-permute-start | bytes 491528 | tf_op jit(solution)/shard_map/ppermute | solution.py:264
  130.9 20.9 %collective-permute-start.25 = (bf16[32,2560]{1,0:T(8,128)(2,1)S(1)}, bf16[32,2560]{1,0:T(8,128)(2,1)S(1)}, u32[]{:S(2)}, u32[]{:S(2)}) collective-permute-start(bf16[32,2560]{1,0:T(8,128)(2,1)S(1)} %shard_map.102.refs_0_.grad_ref.refs_12_), channel_id=1, source_target_pairs={{0,2},{2,4},{4,6},{6,0},{1,3},{3,5},{5,7},{7,1},{8,10},{10,12},{12... | collective-permute-start | bytes 491528 | tf_op jit(solution)/shard_map/ppermute | solution.py:264
  130.9 22.3 %collective-permute-start.26 = (bf16[32,2560]{1,0:T(8,128)(2,1)S(1)}, bf16[32,2560]{1,0:T(8,128)(2,1)S(1)}, u32[]{:S(2)}, u32[]{:S(2)}) collective-permute-start(bf16[32,2560]{1,0:T(8,128)(2,1)S(1)} %shard_map.102.refs_0_.grad_ref.refs_12_), channel_id=1, source_target_pairs={{0,4},{2,6},{4,0},{6,2},{1,5},{3,7},{5,1},{7,3},{8,12},{10,14},{12... | collective-permute-start | bytes 491528 | tf_op jit(solution)/shard_map/ppermute | solution.py:264
  131.6 22.4 %collective-permute-start.27 = (bf16[32,2560]{1,0:T(8,128)(2,1)S(1)}, bf16[32,2560]{1,0:T(8,128)(2,1)S(1)}, u32[]{:S(2)}, u32[]{:S(2)}) collective-permute-start(bf16[32,2560]{1,0:T(8,128)(2,1)S(1)} %shard_map.102.refs_0_.grad_ref.refs_12_), channel_id=1, source_target_pairs={{0,6},{2,0},{4,2},{6,4},{1,7},{3,1},{5,3},{7,5},{8,14},{10,8},{12,... | collective-permute-start | bytes 491528 | tf_op jit(solution)/shard_map/ppermute | solution.py:264
  140.5 21.1 %collective-permute-start.37 = (bf16[2,32,2560]{2,1,0:T(8,128)(2,1)}, bf16[2,32,2560]{2,1,0:T(8,128)(2,1)S(1)}, u32[]{:S(2)}, u32[]{:S(2)}) collective-permute-start(bf16[2,32,2560]{2,1,0:T(8,128)(2,1)} %bitcast.8.refs_0_.refs_4_), channel_id=1, source_target_pairs={{0,1},{1,0},{2,3},{3,2},{4,5},{5,4},{6,7},{7,6},{8,9},{9,8},{10,11... | collective-permute-start | bytes 983048 | tf_op jit(solution)/shard_map/ppermute | solution.py:264
  146.6 30.6 %collective-permute-start.39 = (bf16[2,32,2560]{2,1,0:T(8,128)(2,1)}, bf16[2,32,2560]{2,1,0:T(8,128)(2,1)S(1)}, u32[]{:S(2)}, u32[]{:S(2)}) collective-permute-start(bf16[2,32,2560]{2,1,0:T(8,128)(2,1)} %collective-permute-done.1.refs_2_.refs_6_), channel_id=1, source_target_pairs={{0,1},{1,0},{2,3},{3,2},{4,5},{5,4},{6,7},{7,6},{8,9},{9,8},{10,11... | collective-permute-start | bytes 983048 | tf_op jit(solution)/shard_map/ppermute | solution.py:264
  151.8 35.7 %collective-permute-start.38 = (bf16[2,32,2560]{2,1,0:T(8,128)(2,1)S(1)}, bf16[2,32,2560]{2,1,0:T(8,128)(2,1)S(1)}, u32[]{:S(2)}, u32[]{:S(2)}) collective-permute-start(bf16[2,32,2560]{2,1,0:T(8,128)(2,1)S(1)} %shard_map.106.refs_5_), channel_id=1, source_target_pairs={{0,1},{1,0},{2,3},{3,2},{4,5},{5,4},{6,7},{7,6},{8,9},{9,8},{10,11... | collective-permute-start | bytes 983048 | tf_op jit(solution)/shard_map/ppermute | solution.py:264
  153.2 35.8 %collective-permute-start.40 = (bf16[2,32,2560]{2,1,0:T(8,128)(2,1)S(1)}, bf16[2,32,2560]{2,1,0:T(8,128)(2,1)S(1)}, u32[]{:S(2)}, u32[]{:S(2)}) collective-permute-start(bf16[2,32,2560]{2,1,0:T(8,128)(2,1)S(1)} %shard_map.107.refs_7_), channel_id=1, source_target_pairs={{0,1},{1,0},{2,3},{3,2},{4,5},{5,4},{6,7},{7,6},{8,9},{9,8},{10,11... | collective-permute-start | bytes 983048 | tf_op jit(solution)/shard_map/ppermute | solution.py:264
  157.7 16.6 %copy-start.10 = (bf16[2,128,2560]{2,1,0:T(8,128)(2,1)S(1)}, bf16[2,128,2560]{2,1,0:T(8,128)(2,1)}, u32[]{:S(2)}) copy-start(bf16[2,128,2560]{2,1,0:T(8,128)(2,1)} %copy-done.9) | copy-start | bytes 3932164
  160.2 12.6 %collective-permute-start.49 = (f32[2,1,2560]{2,1,0:T(1,128)S(1)}, f32[2,1,2560]{2,1,0:T(1,128)S(1)}, u32[]{:S(2)}, u32[]{:S(2)}) collective-permute-start(f32[2,1,2560]{2,1,0:T(1,128)S(1)} %add.122), channel_id=1, source_target_pairs={{0,1},{1,0},{2,3},{3,2},{4,5},{5,4},{6,7},{7,6},{8,9},{9,8},{10,11... | collective-permute-start | bytes 61448 | tf_op jit(solution)/shard_map/ppermute | solution.py:272
  161.6 14.0 %collective-permute-start.35 = (bf16[2,128,256]{2,1,0:T(8,128)(2,1)S(1)}, bf16[2,128,256]{2,1,0:T(8,128)(2,1)S(1)}, u32[]{:S(2)}, u32[]{:S(2)}) collective-permute-start(bf16[2,128,256]{2,1,0:T(8,128)(2,1)S(1)} %get-tuple-element.78), channel_id=1, source_target_pairs={{0,1},{1,0},{2,3},{3,2},{4,5},{5,4},{6,7},{7,6},{8,9},{9,8},{10,11... | collective-permute-start | bytes 393224 | tf_op jit(solution)/shard_map/ppermute | solution.py:264
  172.8 14.3 %collective-permute-start.36 = (bf16[2,128,256]{2,1,0:T(8,128)(2,1)S(1)}, bf16[2,128,256]{2,1,0:T(8,128)(2,1)S(1)}, u32[]{:S(2)}, u32[]{:S(2)}) collective-permute-start(bf16[2,128,256]{2,1,0:T(8,128)(2,1)S(1)} %get-tuple-element.76), channel_id=1, source_target_pairs={{0,1},{1,0},{2,3},{3,2},{4,5},{5,4},{6,7},{7,6},{8,9},{9,8},{10,11... | collective-permute-start | bytes 393224 | tf_op jit(solution)/shard_map/ppermute | solution.py:264
  174.4 20.3 %copy-start.32 = (bf16[128,640]{1,0:T(8,128)(2,1)S(1)}, bf16[128,640]{1,0:T(8,128)(2,1)}, u32[]{:S(2)}) copy-start(bf16[128,640]{1,0:T(8,128)(2,1)} %copy-done.31) | copy-start | bytes 491524
  174.4 20.3 %copy-start.34 = (bf16[128,640]{1,0:T(8,128)(2,1)S(1)}, bf16[128,640]{1,0:T(8,128)(2,1)}, u32[]{:S(2)}) copy-start(bf16[128,640]{1,0:T(8,128)(2,1)} %copy-done.33) | copy-start | bytes 491524
  174.4 28.9 %copy-start.8 = (bf16[32,2560]{1,0:T(8,128)(2,1)S(1)}, bf16[32,2560]{1,0:T(8,128)(2,1)}, u32[]{:S(2)}) copy-start(bf16[32,2560]{1,0:T(8,128)(2,1)} %copy-done.7) | copy-start | bytes 491524
  174.4 28.9 %copy-start.17 = (bf16[32,2560]{1,0:T(8,128)(2,1)S(1)}, bf16[32,2560]{1,0:T(8,128)(2,1)}, u32[]{:S(2)}) copy-start(bf16[32,2560]{1,0:T(8,128)(2,1)} %copy-done.16) | copy-start | bytes 491524
  175.6 13.6 %collective-permute-start.45 = (bf16[32,2560]{1,0:T(8,128)(2,1)S(1)}, bf16[32,2560]{1,0:T(8,128)(2,1)S(1)}, u32[]{:S(2)}, u32[]{:S(2)}) collective-permute-start(bf16[32,2560]{1,0:T(8,128)(2,1)S(1)} %shard_map.102.refs_0_.grad_ref.refs_12_), channel_id=1, source_target_pairs={{0,1},{1,0},{2,3},{3,2},{4,5},{5,4},{6,7},{7,6},{8,9},{9,8},{10,11... | collective-permute-start | bytes 491528 | tf_op jit(solution)/shard_map/ppermute | solution.py:264
  177.2 25.5 %collective-permute-start.21 = (bf16[32,2560]{1,0:T(8,128)(2,1)S(1)}, bf16[32,2560]{1,0:T(8,128)(2,1)S(1)}, u32[]{:S(2)}, u32[]{:S(2)}) collective-permute-start(bf16[32,2560]{1,0:T(8,128)(2,1)S(1)} %get-tuple-element.45.refs_6_), channel_id=1, source_target_pairs={{0,6},{2,0},{4,2},{6,4},{1,7},{3,1},{5,3},{7,5},{8,14},{10,8},{12,... | collective-permute-start | bytes 491528 | tf_op jit(solution)/shard_map/ppermute | solution.py:264
  187.0 12.1 %collective-permute-start.46 = (bf16[32,2560]{1,0:T(8,128)(2,1)S(1)}, bf16[32,2560]{1,0:T(8,128)(2,1)S(1)}, u32[]{:S(2)}, u32[]{:S(2)}) collective-permute-start(bf16[32,2560]{1,0:T(8,128)(2,1)S(1)} %collective-permute-done.25.refs_1_.refs_13_), channel_id=1, source_target_pairs={{0,1},{1,0},{2,3},{3,2},{4,5},{5,4},{6,7},{7,6},{8,9},{9,8},{10,11... | collective-permute-start | bytes 491528 | tf_op jit(solution)/shard_map/ppermute | solution.py:264
  187.5 15.1 %collective-permute-start.47 = (bf16[32,2560]{1,0:T(8,128)(2,1)S(1)}, bf16[32,2560]{1,0:T(8,128)(2,1)S(1)}, u32[]{:S(2)}, u32[]{:S(2)}) collective-permute-start(bf16[32,2560]{1,0:T(8,128)(2,1)S(1)} %collective-permute-done.26.refs_2_.refs_14_), channel_id=1, source_target_pairs={{0,1},{1,0},{2,3},{3,2},{4,5},{5,4},{6,7},{7,6},{8,9},{9,8},{10,11... | collective-permute-start | bytes 491528 | tf_op jit(solution)/shard_map/ppermute | solution.py:264
  189.0 3.8 %collective-permute-start.50 = (f32[2,1,2560]{2,1,0:T(1,128)S(1)}, f32[2,1,2560]{2,1,0:T(1,128)S(1)}, u32[]{:S(2)}, u32[]{:S(2)}) collective-permute-start(f32[2,1,2560]{2,1,0:T(1,128)S(1)} %add.123), channel_id=1, source_target_pairs={{0,2},{2,0},{4,6},{6,4},{1,3},{3,1},{5,7},{7,5},{8,10},{10,8},{12,... | collective-permute-start | bytes 61448 | tf_op jit(solution)/shard_map/ppermute | solution.py:272
  189.1 5.5 %collective-permute-start.51 = (f32[2,1,2560]{2,1,0:T(1,128)S(1)}, f32[2,1,2560]{2,1,0:T(1,128)S(1)}, u32[]{:S(2)}, u32[]{:S(2)}) collective-permute-start(f32[2,1,2560]{2,1,0:T(1,128)S(1)} %add.123), channel_id=1, source_target_pairs={{0,4},{2,6},{4,0},{6,2},{1,5},{3,7},{5,1},{7,3},{8,12},{10,14},{12... | collective-permute-start | bytes 61448 | tf_op jit(solution)/shard_map/ppermute | solution.py:272
  192.8 6.0 %collective-permute-start.52 = (f32[2,1,2560]{2,1,0:T(1,128)S(1)}, f32[2,1,2560]{2,1,0:T(1,128)S(1)}, u32[]{:S(2)}, u32[]{:S(2)}) collective-permute-start(f32[2,1,2560]{2,1,0:T(1,128)S(1)} %add.123), channel_id=1, source_target_pairs={{0,6},{2,4},{4,2},{6,0},{1,7},{3,5},{5,3},{7,1},{8,14},{10,12},{12... | collective-permute-start | bytes 61448 | tf_op jit(solution)/shard_map/ppermute | solution.py:272
  194.7 15.8 %collective-permute-start.22 = (bf16[32,2560]{1,0:T(8,128)(2,1)S(1)}, bf16[32,2560]{1,0:T(8,128)(2,1)S(1)}, u32[]{:S(2)}, u32[]{:S(2)}) collective-permute-start(bf16[32,2560]{1,0:T(8,128)(2,1)S(1)} %get-tuple-element.46.refs_7_), channel_id=1, source_target_pairs={{0,4},{2,6},{4,0},{6,2},{1,5},{3,7},{5,1},{7,3},{8,12},{10,14},{12... | collective-permute-start | bytes 491528 | tf_op jit(solution)/shard_map/ppermute | solution.py:264
  198.8 12.4 %collective-permute-start.23 = (bf16[32,2560]{1,0:T(8,128)(2,1)S(1)}, bf16[32,2560]{1,0:T(8,128)(2,1)S(1)}, u32[]{:S(2)}, u32[]{:S(2)}) collective-permute-start(bf16[32,2560]{1,0:T(8,128)(2,1)S(1)} %get-tuple-element.47.refs_8_), channel_id=1, source_target_pairs={{0,2},{2,4},{4,6},{6,0},{1,3},{3,5},{5,7},{7,1},{8,10},{10,12},{12... | collective-permute-start | bytes 491528 | tf_op jit(solution)/shard_map/ppermute | solution.py:264
  199.1 13.3 %collective-permute-start.28 = (bf16[32,2560]{1,0:T(8,128)(2,1)S(1)}, bf16[32,2560]{1,0:T(8,128)(2,1)S(1)}, u32[]{:S(2)}, u32[]{:S(2)}) collective-permute-start(bf16[32,2560]{1,0:T(8,128)(2,1)S(1)} %get-tuple-element.49.refs_10_), channel_id=1, source_target_pairs={{0,6},{2,0},{4,2},{6,4},{1,7},{3,1},{5,3},{7,5},{8,14},{10,8},{12,... | collective-permute-start | bytes 491528 | tf_op jit(solution)/shard_map/ppermute | solution.py:264
  202.7 17.6 %collective-permute-start.29 = (bf16[32,2560]{1,0:T(8,128)(2,1)S(1)}, bf16[32,2560]{1,0:T(8,128)(2,1)S(1)}, u32[]{:S(2)}, u32[]{:S(2)}) collective-permute-start(bf16[32,2560]{1,0:T(8,128)(2,1)S(1)} %get-tuple-element.50.refs_11_), channel_id=1, source_target_pairs={{0,4},{2,6},{4,0},{6,2},{1,5},{3,7},{5,1},{7,3},{8,12},{10,14},{12... | collective-permute-start | bytes 491528 | tf_op jit(solution)/shard_map/ppermute | solution.py:264
  202.7 18.1 %collective-permute-start.30 = (bf16[32,2560]{1,0:T(8,128)(2,1)S(1)}, bf16[32,2560]{1,0:T(8,128)(2,1)S(1)}, u32[]{:S(2)}, u32[]{:S(2)}) collective-permute-start(bf16[32,2560]{1,0:T(8,128)(2,1)S(1)} %get-tuple-element.51.refs_12_), channel_id=1, source_target_pairs={{0,2},{2,4},{4,6},{6,0},{1,3},{3,5},{5,7},{7,1},{8,10},{10,12},{12... | collective-permute-start | bytes 491528 | tf_op jit(solution)/shard_map/ppermute | solution.py:264
  210.5 19.5 %collective-permute-start.41 = (bf16[32,2560]{1,0:T(8,128)(2,1)}, bf16[32,2560]{1,0:T(8,128)(2,1)S(1)}, u32[]{:S(2)}, u32[]{:S(2)}) collective-permute-start(bf16[32,2560]{1,0:T(8,128)(2,1)} %shard_map.98.refs_0_.grad_ref.refs_12_), channel_id=1, source_target_pairs={{0,1},{1,0},{2,3},{3,2},{4,5},{5,4},{6,7},{7,6},{8,9},{9,8},{10,11... | collective-permute-start | bytes 491528 | tf_op jit(solution)/shard_map/ppermute | solution.py:264
  211.3 14.2 %collective-permute-start.48 = (bf16[32,2560]{1,0:T(8,128)(2,1)S(1)}, bf16[32,2560]{1,0:T(8,128)(2,1)S(1)}, u32[]{:S(2)}, u32[]{:S(2)}) collective-permute-start(bf16[32,2560]{1,0:T(8,128)(2,1)S(1)} %collective-permute-done.27.refs_3_.refs_15_), channel_id=1, source_target_pairs={{0,1},{1,0},{2,3},{3,2},{4,5},{5,4},{6,7},{7,6},{8,9},{9,8},{10,11... | collective-permute-start | bytes 491528 | tf_op jit(solution)/shard_map/ppermute | solution.py:264
  212.5 19.0 %collective-permute-start.42 = (bf16[32,2560]{1,0:T(8,128)(2,1)}, bf16[32,2560]{1,0:T(8,128)(2,1)S(1)}, u32[]{:S(2)}, u32[]{:S(2)}) collective-permute-start(bf16[32,2560]{1,0:T(8,128)(2,1)} %collective-permute-done.14.refs_1_.refs_13_), channel_id=1, source_target_pairs={{0,1},{1,0},{2,3},{3,2},{4,5},{5,4},{6,7},{7,6},{8,9},{9,8},{10,11... | collective-permute-start | bytes 491528 | tf_op jit(solution)/shard_map/ppermute | solution.py:264
  220.2 11.7 %collective-permute-start.43 = (bf16[32,2560]{1,0:T(8,128)(2,1)}, bf16[32,2560]{1,0:T(8,128)(2,1)S(1)}, u32[]{:S(2)}, u32[]{:S(2)}) collective-permute-start(bf16[32,2560]{1,0:T(8,128)(2,1)} %collective-permute-done.15.refs_2_.refs_14_), channel_id=1, source_target_pairs={{0,1},{1,0},{2,3},{3,2},{4,5},{5,4},{6,7},{7,6},{8,9},{9,8},{10,11... | collective-permute-start | bytes 491528 | tf_op jit(solution)/shard_map/ppermute | solution.py:264
  220.8 12.7 %collective-permute-start.44 = (bf16[32,2560]{1,0:T(8,128)(2,1)S(1)}, bf16[32,2560]{1,0:T(8,128)(2,1)S(1)}, u32[]{:S(2)}, u32[]{:S(2)}) collective-permute-start(bf16[32,2560]{1,0:T(8,128)(2,1)S(1)} %collective-permute-done.16.refs_3_.refs_15_), channel_id=1, source_target_pairs={{0,1},{1,0},{2,3},{3,2},{4,5},{5,4},{6,7},{7,6},{8,9},{9,8},{10,11... | collective-permute-start | bytes 491528 | tf_op jit(solution)/shard_map/ppermute | solution.py:264
  225.5 26.6 %collective-permute-start.31 = (bf16[2,128,1280]{2,1,0:T(8,128)(2,1)S(1)}, bf16[2,128,1280]{2,1,0:T(8,128)(2,1)S(1)}, u32[]{:S(2)}, u32[]{:S(2)}) collective-permute-start(bf16[2,128,1280]{2,1,0:T(8,128)(2,1)S(1)} %get-tuple-element.70), channel_id=1, source_target_pairs={{0,1},{1,0},{2,3},{3,2},{4,5},{5,4},{6,7},{7,6},{8,9},{9,8},{10,11... | collective-permute-start | bytes 1966088 | tf_op jit(solution)/shard_map/ppermute | solution.py:264
  229.9 22.2 %collective-permute-start.33 = (bf16[2,128,640]{2,1,0:T(8,128)(2,1)S(1)}, bf16[2,128,640]{2,1,0:T(8,128)(2,1)S(1)}, u32[]{:S(2)}, u32[]{:S(2)}) collective-permute-start(bf16[2,128,640]{2,1,0:T(8,128)(2,1)S(1)} %pad_maximum_fusion.refs_4_), channel_id=1, source_target_pairs={{0,1},{1,0},{2,3},{3,2},{4,5},{5,4},{6,7},{7,6},{8,9},{9,8},{10,11... | collective-permute-start | bytes 983048 | tf_op jit(solution)/shard_map/ppermute | solution.py:264
  231.4 34.7 %collective-permute-start.32 = (bf16[2,128,1280]{2,1,0:T(8,128)(2,1)S(1)}, bf16[2,128,1280]{2,1,0:T(8,128)(2,1)S(1)}, u32[]{:S(2)}, u32[]{:S(2)}) collective-permute-start(bf16[2,128,1280]{2,1,0:T(8,128)(2,1)S(1)} %get-tuple-element.68), channel_id=1, source_target_pairs={{0,1},{1,0},{2,3},{3,2},{4,5},{5,4},{6,7},{7,6},{8,9},{9,8},{10,11... | collective-permute-start | bytes 1966088 | tf_op jit(solution)/shard_map/ppermute | solution.py:264
  232.0 39.6 %collective-permute-start.34 = (bf16[2,128,640]{2,1,0:T(8,128)(2,1)S(1)}, bf16[2,128,640]{2,1,0:T(8,128)(2,1)S(1)}, u32[]{:S(2)}, u32[]{:S(2)}) collective-permute-start(bf16[2,128,640]{2,1,0:T(8,128)(2,1)S(1)} %pad_maximum_fusion.1.refs_6_), channel_id=1, source_target_pairs={{0,1},{1,0},{2,3},{3,2},{4,5},{5,4},{6,7},{7,6},{8,9},{9,8},{10,11... | collective-permute-start | bytes 983048 | tf_op jit(solution)/shard_map/ppermute | solution.py:264
  (28 other events, 214.9 us)

commit v2 on v1

--- a/solution.py
+++ b/solution.py
@@ -18,7 +18,7 @@
 
 ROWS = (((0,), (0,)), ((), ()))
 COLS = (((1,), (1,)), ((), ()))
-VMEM_BYTES = 8 * 1024 * 1024
+VMEM_BYTES = 16 * 1024 * 1024
 
 
 def swap_halves(values, lane):
@@ -157,6 +157,17 @@
         partial_refs[k][...] = partial[k * own : (k + 1) * own]
 
 
+def join_kernel(nt, flag_ref, *refs):
+    parts, out_ref = refs[:-1], refs[-1]
+    own = parts[0].shape[-2]
+    for m in range(out_ref.shape[0]) if len(out_ref.shape) == 3 else (None,):
+        for k, block in enumerate(pick(parts, nt, flag_ref, m)[1:]):
+            if m is None:
+                out_ref[k * own : (k + 1) * own] = block
+            else:
+                out_ref[m, k * own : (k + 1) * own] = block
+
+
 def choose_kernel(flag, where_ref, chosen_ref, otherwise_ref, out_ref):
     out_ref[...] = jnp.where(where_ref[flag] == 1, chosen_ref[...], otherwise_ref[...])
 
@@ -218,7 +229,7 @@
     depth = sum(a.shape[-2] for a in lefts)
     high, wide = lefts[0].shape[-1], rights[0].shape[-1]
     extent = high if split_left else wide
-    tile = 640 if extent % 640 == 0 else extent
+    tile = 1280 if extent % 1280 == 0 else extent
 
     def member(m):
         return m if only is None else only
@@ -268,12 +279,11 @@
     count = lax.axis_size(axis)
     if count & (count - 1):
         return lax.psum(value, axis)
-    terms = [value] + [
-        lax.ppermute(value, axis, [(i, i ^ step) for i in range(count)]) for step in range(1, count)
-    ]
-    while len(terms) > 1:
-        terms = [terms[i] + terms[i + 1] for i in range(0, len(terms), 2)]
-    return terms[0]
+    step = 1
+    while step < count:
+        value = value + lax.ppermute(value, axis, [(i, i ^ step) for i in range(count)])
+        step *= 2
+    return value
 
 
 def local(layer_in, carry_in, top_grad, w_qkv, w_out, gain):
@@ -289,7 +299,6 @@
     replica = lax.axis_index("dp")
     at_first = section == 0
     at_last = section == ns - 1
-    at_far_low, at_far_high = place == 0, place == nt - 1
     x_rows = layer_in[:, :, 0, 0]
     carried = carry_in[:, 0, 0]
     fresh_rows = top_grad[:, 0]
@@ -340,7 +349,7 @@
     def shaped(*shape, dtype=bf16):
         return jax.ShapeDtypeStruct((2,) + shape, dtype)
 
-    where = jnp.stack([place, at_last, at_first, at_far_low, at_far_high]).astype(jnp.int32)
+    where = jnp.stack([place, at_last, at_first]).astype(jnp.int32)
 
     def choose(flag, chosen, otherwise):
         return call(
@@ -352,12 +361,14 @@
 
 
     def settled(parts):
-        if len(parts) == nt:
-            return parts
-        parts, ends = list(parts[:nt]), parts[nt]
-        parts[1] = choose(3, ends, parts[1])
-        parts[nt - 1] = choose(4, ends, parts[nt - 1])
-        return parts
+        shape = parts[0].shape[:-2] + (length - own_rows, width)
+        others = call(
+            functools.partial(join_kernel, nt),
+            [where, *parts],
+            [jax.ShapeDtypeStruct(shape, bf16)],
+            length * width,
+        )[0]
+        return [parts[0], others]
 
     def forward(parts):
         return call(
@@ -383,9 +394,9 @@
         return outs[0], outs[1:]
 
     members = (1, 0)
-    x_parts = gather_rotated(x_rows[0])
+    x_parts = gather_line(x_rows[0], x_rows[0])
     own_grads = [carried[0], carried[1]]
-    first_parts = gather_line(carried, carried)
+    first_parts = gather_rotated(carried)
     grad_parts = [first_parts, first_parts]
     normed, attended, rotated, softmax = forward(x_parts)
     normed_peers = peers(normed, True)
@@ -393,7 +404,7 @@
     placed = settled(first_parts)
     shared = send_parts(placed)
     placed, sent_parts = [placed, placed], [shared, shared]
-    qkv_lefts, qkv_rights, out_lefts, out_rights = [], [], [], [[], []]
+    qkv_lefts, qkv_rights, out_lefts, out_rights = [], [[], []], [], [[], []]
     gain_total = 0.0
     per_tick = []
     for t in range(ticks):
@@ -403,8 +414,9 @@
             projected[m], partials[m] = backward(grad_parts[m], m, rotated, softmax)
             for k in range(1, nt):
                 received[m].append(shift(partials[m][k], "tensor", -k))
-        projected = jnp.stack(projected)
-        projected_peers = peers(projected, False)
+        projected_peers = [None, None]
+        for m in members:
+            projected_peers[m] = peers(projected[m], False)
         gain_total = gain_total + call(
             functools.partial(gain_kernel, nt, len(x_parts)),
             [where, *x_parts, *partials[0], *partials[1]],
@@ -421,7 +433,8 @@
             )[0]
         per_tick.append(jnp.stack(outcome))
         qkv_lefts.extend([slice_for(normed, 0), *normed_peers])
-        qkv_rights.extend([projected, *projected_peers])
+        for m in members:
+            qkv_rights[m].extend([projected[m], *projected_peers[m]])
         out_lefts.extend([slice_for(attended, 0), *attended_peers])
         for m in members:
             out_rights[m].extend(placed[m])
@@ -435,7 +448,8 @@
             normed, attended, rotated, softmax = forward(x_parts)
             normed_peers = peers(normed, True)
             attended_peers = peers(attended, True)
-            own_grads, grad_parts, sent_parts = [None, None], [None, None], [None, None]
+            own_grads, grad_parts = [None, None], [None, None]
+            placed, sent_parts = [None, None], [None, None]
             for m in members:
                 if m == 1:
                     moves = [(s, s + 1) for s in range(ns - 1)]
@@ -446,13 +460,14 @@
                     came = lax.ppermute(outcome[0], "section", moves)
                     own_grads[0] = choose(1, outcome[1], came)
                 grad_parts[m] = gather_rotated(own_grads[m])
-                sent_parts[m] = send_parts(grad_parts[m])
-            placed = grad_parts
-
-    grad_out = None
+                placed[m] = settled(grad_parts[m])
+                sent_parts[m] = send_parts(placed[m])
+
+    grad_out = grad_qkv = None
     for m in members:
         grad_out = weight_grad(out_lefts, out_rights[m], False, m, grad_out)
-    grad_qkv = weight_grad(qkv_lefts, qkv_rights, True)
+    for m in members:
+        grad_qkv = weight_grad(qkv_lefts, qkv_rights[m], True, m, grad_qkv)
     for axis in ("dp", "tensor"):
         gain_total = sum_over(gain_total, axis)
     return (

time: 277 us -> 278 us (level)
  waiting for transfers between devices: 103 us -> 151 us
  starting transfers between devices: 97.3 us -> 72.1 us
  local copies, waits for them, and re-layouts: 20 us -> 8.22 us
  Pallas kernels: 52.4 us -> 40.8 us
    ppermute x41 -> x37, waiting for transfers between devices: 86.8 us -> 118 us  [shift(): lax.ppermute(value, axis, [(i, (i + steps) % count) for i in range(count)])]
    ppermute x2, waiting for transfers between devices: 1.7 us -> 19.9 us  [gather_line(): ends = lax.ppermute(middle, 'tensor', [(1, 0), (nt - 2, nt - 1)])]
    ppermute x41 -> x37, starting transfers between devices: 67.3 us -> 51.4 us  [shift(): lax.ppermute(value, axis, [(i, (i + steps) % count) for i in range(count)])]
    ppermute x4 -> x3, waiting for transfers between devices: 14 us -> 5 us  [sum_over(): lax.ppermute(value, axis, [(i, i ^ step) for i in range(count)])]
    pallas_call x16 -> x17, Pallas kernels: 40.4 us -> 31.7 us  [call(): pl.pallas_call(kernel, out_shape=outs, in_specs=[pl.BlockSpec(memory_spac...]
    ppermute x2, starting transfers between devices: 14.9 us -> 6.27 us  [gather_line(): ahead = lax.ppermute(near, 'tensor', [(i, i + 1) for i in range(nt - 1)])]
    ppermute x2, waiting for transfers between devices: 0.01 us -> 8.2 us  [gather_line(): behind = lax.ppermute(near, 'tensor', [(i, i - 1) for i in range(1, nt)])]
    unnamed x78 -> x82, local copies, waits for them, and re-layouts: 7.75 us -> 2.88 us
  transfers between devices with their start and end apart: 53 -> 48, of which waited for: 13 -> 18; matrix products, arithmetic and copies ran while one was open for 5% -> 2% of each run, Pallas kernels for 16% -> 11%
where the time goes in v2:
time: 278 us; the launch traced here: 276 us
  waiting for transfers between devices  151 us (54%)
  starting transfers between devices  72.1 us (26%)
  Pallas kernels  40.8 us (15%)
  local copies, waits for them, and re-layouts  8.22 us (3%)
    ppermute x37, waiting for transfers between devices, shift(): lax.ppermute(value, axis, [(i, (i + steps) % count) for i in range(count)])  118 us
    ppermute x37, starting transfers between devices, shift(): lax.ppermute(value, axis, [(i, (i + steps) % count) for i in range(count)])  51.4 us
    pallas_call x17, Pallas kernels, call(): pl.pallas_call(kernel, out_shape=outs, in_specs=[pl.BlockSpec(memory_spac...  31.7 us
    ppermute x2, waiting for transfers between devices, gather_line(): ends = lax.ppermute(middle, 'tensor', [(1, 0), (nt - 2, nt - 1)])  19.9 us
    pallas_call x4, Pallas kernels, weight_grad(): pl.pallas_call(functools.partial(weight_kernel, len(lefts), len(rights)),...  9.2 us
    ppermute x2, waiting for transfers between devices, gather_line(): behind = lax.ppermute(near, 'tensor', [(i, i - 1) for i in range(1, nt)])  8.2 us
    ppermute x3, starting transfers between devices, sum_over(): lax.ppermute(value, axis, [(i, i ^ step) for i in range(count)])  6.64 us
    ppermute x2, starting transfers between devices, gather_line(): ahead = lax.ppermute(near, 'tensor', [(i, i + 1) for i in range(nt - 1)])  6.27 us
  transfers between devices with their start and end apart: 48, of which 18 were waited for; matrix products, arithmetic and copies ran while one was open for 2% of the time, Pallas kernels for 11%

profile of v2, /device:TPU:0, one launch (start us, length us, event | category | flops | bytes accessed | tf_op | source)
XLA Modules:
  0.0 275.8 jit_solution(17314725858215450255)
XLA Ops:
  0.6 1.1 slice_bitcast_fusion.5
  1.7 4.1 %collective-permute-start.4 = (bf16[2,32,2560]{2,1,0:T(8,128)(2,1)S(1)}, bf16[2,32,2560]{2,1,0:T(8,128)(2,1)S(1)}, u32[]{:S(2)}, u32[]{:S(2)}) collective-permute-start(bf16[2,32,2560]{2,1,0:T(8,128)(2,1)S(1)} %get-tuple-element.72.refs_0_.x_ref), channel_id=1, source_target_pairs={{0,4},{2,6},{4,0},{6,2},{1,5},{3,7},{5,1},{7,3},{8,12},{10,14},{12... | collective-permute-start | bytes 983048 | tf_op jit(solution)/shard_map/ppermute | solution.py:275
  5.9 3.5 %collective-permute-start.3 = (bf16[2,32,2560]{2,1,0:T(8,128)(2,1)S(1)}, bf16[2,32,2560]{2,1,0:T(8,128)(2,1)S(1)}, u32[]{:S(2)}, u32[]{:S(2)}) collective-permute-start(bf16[2,32,2560]{2,1,0:T(8,128)(2,1)S(1)} %get-tuple-element.72.refs_0_.x_ref), channel_id=1, source_target_pairs={{0,2},{2,4},{4,6},{1,3},{3,5},{5,7},{8,10},{10,12},{12,14},{9,11},... | collective-permute-start | bytes 983048 | tf_op jit(solution)/shard_map/ppermute | solution.py:331
  9.4 1.3 collective-permute-start.5
  10.7 2.7 collective-permute-start
  13.8 3.6 %slice_bitcast_fusion.1 = (bf16[2560,640]{1,0:T(8,128)(2,1)S(1)}, bf16[2560,640]{1,0:T(8,128)(2,1)S(1)}) fusion(bf16[2,1,2560,640]{3,2,1,0:T(8,128)(2,1)} %param.9), kind=kLoop, calls=%fused_computation.1 | loop fusion | bytes 13107200 | tf_op jit(solution)/shard_map/squeeze | solution.py:305
  18.6 3.8 %collective-permute-done.4.refs_2_ = bf16[2,32,2560]{2,1,0:T(8,128)(2,1)S(1)} collective-permute-done((bf16[2,32,2560]{2,1,0:T(8,128)(2,1)S(1)}, bf16[2,32,2560]{2,1,0:T(8,128)(2,1)S(1)}, u32[]{:S(2)}, u32[]{:S(2)}) %collective-permute-start.4) | collective-permute-done | bytes 327712 | tf_op jit(solution)/shard_map/ppermute | solution.py:275
  22.4 1.9 collective-permute-start.2
  24.3 1.3 collective-permute-start.6
  26.0 8.2 %collective-permute-done.5.refs_3_ = bf16[2,32,2560]{2,1,0:T(8,128)(2,1)S(1)} collective-permute-done((bf16[2,32,2560]{2,1,0:T(8,128)(2,1)S(1)}, bf16[2,32,2560]{2,1,0:T(8,128)(2,1)S(1)}, u32[]{:S(2)}, u32[]{:S(2)}) %collective-permute-start.5) | collective-permute-done | bytes 327712 | tf_op jit(solution)/shard_map/ppermute | solution.py:332
  34.2 19.9 %collective-permute-done.6.refs_4_ = bf16[2,32,2560]{2,1,0:T(8,128)(2,1)S(1)} collective-permute-done((bf16[2,32,2560]{2,1,0:T(8,128)(2,1)S(1)}, bf16[2,32,2560]{2,1,0:T(8,128)(2,1)S(1)}, u32[]{:S(2)}, u32[]{:S(2)}) %collective-permute-start.6) | collective-permute-done | bytes 327712 | tf_op jit(solution)/shard_map/ppermute | solution.py:333
  54.1 3.7 %shard_map.93 = (bf16[2,128,2560]{2,1,0:T(8,128)(2,1)S(1)}, bf16[2,128,512]{2,1,0:T(8,128)(2,1)S(1)}, bf16[2,128,640]{2,1,0:T(8,128)(2,1)S(1)}, f32[2,128,1024]{2,1,0:T(8,128)S(1)}) custom-call(s32[3]{0:T(128)S(1)} %pad_add_fusion.flag_ref._.where_ref, bf16[2,32,2560]{2,1,0:T(8,128)(2,1)S(1)} %get-tuple-element.72.refs_0_.x_ref, ...), custom_call_target="tpu_custom_call" | custom-call | flops 838860800 | bytes 11358220 | tf_op jit(solution)/shard_map/pallas_call | solution.py:217
  57.9 3.8 %shard_map.94 = (bf16[128,640]{1,0:T(8,128)(2,1)S(1)}, bf16[32,2560]{1,0:T(8,128)(2,1)S(1)}, bf16[32,2560]{1,0:T(8,128)(2,1)S(1)}, bf16[32,2560]{1,0:T(8,128)(2,1)S(1)}, bf16[32,2560]{1,0:T(8,128)(2,1)S(1)}) custom-call(s32[3]{0:T(128)S(1)} %pad_add_fusion.flag_ref._.where_ref, bf16[2,32,2560]{2,1,0:T(8,128)(2,1)S(1)} %bitcast.43, ...), custom_call_target="tpu_custom_call" | custom-call | flops 754974720 | bytes 9535500 | tf_op jit(solution)/shard_map/pallas_call | solution.py:217
  62.4 1.4 collective-permute-start.7
  64.4 2.9 %collective-permute-start.18 = (bf16[2,32,2560]{2,1,0:T(8,128)(2,1)S(1)}, bf16[2,32,2560]{2,1,0:T(8,128)(2,1)S(1)}, u32[]{:S(2)}, u32[]{:S(2)}) collective-permute-start(bf16[2,32,2560]{2,1,0:T(8,128)(2,1)S(1)} %get-tuple-element.73.refs_0_.x_ref), channel_id=1, source_target_pairs={{0,4},{2,6},{4,0},{6,2},{1,5},{3,7},{5,1},{7,3},{8,12},{10,14},{12... | collective-permute-start | bytes 983048 | tf_op jit(solution)/shard_map/ppermute | solution.py:275
  67.3 2.8 %collective-permute-start.17 = (bf16[2,32,2560]{2,1,0:T(8,128)(2,1)S(1)}, bf16[2,32,2560]{2,1,0:T(8,128)(2,1)S(1)}, u32[]{:S(2)}, u32[]{:S(2)}) collective-permute-start(bf16[2,32,2560]{2,1,0:T(8,128)(2,1)S(1)} %get-tuple-element.73.refs_0_.x_ref), channel_id=1, source_target_pairs={{0,2},{2,4},{4,6},{1,3},{3,5},{5,7},{8,10},{10,12},{12,14},{9,11},... | collective-permute-start | bytes 983048 | tf_op jit(solution)/shard_map/ppermute | solution.py:331
  70.1 3.8 %shard_map.96 = (bf16[128,640]{1,0:T(8,128)(2,1)S(1)}, bf16[32,2560]{1,0:T(8,128)(2,1)S(1)}, bf16[32,2560]{1,0:T(8,128)(2,1)S(1)}, bf16[32,2560]{1,0:T(8,128)(2,1)S(1)}, bf16[32,2560]{1,0:T(8,128)(2,1)S(1)}) custom-call(s32[3]{0:T(128)S(1)} %pad_add_fusion.flag_ref._.where_ref, bf16[2,32,2560]{2,1,0:T(8,128)(2,1)S(1)} %bitcast.44, ...), custom_call_target="tpu_custom_call" | custom-call | flops 754974720 | bytes 9535500 | tf_op jit(solution)/shard_map/pallas_call | solution.py:217
  74.6 0.8 collective-permute-start.10
  75.4 10.3 %collective-permute-done.8.refs_2_ = bf16[32,2560]{1,0:T(8,128)(2,1)S(1)} collective-permute-done((bf16[32,2560]{1,0:T(8,128)(2,1)S(1)}, bf16[32,2560]{1,0:T(8,128)(2,1)S(1)}, u32[]{:S(2)}, u32[]{:S(2)}) %collective-permute-start.8) | collective-permute-done | bytes 163872 | tf_op jit(solution)/shard_map/ppermute | solution.py:275
  86.6 0.8 shard_map.95
  87.4 12.0 %collective-permute-done.18.refs_2_ = bf16[2,32,2560]{2,1,0:T(8,128)(2,1)S(1)} collective-permute-done((bf16[2,32,2560]{2,1,0:T(8,128)(2,1)S(1)}, bf16[2,32,2560]{2,1,0:T(8,128)(2,1)S(1)}, u32[]{:S(2)}, u32[]{:S(2)}) %collective-permute-start.18) | collective-permute-done | bytes 327712 | tf_op jit(solution)/shard_map/ppermute | solution.py:275
  99.5 1.3 collective-permute-start.19
  100.8 1.3 collective-permute-start.13
  102.1 4.5 %collective-permute-done.11.refs_2_ = bf16[32,2560]{1,0:T(8,128)(2,1)S(1)} collective-permute-done((bf16[32,2560]{1,0:T(8,128)(2,1)S(1)}, bf16[32,2560]{1,0:T(8,128)(2,1)S(1)}, u32[]{:S(2)}, u32[]{:S(2)}) %collective-permute-start.11) | collective-permute-done | bytes 163872 | tf_op jit(solution)/shard_map/ppermute | solution.py:275
  106.5 1.3 collective-permute-start.20
  107.8 0.8 shard_map.97.chosen_ref
  108.7 1.3 collective-permute-start.24
  110.6 5.9 %collective-permute-start.14 = (bf16[32,2560]{1,0:T(8,128)(2,1)S(1)}, bf16[32,2560]{1,0:T(8,128)(2,1)S(1)}, u32[]{:S(2)}, u32[]{:S(2)}) collective-permute-start(bf16[32,2560]{1,0:T(8,128)(2,1)S(1)} %shard_map.98.refs_0_.grad_ref.refs_8_), channel_id=1, source_target_pairs={{0,2},{2,4},{4,6},{6,0},{1,3},{3,5},{5,7},{7,1},{8,10},{10,12},{12... | collective-permute-start | bytes 491528 | tf_op jit(solution)/shard_map/ppermute | solution.py:275
  116.5 2.9 %collective-permute-start.15 = (bf16[32,2560]{1,0:T(8,128)(2,1)S(1)}, bf16[32,2560]{1,0:T(8,128)(2,1)S(1)}, u32[]{:S(2)}, u32[]{:S(2)}) collective-permute-start(bf16[32,2560]{1,0:T(8,128)(2,1)S(1)} %shard_map.98.refs_0_.grad_ref.refs_8_), channel_id=1, source_target_pairs={{0,4},{2,6},{4,0},{6,2},{1,5},{3,7},{5,1},{7,3},{8,12},{10,14},{12... | collective-permute-start | bytes 491528 | tf_op jit(solution)/shard_map/ppermute | solution.py:275
  119.4 2.8 %collective-permute-start.16 = (bf16[32,2560]{1,0:T(8,128)(2,1)S(1)}, bf16[32,2560]{1,0:T(8,128)(2,1)S(1)}, u32[]{:S(2)}, u32[]{:S(2)}) collective-permute-start(bf16[32,2560]{1,0:T(8,128)(2,1)S(1)} %shard_map.98.refs_0_.grad_ref.refs_8_), channel_id=1, source_target_pairs={{0,6},{2,0},{4,2},{6,4},{1,7},{3,1},{5,3},{7,5},{8,14},{10,8},{12,... | collective-permute-start | bytes 491528 | tf_op jit(solution)/shard_map/ppermute | solution.py:275
  123.4 3.6 %collective-permute-start.27 = (bf16[32,2560]{1,0:T(8,128)(2,1)S(1)}, bf16[32,2560]{1,0:T(8,128)(2,1)S(1)}, u32[]{:S(2)}, u32[]{:S(2)}) collective-permute-start(bf16[32,2560]{1,0:T(8,128)(2,1)S(1)} %shard_map.102.refs_0_.grad_ref.refs_8_), channel_id=1, source_target_pairs={{0,6},{2,0},{4,2},{6,4},{1,7},{3,1},{5,3},{7,5},{8,14},{10,8},{12,... | collective-permute-start | bytes 491528 | tf_op jit(solution)/shard_map/ppermute | solution.py:275
  127.1 1.5 shard_map.112
  128.5 3.7 %shard_map.99 = (bf16[2,128,2560]{2,1,0:T(8,128)(2,1)S(1)}, bf16[2,128,512]{2,1,0:T(8,128)(2,1)S(1)}, bf16[2,128,640]{2,1,0:T(8,128)(2,1)S(1)}, f32[2,128,1024]{2,1,0:T(8,128)S(1)}) custom-call(s32[3]{0:T(128)S(1)} %pad_add_fusion.flag_ref._.where_ref, bf16[2,32,2560]{2,1,0:T(8,128)(2,1)S(1)} %get-tuple-element.73.refs_0_.x_ref, ...), custom_call_target="tpu_custom_call" | custom-call | flops 838860800 | bytes 11358220 | tf_op jit(solution)/shard_map/pallas_call | solution.py:217
  132.3 3.8 %shard_map.100 = (bf16[128,640]{1,0:T(8,128)(2,1)S(1)}, bf16[32,2560]{1,0:T(8,128)(2,1)S(1)}, bf16[32,2560]{1,0:T(8,128)(2,1)S(1)}, bf16[32,2560]{1,0:T(8,128)(2,1)S(1)}, bf16[32,2560]{1,0:T(8,128)(2,1)S(1)}) custom-call(s32[3]{0:T(128)S(1)} %pad_add_fusion.flag_ref._.where_ref, bf16[32,2560]{1,0:T(8,128)(2,1)S(1)} %shard_map.98.refs_0_.grad_ref.refs_8_, ...), custom_call_target="tpu_custom_call" | custom-call | flops 754974720 | bytes 8880140 | tf_op jit(solution)/shard_map/pallas_call | solution.py:217
  136.8 7.3 %collective-permute-done.26.refs_2_ = bf16[32,2560]{1,0:T(8,128)(2,1)S(1)} collective-permute-done((bf16[32,2560]{1,0:T(8,128)(2,1)S(1)}, bf16[32,2560]{1,0:T(8,128)(2,1)S(1)}, u32[]{:S(2)}, u32[]{:S(2)}) %collective-permute-start.26) | collective-permute-done | bytes 163872 | tf_op jit(solution)/shard_map/ppermute | solution.py:275
  144.1 3.8 %shard_map.103 = (bf16[128,640]{1,0:T(8,128)(2,1)S(1)}, bf16[32,2560]{1,0:T(8,128)(2,1)S(1)}, bf16[32,2560]{1,0:T(8,128)(2,1)S(1)}, bf16[32,2560]{1,0:T(8,128)(2,1)S(1)}, bf16[32,2560]{1,0:T(8,128)(2,1)S(1)}) custom-call(s32[3]{0:T(128)S(1)} %pad_add_fusion.flag_ref._.where_ref, bf16[32,2560]{1,0:T(8,128)(2,1)S(1)} %shard_map.102.refs_0_.grad_ref.refs_8_, ...), custom_call_target="tpu_custom_call" | custom-call | flops 754974720 | bytes 8880140 | tf_op jit(solution)/shard_map/pallas_call | solution.py:217
  148.0 1.4 shard_map.113
  149.5 1.6 collective-permute-start.45
  152.3 1.1 collective-permute-done.45
  153.3 4.3 %collective-permute-start.46 = (f32[2,1,2560]{2,1,0:T(1,128)S(1)}, f32[2,1,2560]{2,1,0:T(1,128)S(1)}, u32[]{:S(2)}, u32[]{:S(2)}) collective-permute-start(f32[2,1,2560]{2,1,0:T(1,128)S(1)} %add.120), channel_id=1, source_target_pairs={{0,2},{2,0},{4,6},{6,4},{1,3},{3,1},{5,7},{7,5},{8,10},{10,8},{12,... | collective-permute-start | bytes 61448 | tf_op jit(solution)/shard_map/ppermute | solution.py:284
  157.7 1.6 collective-permute-start.38
  159.3 2.6 collective-permute-start.21
  162.7 2.4 collective-permute-start.22
  165.7 5.0 %collective-permute-start.28 = (bf16[32,2560]{1,0:T(8,128)(2,1)S(1)}, bf16[32,2560]{1,0:T(8,128)(2,1)S(1)}, u32[]{:S(2)}, u32[]{:S(2)}) collective-permute-start(bf16[32,2560]{1,0:T(8,128)(2,1)S(1)} %copy-done.32), channel_id=1, source_target_pairs={{0,6},{2,0},{4,2},{6,4},{1,7},{3,1},{5,3},{7,5},{8,14},{10,8},{12,... | collective-permute-start | bytes 491528 | tf_op jit(solution)/shard_map/ppermute | solution.py:275
  170.8 3.9 %collective-permute-done.47 = f32[2,1,2560]{2,1,0:T(1,128)S(1)} collective-permute-done((f32[2,1,2560]{2,1,0:T(1,128)S(1)}, f32[2,1,2560]{2,1,0:T(1,128)S(1)}, u32[]{:S(2)}, u32[]{:S(2)}) %collective-permute-start.47) | collective-permute-done | bytes 20512 | tf_op jit(solution)/shard_map/ppermute | solution.py:284
  175.2 11.0 %collective-permute-done.22.refs_2_ = bf16[32,2560]{1,0:T(8,128)(2,1)S(1)} collective-permute-done((bf16[32,2560]{1,0:T(8,128)(2,1)S(1)}, bf16[32,2560]{1,0:T(8,128)(2,1)S(1)}, u32[]{:S(2)}, u32[]{:S(2)}) %collective-permute-start.22) | collective-permute-done | bytes 163872 | tf_op jit(solution)/shard_map/ppermute | solution.py:275
  186.3 1.9 collective-permute-start.37
  188.4 3.7 %collective-permute-done.29.refs_2_ = bf16[32,2560]{1,0:T(8,128)(2,1)S(1)} collective-permute-done((bf16[32,2560]{1,0:T(8,128)(2,1)S(1)}, bf16[32,2560]{1,0:T(8,128)(2,1)S(1)}, u32[]{:S(2)}, u32[]{:S(2)}) %collective-permute-start.29) | collective-permute-done | bytes 163872 | tf_op jit(solution)/shard_map/ppermute | solution.py:275
  192.5 1.5 collective-permute-start.33
  196.0 0.8 shard_map.101
  196.8 0.8 shard_map.104
  197.6 16.0 %collective-permute-done.37.refs_1_ = bf16[2,128,256]{2,1,0:T(8,128)(2,1)S(1)} collective-permute-done((bf16[2,128,256]{2,1,0:T(8,128)(2,1)S(1)}, bf16[2,128,256]{2,1,0:T(8,128)(2,1)S(1)}, u32[]{:S(2)}, u32[]{:S(2)}) %collective-permute-start.37) | collective-permute-done | bytes 131104 | tf_op jit(solution)/shard_map/ppermute | solution.py:275
  213.8 17.4 %collective-permute-done.35.refs_5_ = bf16[128,640]{1,0:T(8,128)(2,1)S(1)} collective-permute-done((bf16[128,640]{1,0:T(8,128)(2,1)S(1)}, bf16[128,640]{1,0:T(8,128)(2,1)S(1)}, u32[]{:S(2)}, u32[]{:S(2)}) %collective-permute-start.35) | collective-permute-done | bytes 163872 | tf_op jit(solution)/shard_map/ppermute | solution.py:275
  231.3 3.4 %collective-permute-done.33.refs_5_ = bf16[128,640]{1,0:T(8,128)(2,1)S(1)} collective-permute-done((bf16[128,640]{1,0:T(8,128)(2,1)S(1)}, bf16[128,640]{1,0:T(8,128)(2,1)S(1)}, u32[]{:S(2)}, u32[]{:S(2)}) %collective-permute-start.33) | collective-permute-done | bytes 163872 | tf_op jit(solution)/shard_map/ppermute | solution.py:275
  234.9 17.4 %collective-permute-done.36.refs_7_ = bf16[128,640]{1,0:T(8,128)(2,1)S(1)} collective-permute-done((bf16[128,640]{1,0:T(8,128)(2,1)S(1)}, bf16[128,640]{1,0:T(8,128)(2,1)S(1)}, u32[]{:S(2)}, u32[]{:S(2)}) %collective-permute-start.36) | collective-permute-done | bytes 163872 | tf_op jit(solution)/shard_map/ppermute | solution.py:275
  252.4 3.4 %collective-permute-done.34.refs_7_ = bf16[128,640]{1,0:T(8,128)(2,1)S(1)} collective-permute-done((bf16[128,640]{1,0:T(8,128)(2,1)S(1)}, bf16[128,640]{1,0:T(8,128)(2,1)S(1)}, u32[]{:S(2)}, u32[]{:S(2)}) %collective-permute-start.34) | collective-permute-done | bytes 163872 | tf_op jit(solution)/shard_map/ppermute | solution.py:275
  255.9 1.9 collective-permute-start.42
  257.8 0.9 maximum_bitcast_fusion
  258.8 2.4 shard_map.105.refs_8_
  261.2 2.4 shard_map.106
  263.6 3.0 %collective-permute-done.44.refs_11_ = bf16[96,2560]{1,0:T(8,128)(2,1)S(1)} collective-permute-done((bf16[96,2560]{1,0:T(8,128)(2,1)S(1)}, bf16[96,2560]{1,0:T(8,128)(2,1)S(1)}, u32[]{:S(2)}, u32[]{:S(2)}) %collective-permute-start.44) | collective-permute-done | bytes 491552 | tf_op jit(solution)/shard_map/ppermute | solution.py:275
  266.6 2.2 shard_map.110.refs_12_
  268.8 4.8 %collective-permute-done.41.refs_10_ = bf16[32,2560]{1,0:T(8,128)(2,1)S(1)} collective-permute-done((bf16[32,2560]{1,0:T(8,128)(2,1)S(1)}, bf16[32,2560]{1,0:T(8,128)(2,1)S(1)}, u32[]{:S(2)}, u32[]{:S(2)}) %collective-permute-start.41) | collective-permute-done | bytes 163872 | tf_op jit(solution)/shard_map/ppermute | solution.py:275
  273.6 2.2 shard_map.111
  (158 shorter events, 13.7 us)
Async XLA Ops:
  1.7 20.6 %collective-permute-start.4 = (bf16[2,32,2560]{2,1,0:T(8,128)(2,1)S(1)}, bf16[2,32,2560]{2,1,0:T(8,128)(2,1)S(1)}, u32[]{:S(2)}, u32[]{:S(2)}) collective-permute-start(bf16[2,32,2560]{2,1,0:T(8,128)(2,1)S(1)} %get-tuple-element.72.refs_0_.x_ref), channel_id=1, source_target_pairs={{0,4},{2,6},{4,0},{6,2},{1,5},{3,7},{5,1},{7,3},{8,12},{10,14},{12... | collective-permute-start | bytes 983048 | tf_op jit(solution)/shard_map/ppermute | solution.py:275
  5.9 18.4 %collective-permute-start.3 = (bf16[2,32,2560]{2,1,0:T(8,128)(2,1)S(1)}, bf16[2,32,2560]{2,1,0:T(8,128)(2,1)S(1)}, u32[]{:S(2)}, u32[]{:S(2)}) collective-permute-start(bf16[2,32,2560]{2,1,0:T(8,128)(2,1)S(1)} %get-tuple-element.72.refs_0_.x_ref), channel_id=1, source_target_pairs={{0,2},{2,4},{4,6},{1,3},{3,5},{5,7},{8,10},{10,12},{12,14},{9,11},... | collective-permute-start | bytes 983048 | tf_op jit(solution)/shard_map/ppermute | solution.py:331
  9.4 24.8 %collective-permute-start.5 = (bf16[2,32,2560]{2,1,0:T(8,128)(2,1)S(1)}, bf16[2,32,2560]{2,1,0:T(8,128)(2,1)S(1)}, u32[]{:S(2)}, u32[]{:S(2)}) collective-permute-start(bf16[2,32,2560]{2,1,0:T(8,128)(2,1)S(1)} %get-tuple-element.72.refs_0_.x_ref), channel_id=1, source_target_pairs={{2,0},{4,2},{6,4},{3,1},{5,3},{7,5},{10,8},{12,10},{14,12},{11,9},... | collective-permute-start | bytes 983048 | tf_op jit(solution)/shard_map/ppermute | solution.py:332
  10.7 47.2 %collective-permute-start = (bf16[2,32,2560]{2,1,0:T(8,128)(2,1)}, bf16[2,32,2560]{2,1,0:T(8,128)(2,1)S(1)}, u32[]{:S(2)}, u32[]{:S(2)}) collective-permute-start(bf16[2,32,2560]{2,1,0:T(8,128)(2,1)} %bitcast.40), channel_id=1, source_target_pairs={{0,2},{2,4},{4,6},{6,0},{1,3},{3,5},{5,7},{7,1},{8,10},{10,12},{12... | collective-permute-start | bytes 983048 | tf_op jit(solution)/shard_map/ppermute | solution.py:275
  13.4 44.5 %collective-permute-start.1 = (bf16[2,32,2560]{2,1,0:T(8,128)(2,1)}, bf16[2,32,2560]{2,1,0:T(8,128)(2,1)S(1)}, u32[]{:S(2)}, u32[]{:S(2)}) collective-permute-start(bf16[2,32,2560]{2,1,0:T(8,128)(2,1)} %bitcast.41), channel_id=1, source_target_pairs={{0,4},{2,6},{4,0},{6,2},{1,5},{3,7},{5,1},{7,3},{8,12},{10,14},{12... | collective-permute-start | bytes 983048 | tf_op jit(solution)/shard_map/ppermute | solution.py:275
  18.2 36.0 %copy-start.5 = (f32[2,1,2560]{2,1,0:T(1,128)S(1)}, f32[2,1,2560]{2,1,0:T(1,128)}, u32[]{:S(2)}) copy-start(f32[2,1,2560]{2,1,0:T(1,128)} %gain_ref.7) | copy-start | bytes 61444
  22.4 35.5 %collective-permute-start.2 = (bf16[2,32,2560]{2,1,0:T(8,128)(2,1)S(1)}, bf16[2,32,2560]{2,1,0:T(8,128)(2,1)S(1)}, u32[]{:S(2)}, u32[]{:S(2)}) collective-permute-start(bf16[2,32,2560]{2,1,0:T(8,128)(2,1)S(1)} %bitcast.42), channel_id=1, source_target_pairs={{0,6},{2,0},{4,2},{6,4},{1,7},{3,1},{5,3},{7,5},{8,14},{10,8},{12,... | collective-permute-start | bytes 983048 | tf_op jit(solution)/shard_map/ppermute | solution.py:275
  24.3 29.8 %collective-permute-start.6 = (bf16[2,32,2560]{2,1,0:T(8,128)(2,1)S(1)}, bf16[2,32,2560]{2,1,0:T(8,128)(2,1)S(1)}, u32[]{:S(2)}, u32[]{:S(2)}) collective-permute-start(bf16[2,32,2560]{2,1,0:T(8,128)(2,1)S(1)} %collective-permute-done.4.refs_2_), channel_id=1, source_target_pairs={{2,0},{4,6},{3,1},{5,7},{10,8},{12,14},{11,9},{13,15},{18,16},{20,... | collective-permute-start | bytes 983048 | tf_op jit(solution)/shard_map/ppermute | solution.py:333
  62.4 12.2 %collective-permute-start.7 = (bf16[32,2560]{1,0:T(8,128)(2,1)S(1)}, bf16[32,2560]{1,0:T(8,128)(2,1)S(1)}, u32[]{:S(2)}, u32[]{:S(2)}) collective-permute-start(bf16[32,2560]{1,0:T(8,128)(2,1)S(1)} %get-tuple-element.35.refs_6_), channel_id=1, source_target_pairs={{0,6},{2,0},{4,2},{6,4},{1,7},{3,1},{5,3},{7,5},{8,14},{10,8},{12,... | collective-permute-start | bytes 491528 | tf_op jit(solution)/shard_map/ppermute | solution.py:275
  63.8 22.0 %collective-permute-start.8 = (bf16[32,2560]{1,0:T(8,128)(2,1)S(1)}, bf16[32,2560]{1,0:T(8,128)(2,1)S(1)}, u32[]{:S(2)}, u32[]{:S(2)}) collective-permute-start(bf16[32,2560]{1,0:T(8,128)(2,1)S(1)} %get-tuple-element.36.refs_7_), channel_id=1, source_target_pairs={{0,4},{2,6},{4,0},{6,2},{1,5},{3,7},{5,1},{7,3},{8,12},{10,14},{12... | collective-permute-start | bytes 491528 | tf_op jit(solution)/shard_map/ppermute | solution.py:275
  63.8 22.0 %collective-permute-start.9 = (bf16[32,2560]{1,0:T(8,128)(2,1)S(1)}, bf16[32,2560]{1,0:T(8,128)(2,1)S(1)}, u32[]{:S(2)}, u32[]{:S(2)}) collective-permute-start(bf16[32,2560]{1,0:T(8,128)(2,1)S(1)} %get-tuple-element.37.refs_8_), channel_id=1, source_target_pairs={{0,2},{2,4},{4,6},{6,0},{1,3},{3,5},{5,7},{7,1},{8,10},{10,12},{12... | collective-permute-start | bytes 491528 | tf_op jit(solution)/shard_map/ppermute | solution.py:275
  64.4 35.1 %collective-permute-start.18 = (bf16[2,32,2560]{2,1,0:T(8,128)(2,1)S(1)}, bf16[2,32,2560]{2,1,0:T(8,128)(2,1)S(1)}, u32[]{:S(2)}, u32[]{:S(2)}) collective-permute-start(bf16[2,32,2560]{2,1,0:T(8,128)(2,1)S(1)} %get-tuple-element.73.refs_0_.x_ref), channel_id=1, source_target_pairs={{0,4},{2,6},{4,0},{6,2},{1,5},{3,7},{5,1},{7,3},{8,12},{10,14},{12... | collective-permute-start | bytes 983048 | tf_op jit(solution)/shard_map/ppermute | solution.py:275
  67.3 49.2 %collective-permute-start.17 = (bf16[2,32,2560]{2,1,0:T(8,128)(2,1)S(1)}, bf16[2,32,2560]{2,1,0:T(8,128)(2,1)S(1)}, u32[]{:S(2)}, u32[]{:S(2)}) collective-permute-start(bf16[2,32,2560]{2,1,0:T(8,128)(2,1)S(1)} %get-tuple-element.73.refs_0_.x_ref), channel_id=1, source_target_pairs={{0,2},{2,4},{4,6},{1,3},{3,5},{5,7},{8,10},{10,12},{12,14},{9,11},... | collective-permute-start | bytes 983048 | tf_op jit(solution)/shard_map/ppermute | solution.py:331
  74.6 47.6 %copy-start.34 = (bf16[1,1,32,2560]{3,2,1,0:T(8,128)(2,1)S(1)}, bf16[1,1,32,2560]{3,2,1,0:T(8,128)(2,1)}, u32[]{:S(2)}) copy-start(bf16[1,1,32,2560]{3,2,1,0:T(8,128)(2,1)} %param.8) | copy-start | bytes 491524
  74.6 26.2 %collective-permute-start.10 = (bf16[32,2560]{1,0:T(8,128)(2,1)S(1)}, bf16[32,2560]{1,0:T(8,128)(2,1)S(1)}, u32[]{:S(2)}, u32[]{:S(2)}) collective-permute-start(bf16[32,2560]{1,0:T(8,128)(2,1)S(1)} %get-tuple-element.39.refs_10_), channel_id=1, source_target_pairs={{0,6},{2,0},{4,2},{6,4},{1,7},{3,1},{5,3},{7,5},{8,14},{10,8},{12,... | collective-permute-start | bytes 491528 | tf_op jit(solution)/shard_map/ppermute | solution.py:275
  85.7 20.8 %collective-permute-start.11 = (bf16[32,2560]{1,0:T(8,128)(2,1)S(1)}, bf16[32,2560]{1,0:T(8,128)(2,1)S(1)}, u32[]{:S(2)}, u32[]{:S(2)}) collective-permute-start(bf16[32,2560]{1,0:T(8,128)(2,1)S(1)} %get-tuple-element.40.refs_11_), channel_id=1, source_target_pairs={{0,4},{2,6},{4,0},{6,2},{1,5},{3,7},{5,1},{7,3},{8,12},{10,14},{12... | collective-permute-start | bytes 491528 | tf_op jit(solution)/shard_map/ppermute | solution.py:275
  85.8 22.1 %collective-permute-start.12 = (bf16[32,2560]{1,0:T(8,128)(2,1)S(1)}, bf16[32,2560]{1,0:T(8,128)(2,1)S(1)}, u32[]{:S(2)}, u32[]{:S(2)}) collective-permute-start(bf16[32,2560]{1,0:T(8,128)(2,1)S(1)} %get-tuple-element.41.refs_12_), channel_id=1, source_target_pairs={{0,2},{2,4},{4,6},{6,0},{1,3},{3,5},{5,7},{7,1},{8,10},{10,12},{12... | collective-permute-start | bytes 491528 | tf_op jit(solution)/shard_map/ppermute | solution.py:275
  87.4 34.8 %copy-start.6 = (bf16[32,2560]{1,0:T(8,128)(2,1)}, bf16[32,2560]{1,0:T(8,128)(2,1)S(1)}, u32[]{:S(2)}) copy-start(bf16[32,2560]{1,0:T(8,128)(2,1)S(1)} %shard_map.95) | copy-start | bytes 491524
  99.5 23.3 %collective-permute-start.19 = (bf16[2,32,2560]{2,1,0:T(8,128)(2,1)S(1)}, bf16[2,32,2560]{2,1,0:T(8,128)(2,1)S(1)}, u32[]{:S(2)}, u32[]{:S(2)}) collective-permute-start(bf16[2,32,2560]{2,1,0:T(8,128)(2,1)S(1)} %get-tuple-element.73.refs_0_.x_ref), channel_id=1, source_target_pairs={{2,0},{4,2},{6,4},{3,1},{5,3},{7,5},{10,8},{12,10},{14,12},{11,9},... | collective-permute-start | bytes 983048 | tf_op jit(solution)/shard_map/ppermute | solution.py:332
  100.8 9.2 %collective-permute-start.13 = (bf16[32,2560]{1,0:T(8,128)(2,1)S(1)}, bf16[32,2560]{1,0:T(8,128)(2,1)S(1)}, u32[]{:S(2)}, u32[]{:S(2)}) collective-permute-start(bf16[32,2560]{1,0:T(8,128)(2,1)S(1)} %shard_map.95), channel_id=1, source_target_pairs={{8,0},{16,8},{24,16},{9,1},{17,9},{25,17},{10,2},{18,10},{26,18},{... | collective-permute-start | bytes 491528 | tf_op jit(solution)/shard_map/ppermute | solution.py:460
  106.5 16.3 %collective-permute-start.20 = (bf16[2,32,2560]{2,1,0:T(8,128)(2,1)S(1)}, bf16[2,32,2560]{2,1,0:T(8,128)(2,1)S(1)}, u32[]{:S(2)}, u32[]{:S(2)}) collective-permute-start(bf16[2,32,2560]{2,1,0:T(8,128)(2,1)S(1)} %collective-permute-done.18.refs_2_), channel_id=1, source_target_pairs={{2,0},{4,6},{3,1},{5,7},{10,8},{12,14},{11,9},{13,15},{18,16},{20,... | collective-permute-start | bytes 983048 | tf_op jit(solution)/shard_map/ppermute | solution.py:333
  108.7 10.7 %collective-permute-start.24 = (bf16[32,2560]{1,0:T(8,128)(2,1)S(1)}, bf16[32,2560]{1,0:T(8,128)(2,1)S(1)}, u32[]{:S(2)}, u32[]{:S(2)}) collective-permute-start(bf16[32,2560]{1,0:T(8,128)(2,1)S(1)} %shard_map.97.chosen_ref), channel_id=1, source_target_pairs={{0,8},{8,16},{16,24},{1,9},{9,17},{17,25},{2,10},{10,18},{18,26},{... | collective-permute-start | bytes 491528 | tf_op jit(solution)/shard_map/ppermute | solution.py:456
  110.6 12.9 %collective-permute-start.14 = (bf16[32,2560]{1,0:T(8,128)(2,1)S(1)}, bf16[32,2560]{1,0:T(8,128)(2,1)S(1)}, u32[]{:S(2)}, u32[]{:S(2)}) collective-permute-start(bf16[32,2560]{1,0:T(8,128)(2,1)S(1)} %shard_map.98.refs_0_.grad_ref.refs_8_), channel_id=1, source_target_pairs={{0,2},{2,4},{4,6},{6,0},{1,3},{3,5},{5,7},{7,1},{8,10},{10,12},{12... | collective-permute-start | bytes 491528 | tf_op jit(solution)/shard_map/ppermute | solution.py:275
  116.5 15.7 %collective-permute-start.15 = (bf16[32,2560]{1,0:T(8,128)(2,1)S(1)}, bf16[32,2560]{1,0:T(8,128)(2,1)S(1)}, u32[]{:S(2)}, u32[]{:S(2)}) collective-permute-start(bf16[32,2560]{1,0:T(8,128)(2,1)S(1)} %shard_map.98.refs_0_.grad_ref.refs_8_), channel_id=1, source_target_pairs={{0,4},{2,6},{4,0},{6,2},{1,5},{3,7},{5,1},{7,3},{8,12},{10,14},{12... | collective-permute-start | bytes 491528 | tf_op jit(solution)/shard_map/ppermute | solution.py:275
  119.4 12.9 %collective-permute-start.16 = (bf16[32,2560]{1,0:T(8,128)(2,1)S(1)}, bf16[32,2560]{1,0:T(8,128)(2,1)S(1)}, u32[]{:S(2)}, u32[]{:S(2)}) collective-permute-start(bf16[32,2560]{1,0:T(8,128)(2,1)S(1)} %shard_map.98.refs_0_.grad_ref.refs_8_), channel_id=1, source_target_pairs={{0,6},{2,0},{4,2},{6,4},{1,7},{3,1},{5,3},{7,5},{8,14},{10,8},{12,... | collective-permute-start | bytes 491528 | tf_op jit(solution)/shard_map/ppermute | solution.py:275
  122.8 14.0 %collective-permute-start.25 = (bf16[32,2560]{1,0:T(8,128)(2,1)S(1)}, bf16[32,2560]{1,0:T(8,128)(2,1)S(1)}, u32[]{:S(2)}, u32[]{:S(2)}) collective-permute-start(bf16[32,2560]{1,0:T(8,128)(2,1)S(1)} %shard_map.102.refs_0_.grad_ref.refs_8_), channel_id=1, source_target_pairs={{0,2},{2,4},{4,6},{6,0},{1,3},{3,5},{5,7},{7,1},{8,10},{10,12},{12... | collective-permute-start | bytes 491528 | tf_op jit(solution)/shard_map/ppermute | solution.py:275
  122.9 21.2 %collective-permute-start.26 = (bf16[32,2560]{1,0:T(8,128)(2,1)S(1)}, bf16[32,2560]{1,0:T(8,128)(2,1)S(1)}, u32[]{:S(2)}, u32[]{:S(2)}) collective-permute-start(bf16[32,2560]{1,0:T(8,128)(2,1)S(1)} %shard_map.102.refs_0_.grad_ref.refs_8_), channel_id=1, source_target_pairs={{0,4},{2,6},{4,0},{6,2},{1,5},{3,7},{5,1},{7,3},{8,12},{10,14},{12... | collective-permute-start | bytes 491528 | tf_op jit(solution)/shard_map/ppermute | solution.py:275
  123.4 20.7 %collective-permute-start.27 = (bf16[32,2560]{1,0:T(8,128)(2,1)S(1)}, bf16[32,2560]{1,0:T(8,128)(2,1)S(1)}, u32[]{:S(2)}, u32[]{:S(2)}) collective-permute-start(bf16[32,2560]{1,0:T(8,128)(2,1)S(1)} %shard_map.102.refs_0_.grad_ref.refs_8_), channel_id=1, source_target_pairs={{0,6},{2,0},{4,2},{6,4},{1,7},{3,1},{5,3},{7,5},{8,14},{10,8},{12,... | collective-permute-start | bytes 491528 | tf_op jit(solution)/shard_map/ppermute | solution.py:275
  149.5 3.8 %collective-permute-start.45 = (f32[2,1,2560]{2,1,0:T(1,128)S(1)}, f32[2,1,2560]{2,1,0:T(1,128)S(1)}, u32[]{:S(2)}, u32[]{:S(2)}) collective-permute-start(f32[2,1,2560]{2,1,0:T(1,128)S(1)} %add.119), channel_id=1, source_target_pairs={{0,1},{1,0},{2,3},{3,2},{4,5},{5,4},{6,7},{7,6},{8,9},{9,8},{10,11... | collective-permute-start | bytes 61448 | tf_op jit(solution)/shard_map/ppermute | solution.py:284
  151.1 14.0 %collective-permute-start.39 = (bf16[2,32,2560]{2,1,0:T(8,128)(2,1)S(1)}, bf16[2,32,2560]{2,1,0:T(8,128)(2,1)S(1)}, u32[]{:S(2)}, u32[]{:S(2)}) collective-permute-start(bf16[2,32,2560]{2,1,0:T(8,128)(2,1)S(1)} %bitcast.45), channel_id=1, source_target_pairs={{0,1},{1,0},{2,3},{3,2},{4,5},{5,4},{6,7},{7,6},{8,9},{9,8},{10,11... | collective-permute-start | bytes 983048 | tf_op jit(solution)/shard_map/ppermute | solution.py:275
  151.6 23.1 %copy-start.28 = (bf16[32,2560]{1,0:T(8,128)(2,1)S(1)}, bf16[32,2560]{1,0:T(8,128)(2,1)}, u32[]{:S(2)}) copy-start(bf16[32,2560]{1,0:T(8,128)(2,1)} %copy-done.27) | copy-start | bytes 491524
  151.6 23.4 %copy-start.2 = (bf16[2,128,2560]{2,1,0:T(8,128)(2,1)S(1)}, bf16[2,128,2560]{2,1,0:T(8,128)(2,1)}, u32[]{:S(2)}) copy-start(bf16[2,128,2560]{2,1,0:T(8,128)(2,1)} %copy-done.1) | copy-start | bytes 3932164
  152.2 22.9 %copy-start.21 = (bf16[2,128,512]{2,1,0:T(8,128)(2,1)S(1)}, bf16[2,128,512]{2,1,0:T(8,128)(2,1)}, u32[]{:S(2)}) copy-start(bf16[2,128,512]{2,1,0:T(8,128)(2,1)} %copy-done.20) | copy-start | bytes 786436
  152.2 39.8 %copy-start.23 = (bf16[128,640]{1,0:T(8,128)(2,1)S(1)}, bf16[128,640]{1,0:T(8,128)(2,1)}, u32[]{:S(2)}) copy-start(bf16[128,640]{1,0:T(8,128)(2,1)} %copy-done.22) | copy-start | bytes 491524
  152.2 40.3 %copy-start.36 = (bf16[128,640]{1,0:T(8,128)(2,1)S(1)}, bf16[128,640]{1,0:T(8,128)(2,1)}, u32[]{:S(2)}) copy-start(bf16[128,640]{1,0:T(8,128)(2,1)} %copy-done.35) | copy-start | bytes 491524
  152.2 41.8 %copy-start.7 = (bf16[32,2560]{1,0:T(8,128)(2,1)S(1)}, bf16[32,2560]{1,0:T(8,128)(2,1)}, u32[]{:S(2)}) copy-start(bf16[32,2560]{1,0:T(8,128)(2,1)} %copy-done.6) | copy-start | bytes 491524
  153.3 8.6 %collective-permute-start.46 = (f32[2,1,2560]{2,1,0:T(1,128)S(1)}, f32[2,1,2560]{2,1,0:T(1,128)S(1)}, u32[]{:S(2)}, u32[]{:S(2)}) collective-permute-start(f32[2,1,2560]{2,1,0:T(1,128)S(1)} %add.120), channel_id=1, source_target_pairs={{0,2},{2,0},{4,6},{6,4},{1,3},{3,1},{5,7},{7,5},{8,10},{10,8},{12,... | collective-permute-start | bytes 61448 | tf_op jit(solution)/shard_map/ppermute | solution.py:284
  157.7 36.4 %copy-start.15 = (bf16[32,2560]{1,0:T(8,128)(2,1)S(1)}, bf16[32,2560]{1,0:T(8,128)(2,1)}, u32[]{:S(2)}) copy-start(bf16[32,2560]{1,0:T(8,128)(2,1)} %copy-done.14) | copy-start | bytes 491524
  157.7 36.4 %copy-start.17 = (bf16[32,2560]{1,0:T(8,128)(2,1)S(1)}, bf16[32,2560]{1,0:T(8,128)(2,1)}, u32[]{:S(2)}) copy-start(bf16[32,2560]{1,0:T(8,128)(2,1)} %copy-done.16) | copy-start | bytes 491524
  157.7 36.4 %copy-start.19 = (bf16[32,2560]{1,0:T(8,128)(2,1)S(1)}, bf16[32,2560]{1,0:T(8,128)(2,1)}, u32[]{:S(2)}) copy-start(bf16[32,2560]{1,0:T(8,128)(2,1)} %copy-done.18) | copy-start | bytes 491524
  157.7 8.0 %collective-permute-start.38 = (bf16[2,128,256]{2,1,0:T(8,128)(2,1)S(1)}, bf16[2,128,256]{2,1,0:T(8,128)(2,1)S(1)}, u32[]{:S(2)}, u32[]{:S(2)}) collective-permute-start(bf16[2,128,256]{2,1,0:T(8,128)(2,1)S(1)} %get-tuple-element.76), channel_id=1, source_target_pairs={{0,1},{1,0},{2,3},{3,2},{4,5},{5,4},{6,7},{7,6},{8,9},{9,8},{10,11... | collective-permute-start | bytes 393224 | tf_op jit(solution)/shard_map/ppermute | solution.py:275
  159.3 15.4 %collective-permute-start.21 = (bf16[32,2560]{1,0:T(8,128)(2,1)}, bf16[32,2560]{1,0:T(8,128)(2,1)S(1)}, u32[]{:S(2)}, u32[]{:S(2)}) collective-permute-start(bf16[32,2560]{1,0:T(8,128)(2,1)} %copy-done.33), channel_id=1, source_target_pairs={{0,6},{2,0},{4,2},{6,4},{1,7},{3,1},{5,3},{7,5},{8,14},{10,8},{12,... | collective-permute-start | bytes 491528 | tf_op jit(solution)/shard_map/ppermute | solution.py:275
  161.9 12.8 %collective-permute-start.47 = (f32[2,1,2560]{2,1,0:T(1,128)S(1)}, f32[2,1,2560]{2,1,0:T(1,128)S(1)}, u32[]{:S(2)}, u32[]{:S(2)}) collective-permute-start(f32[2,1,2560]{2,1,0:T(1,128)S(1)} %add.121), channel_id=1, source_target_pairs={{0,4},{2,6},{4,0},{6,2},{1,5},{3,7},{5,1},{7,3},{8,12},{10,14},{12... | collective-permute-start | bytes 61448 | tf_op jit(solution)/shard_map/ppermute | solution.py:284
  162.6 32.1 %copy-start.9 = (bf16[32,2560]{1,0:T(8,128)(2,1)S(1)}, bf16[32,2560]{1,0:T(8,128)(2,1)}, u32[]{:S(2)}) copy-start(bf16[32,2560]{1,0:T(8,128)(2,1)} %copy-done.8) | copy-start | bytes 491524
  162.6 32.1 %copy-start.11 = (bf16[32,2560]{1,0:T(8,128)(2,1)S(1)}, bf16[32,2560]{1,0:T(8,128)(2,1)}, u32[]{:S(2)}) copy-start(bf16[32,2560]{1,0:T(8,128)(2,1)} %copy-done.10) | copy-start | bytes 491524
  162.6 32.1 %copy-start.13 = (bf16[32,2560]{1,0:T(8,128)(2,1)S(1)}, bf16[32,2560]{1,0:T(8,128)(2,1)}, u32[]{:S(2)}) copy-start(bf16[32,2560]{1,0:T(8,128)(2,1)} %copy-done.12) | copy-start | bytes 491524
  162.7 23.4 %collective-permute-start.22 = (bf16[32,2560]{1,0:T(8,128)(2,1)S(1)}, bf16[32,2560]{1,0:T(8,128)(2,1)S(1)}, u32[]{:S(2)}, u32[]{:S(2)}) collective-permute-start(bf16[32,2560]{1,0:T(8,128)(2,1)S(1)} %copy-done.30), channel_id=1, source_target_pairs={{0,4},{2,6},{4,0},{6,2},{1,5},{3,7},{5,1},{7,3},{8,12},{10,14},{12... | collective-permute-start | bytes 491528 | tf_op jit(solution)/shard_map/ppermute | solution.py:275
  165.1 21.2 %collective-permute-start.23 = (bf16[32,2560]{1,0:T(8,128)(2,1)S(1)}, bf16[32,2560]{1,0:T(8,128)(2,1)S(1)}, u32[]{:S(2)}, u32[]{:S(2)}) collective-permute-start(bf16[32,2560]{1,0:T(8,128)(2,1)S(1)} %copy-done.26), channel_id=1, source_target_pairs={{0,2},{2,4},{4,6},{6,0},{1,3},{3,5},{5,7},{7,1},{8,10},{10,12},{12... | collective-permute-start | bytes 491528 | tf_op jit(solution)/shard_map/ppermute | solution.py:275
  165.7 22.5 %collective-permute-start.28 = (bf16[32,2560]{1,0:T(8,128)(2,1)S(1)}, bf16[32,2560]{1,0:T(8,128)(2,1)S(1)}, u32[]{:S(2)}, u32[]{:S(2)}) collective-permute-start(bf16[32,2560]{1,0:T(8,128)(2,1)S(1)} %copy-done.32), channel_id=1, source_target_pairs={{0,6},{2,0},{4,2},{6,4},{1,7},{3,1},{5,3},{7,5},{8,14},{10,8},{12,... | collective-permute-start | bytes 491528 | tf_op jit(solution)/shard_map/ppermute | solution.py:275
  174.7 17.3 %collective-permute-start.29 = (bf16[32,2560]{1,0:T(8,128)(2,1)S(1)}, bf16[32,2560]{1,0:T(8,128)(2,1)S(1)}, u32[]{:S(2)}, u32[]{:S(2)}) collective-permute-start(bf16[32,2560]{1,0:T(8,128)(2,1)S(1)} %copy-done.28), channel_id=1, source_target_pairs={{0,4},{2,6},{4,0},{6,2},{1,5},{3,7},{5,1},{7,3},{8,12},{10,14},{12... | collective-permute-start | bytes 491528 | tf_op jit(solution)/shard_map/ppermute | solution.py:275
  174.7 17.8 %collective-permute-start.30 = (bf16[32,2560]{1,0:T(8,128)(2,1)}, bf16[32,2560]{1,0:T(8,128)(2,1)S(1)}, u32[]{:S(2)}, u32[]{:S(2)}) collective-permute-start(bf16[32,2560]{1,0:T(8,128)(2,1)} %copy-done.24), channel_id=1, source_target_pairs={{0,2},{2,4},{4,6},{6,0},{1,3},{3,5},{5,7},{7,1},{8,10},{10,12},{12... | collective-permute-start | bytes 491528 | tf_op jit(solution)/shard_map/ppermute | solution.py:275
  175.1 59.6 %copy-start.38 = (bf16[128,640]{1,0:T(8,128)(2,1)S(1)}, bf16[128,640]{1,0:T(8,128)(2,1)}, u32[]{:S(2)}) copy-start(bf16[128,640]{1,0:T(8,128)(2,1)} %copy-done.37) | copy-start | bytes 491524
  186.2 77.4 %collective-permute-start.40 = (bf16[2,96,2560]{2,1,0:T(8,128)(2,1)S(1)}, bf16[2,96,2560]{2,1,0:T(8,128)(2,1)S(1)}, u32[]{:S(2)}, u32[]{:S(2)}) collective-permute-start(bf16[2,96,2560]{2,1,0:T(8,128)(2,1)S(1)} %shard_map.107.refs_5_), channel_id=1, source_target_pairs={{0,1},{1,0},{2,3},{3,2},{4,5},{5,4},{6,7},{7,6},{8,9},{9,8},{10,11... | collective-permute-start | bytes 2949128 | tf_op jit(solution)/shard_map/ppermute | solution.py:275
  186.3 27.3 %collective-permute-start.37 = (bf16[2,128,256]{2,1,0:T(8,128)(2,1)S(1)}, bf16[2,128,256]{2,1,0:T(8,128)(2,1)S(1)}, u32[]{:S(2)}, u32[]{:S(2)}) collective-permute-start(bf16[2,128,256]{2,1,0:T(8,128)(2,1)S(1)} %get-tuple-element.78), channel_id=1, source_target_pairs={{0,1},{1,0},{2,3},{3,2},{4,5},{5,4},{6,7},{7,6},{8,9},{9,8},{10,11... | collective-permute-start | bytes 393224 | tf_op jit(solution)/shard_map/ppermute | solution.py:275
  188.2 67.7 %collective-permute-start.32 = (bf16[2,128,1280]{2,1,0:T(8,128)(2,1)S(1)}, bf16[2,128,1280]{2,1,0:T(8,128)(2,1)S(1)}, u32[]{:S(2)}, u32[]{:S(2)}) collective-permute-start(bf16[2,128,1280]{2,1,0:T(8,128)(2,1)S(1)} %get-tuple-element.68), channel_id=1, source_target_pairs={{0,1},{1,0},{2,3},{3,2},{4,5},{5,4},{6,7},{7,6},{8,9},{9,8},{10,11... | collective-permute-start | bytes 1966088 | tf_op jit(solution)/shard_map/ppermute | solution.py:275
  192.0 39.1 %collective-permute-start.35 = (bf16[128,640]{1,0:T(8,128)(2,1)S(1)}, bf16[128,640]{1,0:T(8,128)(2,1)S(1)}, u32[]{:S(2)}, u32[]{:S(2)}) collective-permute-start(bf16[128,640]{1,0:T(8,128)(2,1)S(1)} %copy-done.23), channel_id=1, source_target_pairs={{0,1},{1,0},{2,3},{3,2},{4,5},{5,4},{6,7},{7,6},{8,9},{9,8},{10,11... | collective-permute-start | bytes 491528 | tf_op jit(solution)/shard_map/ppermute | solution.py:275
  192.5 42.2 %collective-permute-start.33 = (bf16[128,640]{1,0:T(8,128)(2,1)S(1)}, bf16[128,640]{1,0:T(8,128)(2,1)S(1)}, u32[]{:S(2)}, u32[]{:S(2)}) collective-permute-start(bf16[128,640]{1,0:T(8,128)(2,1)S(1)} %copy-done.36), channel_id=1, source_target_pairs={{0,1},{1,0},{2,3},{3,2},{4,5},{5,4},{6,7},{7,6},{8,9},{9,8},{10,11... | collective-permute-start | bytes 491528 | tf_op jit(solution)/shard_map/ppermute | solution.py:275
  213.6 45.1 %collective-permute-start.31 = (bf16[2,128,1280]{2,1,0:T(8,128)(2,1)S(1)}, bf16[2,128,1280]{2,1,0:T(8,128)(2,1)S(1)}, u32[]{:S(2)}, u32[]{:S(2)}) collective-permute-start(bf16[2,128,1280]{2,1,0:T(8,128)(2,1)S(1)} %get-tuple-element.70), channel_id=1, source_target_pairs={{0,1},{1,0},{2,3},{3,2},{4,5},{5,4},{6,7},{7,6},{8,9},{9,8},{10,11... | collective-permute-start | bytes 1966088 | tf_op jit(solution)/shard_map/ppermute | solution.py:275
  231.2 21.1 %collective-permute-start.36 = (bf16[128,640]{1,0:T(8,128)(2,1)S(1)}, bf16[128,640]{1,0:T(8,128)(2,1)S(1)}, u32[]{:S(2)}, u32[]{:S(2)}) collective-permute-start(bf16[128,640]{1,0:T(8,128)(2,1)S(1)} %get-tuple-element.57.refs_6_), channel_id=1, source_target_pairs={{0,1},{1,0},{2,3},{3,2},{4,5},{5,4},{6,7},{7,6},{8,9},{9,8},{10,11... | collective-permute-start | bytes 491528 | tf_op jit(solution)/shard_map/ppermute | solution.py:275
  234.7 21.1 %collective-permute-start.34 = (bf16[128,640]{1,0:T(8,128)(2,1)S(1)}, bf16[128,640]{1,0:T(8,128)(2,1)S(1)}, u32[]{:S(2)}, u32[]{:S(2)}) collective-permute-start(bf16[128,640]{1,0:T(8,128)(2,1)S(1)} %copy-done.38), channel_id=1, source_target_pairs={{0,1},{1,0},{2,3},{3,2},{4,5},{5,4},{6,7},{7,6},{8,9},{9,8},{10,11... | collective-permute-start | bytes 491528 | tf_op jit(solution)/shard_map/ppermute | solution.py:275
  252.2 11.4 %collective-permute-start.43 = (bf16[32,2560]{1,0:T(8,128)(2,1)S(1)}, bf16[32,2560]{1,0:T(8,128)(2,1)S(1)}, u32[]{:S(2)}, u32[]{:S(2)}) collective-permute-start(bf16[32,2560]{1,0:T(8,128)(2,1)S(1)} %shard_map.102.refs_0_.grad_ref.refs_8_), channel_id=1, source_target_pairs={{0,1},{1,0},{2,3},{3,2},{4,5},{5,4},{6,7},{7,6},{8,9},{9,8},{10,11... | collective-permute-start | bytes 491528 | tf_op jit(solution)/shard_map/ppermute | solution.py:275
  255.8 10.8 %collective-permute-start.44 = (bf16[96,2560]{1,0:T(8,128)(2,1)S(1)}, bf16[96,2560]{1,0:T(8,128)(2,1)S(1)}, u32[]{:S(2)}, u32[]{:S(2)}) collective-permute-start(bf16[96,2560]{1,0:T(8,128)(2,1)S(1)} %shard_map.109.refs_9_), channel_id=1, source_target_pairs={{0,1},{1,0},{2,3},{3,2},{4,5},{5,4},{6,7},{7,6},{8,9},{9,8},{10,11... | collective-permute-start | bytes 1474568 | tf_op jit(solution)/shard_map/ppermute | solution.py:275
  255.9 17.7 %collective-permute-start.42 = (bf16[96,2560]{1,0:T(8,128)(2,1)S(1)}, bf16[96,2560]{1,0:T(8,128)(2,1)S(1)}, u32[]{:S(2)}, u32[]{:S(2)}) collective-permute-start(bf16[96,2560]{1,0:T(8,128)(2,1)S(1)} %shard_map.108.refs_9_), channel_id=1, source_target_pairs={{0,1},{1,0},{2,3},{3,2},{4,5},{5,4},{6,7},{7,6},{8,9},{9,8},{10,11... | collective-permute-start | bytes 1474568 | tf_op jit(solution)/shard_map/ppermute | solution.py:275
  258.7 14.9 %collective-permute-start.41 = (bf16[32,2560]{1,0:T(8,128)(2,1)S(1)}, bf16[32,2560]{1,0:T(8,128)(2,1)S(1)}, u32[]{:S(2)}, u32[]{:S(2)}) collective-permute-start(bf16[32,2560]{1,0:T(8,128)(2,1)S(1)} %shard_map.98.refs_0_.grad_ref.refs_8_), channel_id=1, source_target_pairs={{0,1},{1,0},{2,3},{3,2},{4,5},{5,4},{6,7},{7,6},{8,9},{9,8},{10,11... | collective-permute-start | bytes 491528 | tf_op jit(solution)/shard_map/ppermute | solution.py:275
  (25 other events, 156.4 us)
